TPU v7x, 32 devices: a whole 2x2x4 slice. The times are simulated.
32 devices in a mesh: dp: 4 (over y, x), expert: 4 (over z), tensor: 2 (over core).
Axes of the slice: x: 2, y: 2, z: 4, core: 2. Of those that a mesh axis runs over, the one named last changes fastest.
Arguments:
- tokens: bfloat16 [1, 256, 3584], P(None, ('dp', 'expert'), 'tensor'), may hold values from -6 to 6
- gate_weight: bfloat16 [16, 3584, 1024], P(('dp', 'expert'), None, 'tensor'), may hold values from -0.09375 to 0.09375
- up_weight: bfloat16 [16, 3584, 1024], P(('dp', 'expert'), None, 'tensor'), may hold values from -0.09375 to 0.09375
- down_weight: bfloat16 [16, 1024, 3584], P(('dp', 'expert'), 'tensor'), may hold values from -0.1875 to 0.1875
- expert_ids: int32 [1, 256, 8], P(None, ('dp', 'expert')), may hold values from 0 to 15, all different within a row; in each aligned block of 16 rows (0 to 15, 16 to 31, ..., all dimensions but the last counted through in order) at most 16 rows name the same one
- gate_codes: int32 [1, 256, 8], P(None, ('dp', 'expert')), may hold values from 1 to 32767
Outputs:
- mixed: bfloat16 [1, 256, 3584], P(None, ('dp', 'expert'), 'tensor')
Inputs may be any that keep to these rules, and one draw needn't show every extreme that they name: `expert_ids`: the 8 experts of one token differ. For every step, of the 16 tokens that one index of dp+expert holds, no expert is named by more than 16.
All inputs are finite; a program needn't handle non-finite values.
Results may differ from a plain program's by a relative error of at most 0.0095.
Values may be sent and summed in bfloat16 or wider, within the bound.
No kernel may reach another device: no remote copies, remote signals or barrier semaphores. Data moves between devices by JAX's collectives and lax.ppermute only.
A program may use at most 64 MiB of HBM per device.

v0:
```python
import jax
import jax.numpy as jnp
from jax import lax
from jax.sharding import PartitionSpec as P


def local(tokens, gate_weight, up_weight, down_weight, expert_ids, gate_codes):
    owners = lax.axis_size("dp") * lax.axis_size("expert")
    tok_rows = tokens.shape[1]
    top_count = expert_ids.shape[2]
    slot_depth = min(tok_rows, max(2, 2 * tok_rows * top_count // owners))
    slot_count = owners * slot_depth
    w_gate = gate_weight[0]
    w_up = up_weight[0]
    w_down = down_weight[0]
    slot_numbers = jnp.arange(slot_count, dtype=jnp.int32)
    owner_numbers = jnp.arange(owners, dtype=jnp.int32)
    step_tokens = tokens[0]
    route_ids = expert_ids[0].reshape(tok_rows * top_count)
    onehot = (route_ids[:, None] == owner_numbers[None, :]).astype(jnp.int32)
    before = jnp.cumsum(onehot, axis=0) - onehot
    slot_rank = jnp.sum(before * onehot, axis=1)
    slot_index = route_ids * slot_depth + slot_rank
    select = (slot_index[:, None] == slot_numbers[None, :]).astype(jnp.bfloat16)
    per_token = jnp.sum(select.reshape(tok_rows, top_count, slot_count), axis=1)
    packed = jnp.einsum(
        "ts,td->sd", per_token, step_tokens, preferred_element_type=jnp.float32
    ).astype(jnp.bfloat16)
    packed = packed.reshape(owners, slot_depth, step_tokens.shape[1])
    arrived = lax.all_to_all(packed, ("dp", "expert"), split_axis=0, concat_axis=0, tiled=True)
    owner_rows = arrived.reshape(slot_count, step_tokens.shape[1])
    owner_rows = lax.all_gather(owner_rows, "tensor", axis=1, tiled=True)
    gated = jnp.dot(owner_rows, w_gate, preferred_element_type=jnp.float32)
    lifted = jnp.dot(owner_rows, w_up, preferred_element_type=jnp.float32)
    hidden = (jax.nn.silu(gated) * lifted).astype(jnp.bfloat16)
    partial_value = jnp.dot(hidden, w_down, preferred_element_type=jnp.float32).astype(jnp.bfloat16)
    summed = (
        lax.psum_scatter(partial_value, "tensor", scatter_dimension=1, tiled=True)
        .astype(jnp.float32)
        .astype(jnp.bfloat16)
    )
    half_width = summed.shape[1]
    result = summed.reshape(owners, slot_depth, half_width)
    returned = lax.all_to_all(result, ("dp", "expert"), split_axis=0, concat_axis=0, tiled=True)
    returned = returned.reshape(slot_count, half_width)
    picked = jnp.dot(select, returned, preferred_element_type=jnp.float32)
    codes = gate_codes[0].astype(jnp.float32)
    shares = codes / jnp.sum(codes, axis=1, keepdims=True)
    mixed_rows = jnp.sum(
        picked.reshape(tok_rows, top_count, half_width) * shares[:, :, None], axis=1
    )
    outputs = [mixed_rows.astype(jnp.bfloat16)]
    return jnp.stack(outputs)


def solution(mesh):
    in_specs = (
        P(None, ("dp", "expert"), "tensor"),
        P(("dp", "expert"), None, "tensor"),
        P(("dp", "expert"), None, "tensor"),
        P(("dp", "expert"), "tensor", None),
        P(None, ("dp", "expert"), None),
        P(None, ("dp", "expert"), None),
    )
    out_specs = P(None, ("dp", "expert"), "tensor")
    return jax.shard_map(local, mesh=mesh, in_specs=in_specs, out_specs=out_specs, check_vma=False)
```

profile of v0, /device:TPU:0, one launch (start us, length us, event | category | flops | bytes accessed | tf_op | source)
XLA Modules:
  0.0 110.7 jit_solution(10478560798243014809)
XLA Ops:
  6.5 0.0 copy-start
  6.5 0.0 all-gather.2.cloned.1.call-start
  6.5 0.8 copy.17
  7.3 0.1 eq.51
  7.4 0.1 fusion.25
  7.5 0.2 reduce_window_sum.11
  7.7 0.2 select_reduce_fusion
  7.8 0.1 reduce_sum.42
  7.9 0.1 copy.18
  8.0 0.7 bitcast_add_fusion
  8.7 0.1 copy.19
  8.8 0.1 fusion.23
  8.9 0.0 copy-done
  8.9 0.4 convolution_convert_fusion.1
  9.3 32.9 %all_to_all.10 = bf16[16,16,1792]{2,1,0:T(8,128)(2,1)} all-to-all(bf16[16,16,1792]{2,1,0:T(8,128)(2,1)S(1)} %bitcast.39), channel_id=1, replica_groups=mesh['dp'=4,'expert'=4,'tensor'=2] {'dp','expert'}, dimensions={0} | all-to-all | bytes 1835008 | tf_op jit(solution)/shard_map/all_to_all | solution.py:30
  42.2 0.0 all-gather.2.cloned.1.call-update
  42.2 0.0 reduce-scatter.2.cloned.1.call-start
  42.3 7.5 %all-gather.2.cloned.1.call-done = bf16[256,3584]{1,0:T(8,128)(2,1)} async-done(((bf16[256,1792]{1,0:T(8,128)(2,1)}), bf16[256,3584]{1,0:T(8,128)(2,1)}) %all-gather.2.cloned.1.call-update) | async-done | bytes 1835024 | tf_op jit(solution)/shard_map/all_gather | solution.py:32
  49.8 0.0 copy-start.2
  49.8 3.8 %fusion.3 = f32[256,512]{1,0:T(8,128)S(1)} fusion(bf16[256,3584]{1,0:T(8,128)(2,1)} %all-gather.2.cloned.1.call-done, bf16[1,3584,512]{2,1,0:T(8,128)(2,1)} %param.7), kind=kOutput, calls=%fused_computation.4 | convolution fusion | flops 939524096 | bytes 6029312 | tf_op jit(solution)/shard_map/dot_general | solution.py:33
  53.6 0.0 copy-done.2
  53.7 6.6 %convolution_convert_fusion = bf16[256,3584]{1,0:T(8,128)(2,1)} fusion(bf16[1,512,3584]{2,1,0:T(8,128)(2,1)} %param.9, bf16[256,3584]{1,0:T(8,128)(2,1)S(1)} %copy-done.2, bf16[1,3584,512]{2,1,0:T(8,128)(2,1)} %param.8, f32[256,512]{1,0:T(8,128)S(1)} %fusion.3), kind=kOutput, calls=%fused_computation | convolution fusion | flops 1880752128 | bytes 11534336 | tf_op jit(solution)/shard_map/dot_general | solution.py:36
  60.2 0.0 copy-start.1
  60.2 0.0 reduce-scatter.2.cloned.1.call-update
  60.2 10.6 %reduce-scatter.2.cloned.1.call-done = bf16[256,1792]{1,0:T(8,128)(2,1)} async-done(((bf16[256,3584]{1,0:T(8,128)(2,1)}), bf16[256,1792]{1,0:T(8,128)(2,1)}) %reduce-scatter.2.cloned.1.call-update) | async-done | bytes 917520 | tf_op jit(solution)/shard_map/reduce_scatter | solution.py:38
  70.9 6.9 %all-to-all-start.1 = ((bf16[16,16,1792]{2,1,0:T(8,128)(2,1)}), bf16[16,16,1792]{2,1,0:T(8,128)(2,1)S(1)}, u32[]{:S(2)}, u32[]{:S(2)}) async-start(bf16[16,16,1792]{2,1,0:T(8,128)(2,1)} %bitcast.40), calls=%async_computation.2 | async-start | bytes 1835008 | tf_op jit(solution)/shard_map/all_to_all | solution.py:44
  77.8 0.0 copy-done.1
  77.8 0.1 copy.21
  77.9 24.9 %all-to-all-done.1 = bf16[16,16,1792]{2,1,0:T(8,128)(2,1)S(1)} async-done(((bf16[16,16,1792]{2,1,0:T(8,128)(2,1)}), bf16[16,16,1792]{2,1,0:T(8,128)(2,1)S(1)}, u32[]{:S(2)}, u32[]{:S(2)}) %all-to-all-start.1) | async-done | bytes 917536 | tf_op jit(solution)/shard_map/all_to_all | solution.py:44
  102.8 1.1 fusion.8
  (2 shorter events, 0.0 us)
Async XLA Ops:
  6.5 2.4 %copy-start = (bf16[1,16,1792]{2,1,0:T(8,128)(2,1)S(1)}, bf16[1,16,1792]{2,1,0:T(8,128)(2,1)}, u32[]{:S(2)}) copy-start(bf16[1,16,1792]{2,1,0:T(8,128)(2,1)} %param.6) | copy-start | bytes 172036
  6.5 43.3 %all-gather.2.cloned.1.call-start = ((), (), s32[]{:S(2)}) async-start(), calls=%async_computation.3 | async-start | bytes 2752512 | tf_op jit(solution)/shard_map/all_gather | solution.py:32
  42.2 28.6 %reduce-scatter.2.cloned.1.call-start = ((), (), s32[]{:S(2)}) async-start(), calls=%async_computation.4 | async-start | bytes 2752512 | tf_op jit(solution)/shard_map/reduce_scatter | solution.py:38
  49.8 3.8 %copy-start.2 = (bf16[256,3584]{1,0:T(8,128)(2,1)S(1)}, bf16[256,3584]{1,0:T(8,128)(2,1)}, u32[]{:S(2)}) copy-start(bf16[256,3584]{1,0:T(8,128)(2,1)} %all-gather.2.cloned.1.call-done) | copy-start | bytes 5505028
  60.2 17.6 %copy-start.1 = (s32[1,16,8]{1,2,0:T(8,128)S(1)}, s32[1,16,8]{1,2,0:T(8,128)}, u32[]{:S(2)}) copy-start(s32[1,16,8]{1,2,0:T(8,128)} %param.11) | copy-start | bytes 1540
  70.9 31.9 %all-to-all-start.1 = ((bf16[16,16,1792]{2,1,0:T(8,128)(2,1)}), bf16[16,16,1792]{2,1,0:T(8,128)(2,1)S(1)}, u32[]{:S(2)}, u32[]{:S(2)}) async-start(bf16[16,16,1792]{2,1,0:T(8,128)(2,1)} %bitcast.40), calls=%async_computation.2 | async-start | bytes 1835008 | tf_op jit(solution)/shard_map/all_to_all | solution.py:44
Sparse Core Ops, SparseCore 0:
  42.4 7.3 all-gather.1
  60.4 10.4 reduce-scatter.1
where the time goes:
time: 111 us
  waiting for transfers between devices  43 us (39%)
  blocking collectives  32.9 us (30%)
  between operations  13.5 us (12%)
  matrix products  11.9 us (11%)
  starting transfers between devices  6.97 us (6%)
  other arithmetic  1.28 us (1%)
  local copies, waits for them, and re-layouts  1.18 us (1%)
    all_to_all x1, blocking collectives, local(): lax.all_to_all(packed, ('dp', 'expert'), split_axis=0, concat_axis=0, til...  32.9 us
    all_to_all x1, waiting for transfers between devices, local(): lax.all_to_all(result, ('dp', 'expert'), split_axis=0, concat_axis=0, til...  24.9 us
    reduce_scatter x1, waiting for transfers between devices, local(): lax.psum_scatter(partial_value, 'tensor', scatter_dimension=1, tiled=True)  10.6 us
    all_gather x1, waiting for transfers between devices, local(): owner_rows = lax.all_gather(owner_rows, 'tensor', axis=1, tiled=True)  7.52 us
    all_to_all x1, starting transfers between devices, local(): lax.all_to_all(result, ('dp', 'expert'), split_axis=0, concat_axis=0, til...  6.92 us
    dot_general x1, matrix products, local(): jnp.dot(hidden, w_down, preferred_element_type=jnp.float32)  6.57 us
    dot_general x1, matrix products, local(): gated = jnp.dot(owner_rows, w_gate, preferred_element_type=jnp.float32)  3.82 us
  transfers between devices with their start and end apart: 3, of which 3 were waited for; matrix products, arithmetic and copies ran while one was open for 0% of the time, Pallas kernels for 0%

commit v1 on v0

--- a/solution.py
+++ b/solution.py
@@ -1,14 +1,21 @@
+import functools
+
 import jax
 import jax.numpy as jnp
 from jax import lax
+from jax.experimental import pallas as pl
+from jax.experimental.pallas import tpu as pltpu
 from jax.sharding import PartitionSpec as P
 
 
-def local(tokens, gate_weight, up_weight, down_weight, expert_ids, gate_codes):
+LANES = 128
+STALL = 20000000000
+
+
+def slotted(tokens, gate_weight, up_weight, down_weight, expert_ids, gate_codes, slot_depth):
     owners = lax.axis_size("dp") * lax.axis_size("expert")
     tok_rows = tokens.shape[1]
     top_count = expert_ids.shape[2]
-    slot_depth = min(tok_rows, max(2, 2 * tok_rows * top_count // owners))
     slot_count = owners * slot_depth
     w_gate = gate_weight[0]
     w_up = up_weight[0]
@@ -49,8 +56,190 @@
     mixed_rows = jnp.sum(
         picked.reshape(tok_rows, top_count, half_width) * shares[:, :, None], axis=1
     )
-    outputs = [mixed_rows.astype(jnp.bfloat16)]
-    return jnp.stack(outputs)
+    return mixed_rows.astype(jnp.bfloat16)[None]
+
+
+def swap(x, axis, offset):
+    count = lax.axis_size(axis)
+    return lax.ppermute(x, axis, [(i, i ^ offset) for i in range(count)])
+
+
+TILE = 256
+VMEM = pl.BlockSpec(memory_space=pltpu.VMEM)
+F32, BF16 = jnp.float32, jnp.bfloat16
+
+
+def call(body, outs, *args, flops=0, scratch=(), limit=2):
+    return pl.pallas_call(
+        body,
+        out_shape=outs,
+        in_specs=[VMEM] * len(args),
+        out_specs=jax.tree.map(lambda _: VMEM, outs),
+        scratch_shapes=scratch,
+        compiler_params=pltpu.CompilerParams(vmem_limit_bytes=limit * 2**20),
+        cost_estimate=pl.CostEstimate(flops=flops, bytes_accessed=0, transcendentals=0),
+    )(*args)
+
+
+def table(owners, out_ref):
+    out_ref[...] = lax.rem(lax.broadcasted_iota(jnp.int32, out_ref.shape, 1), owners)
+
+
+def prepare(owners, tok_ref, ids_ref, codes_ref, expert_ref, out_ref):
+    width = tok_ref.shape[1]
+    rows = tok_ref.shape[0]
+    top_count = ids_ref.shape[0]
+    out_ref[:, :width] = tok_ref[...]
+    ids = jnp.transpose(ids_ref[...])
+    codes = jnp.transpose(codes_ref[...].astype(F32))
+    shares = codes / jnp.sum(codes, axis=1, keepdims=True)
+    lane = lax.broadcasted_iota(jnp.int32, (rows, LANES), 1)
+    expert = expert_ref[...]
+    dense = jnp.zeros((rows, LANES), F32)
+    for k in range(top_count):
+        dense += jnp.where(ids[:, k : k + 1] == expert, shares[:, k : k + 1], 0.0)
+    high = dense.astype(BF16)
+    low = (dense - high.astype(F32)).astype(BF16)
+    out_ref[:, width:] = jnp.where(lane < owners, high, jnp.where(lane < 2 * owners, low, jnp.zeros_like(high)))
+
+
+def stack(blocks, flops=0):
+    def body(*refs):
+        start = 0
+        for ref in refs[:-1]:
+            refs[-1][start : start + ref.shape[0], :] = ref[...]
+            start += ref.shape[0]
+
+    rows = sum(b.shape[0] for b in blocks)
+    return call(body, jax.ShapeDtypeStruct((rows, blocks[0].shape[1]), BF16), *blocks, flops=flops)
+
+
+def dot(a, b):
+    return jnp.dot(a, b, preferred_element_type=F32)
+
+
+def plus(*values):
+    total = values[0].astype(F32)
+    for value in values[1:]:
+        total = total + value.astype(F32)
+    return total
+
+
+def ffn(groups, owners, *refs):
+    own, other = refs[:groups], refs[groups : 2 * groups]
+    gate, up, down = refs[2 * groups : 2 * groups + 3]
+    keep, send = refs[2 * groups + 3 : 3 * groups + 3], refs[3 * groups + 3 : 4 * groups + 3]
+    x_own, x_other, hidden = refs[4 * groups + 3 :]
+    rows, width = keep[0].shape
+    half = lax.axis_index("tensor")
+    expert = lax.axis_index("dp") * lax.axis_size("expert") + lax.axis_index("expert")
+    first = pl.ds(pl.multiple_of(half * width, LANES), width)
+    second = pl.ds(pl.multiple_of((1 - half) * width, LANES), width)
+    scales = []
+    for g in range(groups):
+        there = pl.ds(g * rows, rows)
+        x_own[there, :] = own[g][:, :width]
+        x_other[there, :] = other[g][:, :width]
+        lane = lax.broadcasted_iota(jnp.int32, (rows, LANES), 1)
+        mine = (lane == expert) | (lane == expert + owners)
+        scales.append(jnp.sum(jnp.where(mine, own[g][:, width:].astype(F32), 0.0), axis=1, keepdims=True))
+
+    @pl.loop(0, hidden.shape[1] // TILE)
+    def _(i):
+        columns = pl.ds(pl.multiple_of(i * TILE, TILE), TILE)
+        a, b = x_own[...], x_other[...]
+        gated = dot(a, gate[first, columns]) + dot(b, gate[second, columns])
+        lifted = dot(a, up[first, columns]) + dot(b, up[second, columns])
+        hidden[:, columns] = (jax.nn.silu(gated) * lifted).astype(BF16)
+
+    @pl.loop(0, width // TILE)
+    def _(i):
+        columns = pl.ds(pl.multiple_of(i * TILE, TILE), TILE)
+        h = hidden[...]
+        for start, outs in (((1 - half) * width, send), (half * width, keep)):
+            value = dot(h, down[:, pl.ds(pl.multiple_of(start + i * TILE, LANES), TILE)])
+            for g in range(groups):
+                outs[g][:, columns] = (value[g * rows : (g + 1) * rows] * scales[g]).astype(BF16)
+
+
+def dense(tokens, gate_weight, up_weight, down_weight, expert_ids, gate_codes):
+    dp, ex = lax.axis_size("dp"), lax.axis_size("expert")
+    owners = dp * ex
+    n, width = tokens.shape[1:]
+    units = gate_weight.shape[2]
+    hops = range(1, ex)
+    rows = ex * n
+
+    def block(count):
+        return jax.ShapeDtypeStruct((count, width), BF16)
+
+    experts = call(functools.partial(table, owners), jax.ShapeDtypeStruct((n, LANES), jnp.int32), flops=STALL)
+    first = call(
+        functools.partial(prepare, owners),
+        jax.ShapeDtypeStruct((n, width + LANES), BF16),
+        tokens[0], expert_ids[0].T, gate_codes[0].T, experts,
+    )
+    line = {j: swap(first, "expert", j) for j in reversed(hops)}
+    corner = swap(first, "dp", 3)
+    diag = {j: swap(corner, "expert", j) for j in reversed(hops)}
+    near = stack([first] + [line[j] for j in hops], flops=STALL)
+    own = [near, swap(near, "dp", 1), swap(near, "dp", 2), stack([corner] + [diag[j] for j in hops], flops=STALL)]
+    other = [swap(own[g], "tensor", 1) for g in range(dp)]
+    weights = 3 * 2 * width * units
+    results = call(
+        functools.partial(ffn, dp, owners),
+        [block(rows)] * (2 * dp),
+        *own, *other, gate_weight[0], up_weight[0], down_weight[0],
+        flops=2 * weights * dp * rows, limit=24,
+        scratch=[pltpu.VMEM((dp * rows, width), BF16)] * 2 + [pltpu.VMEM((dp * rows, units), BF16)],
+    )
+    keep, send = results[:dp], results[dp:]
+    back = {g: swap(send[g], "tensor", 1) for g in (1, 2, 3, 0)}
+
+    def add(keep, recv, out):
+        out[...] = plus(keep[...], recv[...]).astype(BF16)
+
+    def add_split(keep, recv, *outs):
+        for i, out in enumerate(outs):
+            there = pl.ds((i + 1) * n, n)
+            out[...] = plus(keep[there, :], recv[there, :]).astype(BF16)
+
+    sides = {g: swap(call(add, block(rows), keep[g], back[g]), "dp", g) for g in (1, 2)}
+    parts = call(add_split, [block(n)] * (ex - 1), keep[3], back[3])
+    spread = [swap(parts[j - 1], "expert", j) for j in reversed(hops)]
+
+    def add_diag(keep, recv, *rest):
+        here = pl.ds(0, n)
+        rest[-1][...] = plus(keep[here, :], recv[here, :], *[r[...] for r in rest[:-1]]).astype(BF16)
+
+    def add_line(keep, recv, x, y, *outs):
+        for i, out in enumerate(outs):
+            there = pl.ds((i + 1) * n, n)
+            out[...] = plus(keep[there, :], recv[there, :], x[there, :], y[there, :]).astype(BF16)
+
+    lines = call(add_line, [block(n)] * (ex - 1), keep[0], back[0], sides[1], sides[2])
+    ends = [swap(lines[j - 1], "expert", j) for j in reversed(hops)]
+    turned = call(add_diag, block(n), keep[3], back[3], *spread)
+    ends.append(swap(turned, "dp", 3))
+
+    def add_end(keep, recv, x, y, *rest):
+        here = pl.ds(0, n)
+        rest[-1][...] = plus(keep[here, :], recv[here, :], x[here, :], y[here, :], *[r[...] for r in rest[:-1]]).astype(BF16)
+
+    return call(add_end, block(n), keep[0], back[0], sides[1], sides[2], *ends)[None]
+
+
+def local(tokens, gate_weight, up_weight, down_weight, expert_ids, gate_codes):
+    dp, ex = lax.axis_size("dp"), lax.axis_size("expert")
+    owners = dp * ex
+    tok_rows = tokens.shape[1]
+    top_count = expert_ids.shape[2]
+    slot_depth = min(tok_rows, max(2, 2 * tok_rows * top_count // owners))
+    args = (tokens, gate_weight, up_weight, down_weight, expert_ids, gate_codes)
+    grid = dp == 4 and ex & (ex - 1) == 0 and ex > 1 and lax.axis_size("tensor") == 2
+    if slot_depth == tok_rows and grid and 2 * owners <= LANES:
+        return dense(*args)
+    return slotted(*args, slot_depth)
 
 
 def solution(mesh):

time: 111 us -> 55.7 us (0.50)
  blocking collectives: 32.9 us -> 0 us
  waiting for transfers between devices: 43 us -> 23.5 us
  starting transfers between devices: 6.97 us -> 25.2 us
  between operations: 13.5 us -> 0.12 us
  matrix products: 11.9 us -> 0 us
  Pallas kernels: 0 us -> 5.8 us
  other arithmetic: 1.28 us -> 0 us
    all_to_all x1 -> x0, blocking collectives: 32.9 us -> none  [local(): lax.all_to_all(packed, ('dp', 'expert'), split_axis=0, concat_axis=0, til...]
    ppermute x0 -> x26, starting transfers between devices: none -> 25.2 us  [swap(): return lax.ppermute(x, axis, [(i, i ^ offset) for i in range(count)])]
    all_to_all x1 -> x0, waiting for transfers between devices: 24.9 us -> none  [local(): lax.all_to_all(result, ('dp', 'expert'), split_axis=0, concat_axis=0, til...]
    ppermute x0 -> x26, waiting for transfers between devices: none -> 23.5 us  [swap(): return lax.ppermute(x, axis, [(i, i ^ offset) for i in range(count)])]
    dot_general x4 -> x0, matrix products: 11.9 us -> none  [the longest x1 6.57 us: local(): jnp.dot(hidden, w_down, preferred_element_type=jnp.float32)]
    reduce_scatter x1 -> x0, waiting for transfers between devices: 10.6 us -> none  [local(): lax.psum_scatter(partial_value, 'tensor', scatter_dimension=1, tiled=True)]
    all_gather x1 -> x0, waiting for transfers between devices: 7.52 us -> none  [local(): owner_rows = lax.all_gather(owner_rows, 'tensor', axis=1, tiled=True)]
    all_to_all x1 -> x0, starting transfers between devices: 6.92 us -> none  [local(): lax.all_to_all(result, ('dp', 'expert'), split_axis=0, concat_axis=0, til...]
  transfers between devices with their start and end apart: 3 -> 26, of which waited for: 3 -> 12; matrix products, arithmetic and copies ran while one was open for 0% -> 0% of each run, Pallas kernels for 0% -> 1%
where the time goes in v1:
time: 55.7 us; the launch traced here: 55.5 us
  starting transfers between devices  25.2 us (45%)
  waiting for transfers between devices  23.5 us (42%)
  Pallas kernels  5.8 us (10%)
  local copies, waits for them, and re-layouts  0.86 us (2%)
    ppermute x26, starting transfers between devices, swap(): return lax.ppermute(x, axis, [(i, i ^ offset) for i in range(count)])  25.2 us
    ppermute x26, waiting for transfers between devices, swap(): return lax.ppermute(x, axis, [(i, i ^ offset) for i in range(count)])  23.5 us
    pallas_call x11, Pallas kernels, call(): pl.pallas_call(body, out_shape=outs, in_specs=[VMEM] * len(args), out_spe...  5.8 us
  transfers between devices with their start and end apart: 26, of which 12 were waited for; matrix products, arithmetic and copies ran while one was open for 0% of the time, Pallas kernels for 1%

profile of v1, /device:TPU:0, one launch (start us, length us, event | category | flops | bytes accessed | tf_op | source)
XLA Modules:
  0.0 55.5 jit_solution(13955488526309921027)
XLA Ops:
  0.0 0.7 %copy-done.5 = s32[1,16,8]{1,2,0:T(8,128)S(1)} copy-done((s32[1,16,8]{1,2,0:T(8,128)S(1)}, s32[1,16,8]{1,2,0:T(8,128)}, u32[]{:S(2)}) %copy-start.5) | copy-done | bytes 536
  0.7 0.0 copy-done.4
  0.7 0.1 copy-done.3
  0.9 0.3 shard_map.65.refs_0_
  1.1 4.0 %collective-permute-start.5 = (bf16[16,1920]{1,0:T(8,128)(2,1)S(1)}, bf16[16,1920]{1,0:T(8,128)(2,1)S(1)}, u32[]{:S(2)}, u32[]{:S(2)}) collective-permute-start(bf16[16,1920]{1,0:T(8,128)(2,1)S(1)} %shard_map.65.refs_0_), channel_id=1, source_target_pairs={{0,24},{8,16},{16,8},{24,0},{1,25},{9,17},{17,9},{25,1},{2,26},{10... | collective-permute-start | bytes 184328 | tf_op jit(solution)/shard_map/ppermute | solution.py:64
  5.1 3.6 %collective-permute-start.2 = (bf16[16,1920]{1,0:T(8,128)(2,1)S(1)}, bf16[16,1920]{1,0:T(8,128)(2,1)S(1)}, u32[]{:S(2)}, u32[]{:S(2)}) collective-permute-start(bf16[16,1920]{1,0:T(8,128)(2,1)S(1)} %shard_map.65.refs_0_), channel_id=1, source_target_pairs={{0,6},{2,4},{4,2},{6,0},{1,7},{3,5},{5,3},{7,1},{8,14},{10,12},{12... | collective-permute-start | bytes 184328 | tf_op jit(solution)/shard_map/ppermute | solution.py:64
  8.7 0.0 collective-permute-start.1
  8.7 0.8 %collective-permute-start = (bf16[16,1920]{1,0:T(8,128)(2,1)S(1)}, bf16[16,1920]{1,0:T(8,128)(2,1)S(1)}, u32[]{:S(2)}, u32[]{:S(2)}) collective-permute-start(bf16[16,1920]{1,0:T(8,128)(2,1)S(1)} %shard_map.65.refs_0_), channel_id=1, source_target_pairs={{0,2},{2,0},{4,6},{6,4},{1,3},{3,1},{5,7},{7,5},{8,10},{10,8},{12,... | collective-permute-start | bytes 184328 | tf_op jit(solution)/shard_map/ppermute | solution.py:64
  9.5 0.0 collective-permute-done.5.refs_0_
  9.5 3.6 %collective-permute-start.8 = (bf16[16,1920]{1,0:T(8,128)(2,1)S(1)}, bf16[16,1920]{1,0:T(8,128)(2,1)S(1)}, u32[]{:S(2)}, u32[]{:S(2)}) collective-permute-start(bf16[16,1920]{1,0:T(8,128)(2,1)S(1)} %collective-permute-done.5.refs_0_), channel_id=1, source_target_pairs={{0,6},{2,4},{4,2},{6,0},{1,7},{3,5},{5,3},{7,1},{8,14},{10,12},{12... | collective-permute-start | bytes 184328 | tf_op jit(solution)/shard_map/ppermute | solution.py:64
  13.1 0.0 collective-permute-start.7
  13.1 0.0 collective-permute-done.2.refs_3_
  13.1 0.8 %collective-permute-start.6 = (bf16[16,1920]{1,0:T(8,128)(2,1)S(1)}, bf16[16,1920]{1,0:T(8,128)(2,1)S(1)}, u32[]{:S(2)}, u32[]{:S(2)}) collective-permute-start(bf16[16,1920]{1,0:T(8,128)(2,1)S(1)} %collective-permute-done.5.refs_0_), channel_id=1, source_target_pairs={{0,2},{2,0},{4,6},{6,4},{1,3},{3,1},{5,7},{7,5},{8,10},{10,8},{12,... | collective-permute-start | bytes 184328 | tf_op jit(solution)/shard_map/ppermute | solution.py:64
  13.9 2.9 %collective-permute-done.1.refs_2_ = bf16[16,1920]{1,0:T(8,128)(2,1)S(1)} collective-permute-done((bf16[16,1920]{1,0:T(8,128)(2,1)S(1)}, bf16[16,1920]{1,0:T(8,128)(2,1)S(1)}, u32[]{:S(2)}, u32[]{:S(2)}) %collective-permute-start.1) | collective-permute-done | bytes 61472 | tf_op jit(solution)/shard_map/ppermute | solution.py:64
  16.8 0.0 collective-permute-done.refs_1_
  16.8 0.0 copy-start
  16.8 0.0 copy-start.1
  16.9 0.0 copy-start.2
  16.9 0.1 collective-permute-start.9
  16.9 0.6 %collective-permute-start.4 = (bf16[64,1920]{1,0:T(8,128)(2,1)S(1)}, bf16[64,1920]{1,0:T(8,128)(2,1)S(1)}, u32[]{:S(2)}, u32[]{:S(2)}) collective-permute-start(bf16[64,1920]{1,0:T(8,128)(2,1)S(1)} %shard_map.66.refs_0_), channel_id=1, source_target_pairs={{0,16},{8,24},{16,0},{24,8},{1,17},{9,25},{17,1},{25,9},{2,18},{10... | collective-permute-start | bytes 737288 | tf_op jit(solution)/shard_map/ppermute | solution.py:64
  17.5 0.0 collective-permute-done.8.refs_3_
  17.5 0.2 collective-permute-start.3
  17.7 1.3 %collective-permute-done.7.refs_2_ = bf16[16,1920]{1,0:T(8,128)(2,1)S(1)} collective-permute-done((bf16[16,1920]{1,0:T(8,128)(2,1)S(1)}, bf16[16,1920]{1,0:T(8,128)(2,1)S(1)}, u32[]{:S(2)}, u32[]{:S(2)}) %collective-permute-start.7) | collective-permute-done | bytes 61472 | tf_op jit(solution)/shard_map/ppermute | solution.py:64
  19.0 0.0 collective-permute-done.6.refs_1_
  19.0 0.1 collective-permute-start.12
  19.1 6.2 %collective-permute-done.4.refs_2_ = bf16[64,1920]{1,0:T(8,128)(2,1)S(1)} collective-permute-done((bf16[64,1920]{1,0:T(8,128)(2,1)S(1)}, bf16[64,1920]{1,0:T(8,128)(2,1)S(1)}, u32[]{:S(2)}, u32[]{:S(2)}) %collective-permute-start.4) | collective-permute-done | bytes 245792 | tf_op jit(solution)/shard_map/ppermute | solution.py:64
  25.3 0.0 collective-permute-start.11
  25.3 0.2 collective-permute-done.3.refs_1_
  25.5 0.3 collective-permute-start.10
  25.8 0.0 collective-permute-done.9.refs_4_
  25.8 0.0 collective-permute-done.12.refs_7_
  25.8 1.0 %collective-permute-done.11.refs_6_ = bf16[64,1920]{1,0:T(8,128)(2,1)S(1)} collective-permute-done((bf16[64,1920]{1,0:T(8,128)(2,1)S(1)}, bf16[64,1920]{1,0:T(8,128)(2,1)S(1)}, u32[]{:S(2)}, u32[]{:S(2)}) %collective-permute-start.11) | collective-permute-done | bytes 245792 | tf_op jit(solution)/shard_map/ppermute | solution.py:64
  26.8 0.4 collective-permute-done.10.refs_5_
  27.2 4.5 %shard_map.68 = (bf16[64,1792]{1,0:T(8,128)(2,1)S(1)}, bf16[64,1792]{1,0:T(8,128)(2,1)S(1)}, bf16[64,1792]{1,0:T(8,128)(2,1)S(1)}, bf16[64,1792]{1,0:T(8,128)(2,...) custom-call(bf16[64,1920]{1,0:T(8,128)(2,1)S(1)} %shard_map.66.refs_, ...), custom_call_target="tpu_custom_call" | custom-call | flops 2818572288 | tf_op jit(solution)/shard_map/pallas_call | solution.py:73
  31.7 0.2 collective-permute-start.14
  32.0 0.3 collective-permute-start.16
  32.3 0.2 collective-permute-start.21
  32.5 0.3 collective-permute-start.13
  32.8 0.5 collective-permute-done.14.recv
  33.3 0.1 shard_map.69
  33.3 0.6 %collective-permute-start.15 = (bf16[64,1792]{1,0:T(8,128)(2,1)S(1)}, bf16[64,1792]{1,0:T(8,128)(2,1)S(1)}, u32[]{:S(2)}, u32[]{:S(2)}) collective-permute-start(bf16[64,1792]{1,0:T(8,128)(2,1)S(1)} %shard_map.69), channel_id=1, source_target_pairs={{0,8},{8,0},{16,24},{24,16},{1,9},{9,1},{17,25},{25,17},{2,10},{10... | collective-permute-start | bytes 688136 | tf_op jit(solution)/shard_map/ppermute | solution.py:64
  33.9 0.0 collective-permute-done.16.recv
  33.9 0.1 shard_map.70
  34.0 1.5 %collective-permute-start.17 = (bf16[64,1792]{1,0:T(8,128)(2,1)S(1)}, bf16[64,1792]{1,0:T(8,128)(2,1)S(1)}, u32[]{:S(2)}, u32[]{:S(2)}) collective-permute-start(bf16[64,1792]{1,0:T(8,128)(2,1)S(1)} %shard_map.70), channel_id=1, source_target_pairs={{0,16},{8,24},{16,0},{24,8},{1,17},{9,25},{17,1},{25,9},{2,18},{10... | collective-permute-start | bytes 688136 | tf_op jit(solution)/shard_map/ppermute | solution.py:64
  35.5 0.0 collective-permute-done.21.recv
  35.5 2.1 %collective-permute-start.22 = (bf16[16,1792]{1,0:T(8,128)(2,1)S(1)}, bf16[16,1792]{1,0:T(8,128)(2,1)S(1)}, u32[]{:S(2)}, u32[]{:S(2)}) collective-permute-start(bf16[16,1792]{1,0:T(8,128)(2,1)S(1)} %get-tuple-element.30), channel_id=1, source_target_pairs={{0,6},{2,4},{4,2},{6,0},{1,7},{3,5},{5,3},{7,1},{8,14},{10,12},{12... | collective-permute-start | bytes 172040 | tf_op jit(solution)/shard_map/ppermute | solution.py:64
  37.6 0.0 collective-permute-start.23
  37.6 4.0 %collective-permute-done.22.rest_0_ = bf16[16,1792]{1,0:T(8,128)(2,1)S(1)} collective-permute-done((bf16[16,1792]{1,0:T(8,128)(2,1)S(1)}, bf16[16,1792]{1,0:T(8,128)(2,1)S(1)}, u32[]{:S(2)}, u32[]{:S(2)}) %collective-permute-start.22) | collective-permute-done | bytes 57376 | tf_op jit(solution)/shard_map/ppermute | solution.py:64
  41.6 0.0 collective-permute-start.24
  41.6 1.7 %collective-permute-done.23.rest_1_ = bf16[16,1792]{1,0:T(8,128)(2,1)S(1)} collective-permute-done((bf16[16,1792]{1,0:T(8,128)(2,1)S(1)}, bf16[16,1792]{1,0:T(8,128)(2,1)S(1)}, u32[]{:S(2)}, u32[]{:S(2)}) %collective-permute-start.23) | collective-permute-done | bytes 57376 | tf_op jit(solution)/shard_map/ppermute | solution.py:64
  43.3 2.4 %collective-permute-done.24.rest_2_ = bf16[16,1792]{1,0:T(8,128)(2,1)S(1)} collective-permute-done((bf16[16,1792]{1,0:T(8,128)(2,1)S(1)}, bf16[16,1792]{1,0:T(8,128)(2,1)S(1)}, u32[]{:S(2)}, u32[]{:S(2)}) %collective-permute-start.24) | collective-permute-done | bytes 57376 | tf_op jit(solution)/shard_map/ppermute | solution.py:64
  45.8 1.6 %collective-permute-start.25 = (bf16[16,1792]{1,0:T(8,128)(2,1)S(1)}, bf16[16,1792]{1,0:T(8,128)(2,1)S(1)}, u32[]{:S(2)}, u32[]{:S(2)}) collective-permute-start(bf16[16,1792]{1,0:T(8,128)(2,1)S(1)} %shard_map.73), channel_id=1, source_target_pairs={{0,24},{8,16},{16,8},{24,0},{1,25},{9,17},{17,9},{25,1},{2,26},{10... | collective-permute-start | bytes 172040 | tf_op jit(solution)/shard_map/ppermute | solution.py:64
  47.4 0.0 collective-permute-done.13.recv
  47.4 0.0 collective-permute-done.15.x
  47.4 0.0 collective-permute-done.17.y
  47.4 0.1 shard_map.71
  47.5 2.1 %collective-permute-start.18 = (bf16[16,1792]{1,0:T(8,128)(2,1)S(1)}, bf16[16,1792]{1,0:T(8,128)(2,1)S(1)}, u32[]{:S(2)}, u32[]{:S(2)}) collective-permute-start(bf16[16,1792]{1,0:T(8,128)(2,1)S(1)} %get-tuple-element.25), channel_id=1, source_target_pairs={{0,6},{2,4},{4,2},{6,0},{1,7},{3,5},{5,3},{7,1},{8,14},{10,12},{12... | collective-permute-start | bytes 172040 | tf_op jit(solution)/shard_map/ppermute | solution.py:64
  49.6 0.0 collective-permute-start.19
  49.6 2.4 %collective-permute-start.20 = (bf16[16,1792]{1,0:T(8,128)(2,1)S(1)}, bf16[16,1792]{1,0:T(8,128)(2,1)S(1)}, u32[]{:S(2)}, u32[]{:S(2)}) collective-permute-start(bf16[16,1792]{1,0:T(8,128)(2,1)S(1)} %get-tuple-element.27), channel_id=1, source_target_pairs={{0,2},{2,0},{4,6},{6,4},{1,3},{3,1},{5,7},{7,5},{8,10},{10,8},{12,... | collective-permute-start | bytes 172040 | tf_op jit(solution)/shard_map/ppermute | solution.py:64
  52.0 0.0 collective-permute-done.25.rest_3_
  52.0 1.6 %collective-permute-done.18.rest_0_ = bf16[16,1792]{1,0:T(8,128)(2,1)S(1)} collective-permute-done((bf16[16,1792]{1,0:T(8,128)(2,1)S(1)}, bf16[16,1792]{1,0:T(8,128)(2,1)S(1)}, u32[]{:S(2)}, u32[]{:S(2)}) %collective-permute-start.18) | collective-permute-done | bytes 57376 | tf_op jit(solution)/shard_map/ppermute | solution.py:64
  53.5 1.2 %collective-permute-done.19.rest_1_ = bf16[16,1792]{1,0:T(8,128)(2,1)S(1)} collective-permute-done((bf16[16,1792]{1,0:T(8,128)(2,1)S(1)}, bf16[16,1792]{1,0:T(8,128)(2,1)S(1)}, u32[]{:S(2)}, u32[]{:S(2)}) %collective-permute-start.19) | collective-permute-done | bytes 57376 | tf_op jit(solution)/shard_map/ppermute | solution.py:64
  54.8 0.0 collective-permute-done.20.rest_2_
  54.8 0.7 %shard_map.74 = bf16[16,1792]{1,0:T(8,128)(2,1)} custom-call(bf16[64,1792]{1,0:T(8,128)(2,1)S(1)} %get-tuple-element.19.keep, bf16[64,1792]{1,0:T(8,128)(2,1)S(1)} %collective-permute-done.13.recv, bf16[64,1792]{1,0:T(8,128)(2,1)S(1)} %collective-permute-done.15.x, bf16[64,1792]{1,0:T(8,128)(2,1)S(1)} %collective-permute-done.17.y, ...), custom_call_target="tpu_custom_call" | custom-call | tf_op jit(solution)/shard_map/pallas_call | solution.py:73
  (11 shorter events, 0.1 us)
Async XLA Ops:
  0.0 0.7 %copy-start.5 = (s32[1,16,8]{1,2,0:T(8,128)S(1)}, s32[1,16,8]{1,2,0:T(8,128)}, u32[]{:S(2)}) copy-start(s32[1,16,8]{1,2,0:T(8,128)} %param.11) | copy-start | bytes 1540
  0.0 0.7 %copy-start.4 = (s32[1,16,8]{1,2,0:T(8,128)S(1)}, s32[1,16,8]{1,2,0:T(8,128)}, u32[]{:S(2)}) copy-start(s32[1,16,8]{1,2,0:T(8,128)} %param.10) | copy-start | bytes 1540
  0.0 0.8 %copy-start.3 = (bf16[1,16,1792]{2,1,0:T(8,128)(2,1)S(1)}, bf16[1,16,1792]{2,1,0:T(8,128)(2,1)}, u32[]{:S(2)}) copy-start(bf16[1,16,1792]{2,1,0:T(8,128)(2,1)} %param.6) | copy-start | bytes 172036
  1.1 8.4 %collective-permute-start.5 = (bf16[16,1920]{1,0:T(8,128)(2,1)S(1)}, bf16[16,1920]{1,0:T(8,128)(2,1)S(1)}, u32[]{:S(2)}, u32[]{:S(2)}) collective-permute-start(bf16[16,1920]{1,0:T(8,128)(2,1)S(1)} %shard_map.65.refs_0_), channel_id=1, source_target_pairs={{0,24},{8,16},{16,8},{24,0},{1,25},{9,17},{17,9},{25,1},{2,26},{10... | collective-permute-start | bytes 184328 | tf_op jit(solution)/shard_map/ppermute | solution.py:64
  5.1 8.0 %collective-permute-start.2 = (bf16[16,1920]{1,0:T(8,128)(2,1)S(1)}, bf16[16,1920]{1,0:T(8,128)(2,1)S(1)}, u32[]{:S(2)}, u32[]{:S(2)}) collective-permute-start(bf16[16,1920]{1,0:T(8,128)(2,1)S(1)} %shard_map.65.refs_0_), channel_id=1, source_target_pairs={{0,6},{2,4},{4,2},{6,0},{1,7},{3,5},{5,3},{7,1},{8,14},{10,12},{12... | collective-permute-start | bytes 184328 | tf_op jit(solution)/shard_map/ppermute | solution.py:64
  8.7 8.1 %collective-permute-start.1 = (bf16[16,1920]{1,0:T(8,128)(2,1)S(1)}, bf16[16,1920]{1,0:T(8,128)(2,1)S(1)}, u32[]{:S(2)}, u32[]{:S(2)}) collective-permute-start(bf16[16,1920]{1,0:T(8,128)(2,1)S(1)} %shard_map.65.refs_0_), channel_id=1, source_target_pairs={{0,4},{2,6},{4,0},{6,2},{1,5},{3,7},{5,1},{7,3},{8,12},{10,14},{12... | collective-permute-start | bytes 184328 | tf_op jit(solution)/shard_map/ppermute | solution.py:64
  8.7 8.1 %collective-permute-start = (bf16[16,1920]{1,0:T(8,128)(2,1)S(1)}, bf16[16,1920]{1,0:T(8,128)(2,1)S(1)}, u32[]{:S(2)}, u32[]{:S(2)}) collective-permute-start(bf16[16,1920]{1,0:T(8,128)(2,1)S(1)} %shard_map.65.refs_0_), channel_id=1, source_target_pairs={{0,2},{2,0},{4,6},{6,4},{1,3},{3,1},{5,7},{7,5},{8,10},{10,8},{12,... | collective-permute-start | bytes 184328 | tf_op jit(solution)/shard_map/ppermute | solution.py:64
  9.5 8.0 %collective-permute-start.8 = (bf16[16,1920]{1,0:T(8,128)(2,1)S(1)}, bf16[16,1920]{1,0:T(8,128)(2,1)S(1)}, u32[]{:S(2)}, u32[]{:S(2)}) collective-permute-start(bf16[16,1920]{1,0:T(8,128)(2,1)S(1)} %collective-permute-done.5.refs_0_), channel_id=1, source_target_pairs={{0,6},{2,4},{4,2},{6,0},{1,7},{3,5},{5,3},{7,1},{8,14},{10,12},{12... | collective-permute-start | bytes 184328 | tf_op jit(solution)/shard_map/ppermute | solution.py:64
  13.1 5.9 %collective-permute-start.7 = (bf16[16,1920]{1,0:T(8,128)(2,1)S(1)}, bf16[16,1920]{1,0:T(8,128)(2,1)S(1)}, u32[]{:S(2)}, u32[]{:S(2)}) collective-permute-start(bf16[16,1920]{1,0:T(8,128)(2,1)S(1)} %collective-permute-done.5.refs_0_), channel_id=1, source_target_pairs={{0,4},{2,6},{4,0},{6,2},{1,5},{3,7},{5,1},{7,3},{8,12},{10,14},{12... | collective-permute-start | bytes 184328 | tf_op jit(solution)/shard_map/ppermute | solution.py:64
  13.1 5.9 %collective-permute-start.6 = (bf16[16,1920]{1,0:T(8,128)(2,1)S(1)}, bf16[16,1920]{1,0:T(8,128)(2,1)S(1)}, u32[]{:S(2)}, u32[]{:S(2)}) collective-permute-start(bf16[16,1920]{1,0:T(8,128)(2,1)S(1)} %collective-permute-done.5.refs_0_), channel_id=1, source_target_pairs={{0,2},{2,0},{4,6},{6,4},{1,3},{3,1},{5,7},{7,5},{8,10},{10,8},{12,... | collective-permute-start | bytes 184328 | tf_op jit(solution)/shard_map/ppermute | solution.py:64
  16.8 10.3 %copy-start = (bf16[1,3584,512]{2,1,0:T(8,128)(2,1)S(1)}, bf16[1,3584,512]{2,1,0:T(8,128)(2,1)}, u32[]{:S(2)}) copy-start(bf16[1,3584,512]{2,1,0:T(8,128)(2,1)} %param.7) | copy-start | bytes 11010052
  16.8 10.3 %copy-start.1 = (bf16[1,3584,512]{2,1,0:T(8,128)(2,1)S(1)}, bf16[1,3584,512]{2,1,0:T(8,128)(2,1)}, u32[]{:S(2)}) copy-start(bf16[1,3584,512]{2,1,0:T(8,128)(2,1)} %param.8) | copy-start | bytes 11010052
  16.9 10.3 %copy-start.2 = (bf16[1,512,3584]{2,1,0:T(8,128)(2,1)S(1)}, bf16[1,512,3584]{2,1,0:T(8,128)(2,1)}, u32[]{:S(2)}) copy-start(bf16[1,512,3584]{2,1,0:T(8,128)(2,1)} %param.9) | copy-start | bytes 11010052
  16.9 9.0 %collective-permute-start.9 = (bf16[64,1920]{1,0:T(8,128)(2,1)S(1)}, bf16[64,1920]{1,0:T(8,128)(2,1)S(1)}, u32[]{:S(2)}, u32[]{:S(2)}) collective-permute-start(bf16[64,1920]{1,0:T(8,128)(2,1)S(1)} %shard_map.66.refs_0_), channel_id=1, source_target_pairs={{0,1},{1,0},{2,3},{3,2},{4,5},{5,4},{6,7},{7,6},{8,9},{9,8},{10,11... | collective-permute-start | bytes 737288 | tf_op jit(solution)/shard_map/ppermute | solution.py:64
  16.9 8.4 %collective-permute-start.4 = (bf16[64,1920]{1,0:T(8,128)(2,1)S(1)}, bf16[64,1920]{1,0:T(8,128)(2,1)S(1)}, u32[]{:S(2)}, u32[]{:S(2)}) collective-permute-start(bf16[64,1920]{1,0:T(8,128)(2,1)S(1)} %shard_map.66.refs_0_), channel_id=1, source_target_pairs={{0,16},{8,24},{16,0},{24,8},{1,17},{9,25},{17,1},{25,9},{2,18},{10... | collective-permute-start | bytes 737288 | tf_op jit(solution)/shard_map/ppermute | solution.py:64
  17.5 8.0 %collective-permute-start.3 = (bf16[64,1920]{1,0:T(8,128)(2,1)S(1)}, bf16[64,1920]{1,0:T(8,128)(2,1)S(1)}, u32[]{:S(2)}, u32[]{:S(2)}) collective-permute-start(bf16[64,1920]{1,0:T(8,128)(2,1)S(1)} %shard_map.66.refs_0_), channel_id=1, source_target_pairs={{0,8},{8,0},{16,24},{24,16},{1,9},{9,1},{17,25},{25,17},{2,10},{10... | collective-permute-start | bytes 737288 | tf_op jit(solution)/shard_map/ppermute | solution.py:64
  19.0 6.8 %collective-permute-start.12 = (bf16[64,1920]{1,0:T(8,128)(2,1)S(1)}, bf16[64,1920]{1,0:T(8,128)(2,1)S(1)}, u32[]{:S(2)}, u32[]{:S(2)}) collective-permute-start(bf16[64,1920]{1,0:T(8,128)(2,1)S(1)} %shard_map.67.refs_3_), channel_id=1, source_target_pairs={{0,1},{1,0},{2,3},{3,2},{4,5},{5,4},{6,7},{7,6},{8,9},{9,8},{10,11... | collective-permute-start | bytes 737288 | tf_op jit(solution)/shard_map/ppermute | solution.py:64
  25.3 1.5 %collective-permute-start.11 = (bf16[64,1920]{1,0:T(8,128)(2,1)S(1)}, bf16[64,1920]{1,0:T(8,128)(2,1)S(1)}, u32[]{:S(2)}, u32[]{:S(2)}) collective-permute-start(bf16[64,1920]{1,0:T(8,128)(2,1)S(1)} %collective-permute-done.4.refs_2_), channel_id=1, source_target_pairs={{0,1},{1,0},{2,3},{3,2},{4,5},{5,4},{6,7},{7,6},{8,9},{9,8},{10,11... | collective-permute-start | bytes 737288 | tf_op jit(solution)/shard_map/ppermute | solution.py:64
  25.5 1.6 %collective-permute-start.10 = (bf16[64,1920]{1,0:T(8,128)(2,1)S(1)}, bf16[64,1920]{1,0:T(8,128)(2,1)S(1)}, u32[]{:S(2)}, u32[]{:S(2)}) collective-permute-start(bf16[64,1920]{1,0:T(8,128)(2,1)S(1)} %collective-permute-done.3.refs_1_), channel_id=1, source_target_pairs={{0,1},{1,0},{2,3},{3,2},{4,5},{5,4},{6,7},{7,6},{8,9},{9,8},{10,11... | collective-permute-start | bytes 737288 | tf_op jit(solution)/shard_map/ppermute | solution.py:64
  31.7 1.6 %collective-permute-start.14 = (bf16[64,1792]{1,0:T(8,128)(2,1)S(1)}, bf16[64,1792]{1,0:T(8,128)(2,1)S(1)}, u32[]{:S(2)}, u32[]{:S(2)}) collective-permute-start(bf16[64,1792]{1,0:T(8,128)(2,1)S(1)} %get-tuple-element.22), channel_id=1, source_target_pairs={{0,1},{1,0},{2,3},{3,2},{4,5},{5,4},{6,7},{7,6},{8,9},{9,8},{10,11... | collective-permute-start | bytes 688136 | tf_op jit(solution)/shard_map/ppermute | solution.py:64
  32.0 2.0 %collective-permute-start.16 = (bf16[64,1792]{1,0:T(8,128)(2,1)S(1)}, bf16[64,1792]{1,0:T(8,128)(2,1)S(1)}, u32[]{:S(2)}, u32[]{:S(2)}) collective-permute-start(bf16[64,1792]{1,0:T(8,128)(2,1)S(1)} %get-tuple-element.24), channel_id=1, source_target_pairs={{0,1},{1,0},{2,3},{3,2},{4,5},{5,4},{6,7},{7,6},{8,9},{9,8},{10,11... | collective-permute-start | bytes 688136 | tf_op jit(solution)/shard_map/ppermute | solution.py:64
  32.3 3.2 %collective-permute-start.21 = (bf16[64,1792]{1,0:T(8,128)(2,1)S(1)}, bf16[64,1792]{1,0:T(8,128)(2,1)S(1)}, u32[]{:S(2)}, u32[]{:S(2)}) collective-permute-start(bf16[64,1792]{1,0:T(8,128)(2,1)S(1)} %get-tuple-element.29), channel_id=1, source_target_pairs={{0,1},{1,0},{2,3},{3,2},{4,5},{5,4},{6,7},{7,6},{8,9},{9,8},{10,11... | collective-permute-start | bytes 688136 | tf_op jit(solution)/shard_map/ppermute | solution.py:64
  32.5 14.9 %collective-permute-start.13 = (bf16[64,1792]{1,0:T(8,128)(2,1)S(1)}, bf16[64,1792]{1,0:T(8,128)(2,1)S(1)}, u32[]{:S(2)}, u32[]{:S(2)}) collective-permute-start(bf16[64,1792]{1,0:T(8,128)(2,1)S(1)} %get-tuple-element.20), channel_id=1, source_target_pairs={{0,1},{1,0},{2,3},{3,2},{4,5},{5,4},{6,7},{7,6},{8,9},{9,8},{10,11... | collective-permute-start | bytes 688136 | tf_op jit(solution)/shard_map/ppermute | solution.py:64
  33.3 14.1 %collective-permute-start.15 = (bf16[64,1792]{1,0:T(8,128)(2,1)S(1)}, bf16[64,1792]{1,0:T(8,128)(2,1)S(1)}, u32[]{:S(2)}, u32[]{:S(2)}) collective-permute-start(bf16[64,1792]{1,0:T(8,128)(2,1)S(1)} %shard_map.69), channel_id=1, source_target_pairs={{0,8},{8,0},{16,24},{24,16},{1,9},{9,1},{17,25},{25,17},{2,10},{10... | collective-permute-start | bytes 688136 | tf_op jit(solution)/shard_map/ppermute | solution.py:64
  34.0 13.4 %collective-permute-start.17 = (bf16[64,1792]{1,0:T(8,128)(2,1)S(1)}, bf16[64,1792]{1,0:T(8,128)(2,1)S(1)}, u32[]{:S(2)}, u32[]{:S(2)}) collective-permute-start(bf16[64,1792]{1,0:T(8,128)(2,1)S(1)} %shard_map.70), channel_id=1, source_target_pairs={{0,16},{8,24},{16,0},{24,8},{1,17},{9,25},{17,1},{25,9},{2,18},{10... | collective-permute-start | bytes 688136 | tf_op jit(solution)/shard_map/ppermute | solution.py:64
  35.5 6.0 %collective-permute-start.22 = (bf16[16,1792]{1,0:T(8,128)(2,1)S(1)}, bf16[16,1792]{1,0:T(8,128)(2,1)S(1)}, u32[]{:S(2)}, u32[]{:S(2)}) collective-permute-start(bf16[16,1792]{1,0:T(8,128)(2,1)S(1)} %get-tuple-element.30), channel_id=1, source_target_pairs={{0,6},{2,4},{4,2},{6,0},{1,7},{3,5},{5,3},{7,1},{8,14},{10,12},{12... | collective-permute-start | bytes 172040 | tf_op jit(solution)/shard_map/ppermute | solution.py:64
  37.6 5.7 %collective-permute-start.23 = (bf16[16,1792]{1,0:T(8,128)(2,1)S(1)}, bf16[16,1792]{1,0:T(8,128)(2,1)S(1)}, u32[]{:S(2)}, u32[]{:S(2)}) collective-permute-start(bf16[16,1792]{1,0:T(8,128)(2,1)S(1)} %get-tuple-element.31), channel_id=1, source_target_pairs={{0,4},{2,6},{4,0},{6,2},{1,5},{3,7},{5,1},{7,3},{8,12},{10,14},{12... | collective-permute-start | bytes 172040 | tf_op jit(solution)/shard_map/ppermute | solution.py:64
  41.6 4.2 %collective-permute-start.24 = (bf16[16,1792]{1,0:T(8,128)(2,1)S(1)}, bf16[16,1792]{1,0:T(8,128)(2,1)S(1)}, u32[]{:S(2)}, u32[]{:S(2)}) collective-permute-start(bf16[16,1792]{1,0:T(8,128)(2,1)S(1)} %get-tuple-element.32), channel_id=1, source_target_pairs={{0,2},{2,0},{4,6},{6,4},{1,3},{3,1},{5,7},{7,5},{8,10},{10,8},{12,... | collective-permute-start | bytes 172040 | tf_op jit(solution)/shard_map/ppermute | solution.py:64
  45.8 6.2 %collective-permute-start.25 = (bf16[16,1792]{1,0:T(8,128)(2,1)S(1)}, bf16[16,1792]{1,0:T(8,128)(2,1)S(1)}, u32[]{:S(2)}, u32[]{:S(2)}) collective-permute-start(bf16[16,1792]{1,0:T(8,128)(2,1)S(1)} %shard_map.73), channel_id=1, source_target_pairs={{0,24},{8,16},{16,8},{24,0},{1,25},{9,17},{17,9},{25,1},{2,26},{10... | collective-permute-start | bytes 172040 | tf_op jit(solution)/shard_map/ppermute | solution.py:64
  47.5 6.0 %collective-permute-start.18 = (bf16[16,1792]{1,0:T(8,128)(2,1)S(1)}, bf16[16,1792]{1,0:T(8,128)(2,1)S(1)}, u32[]{:S(2)}, u32[]{:S(2)}) collective-permute-start(bf16[16,1792]{1,0:T(8,128)(2,1)S(1)} %get-tuple-element.25), channel_id=1, source_target_pairs={{0,6},{2,4},{4,2},{6,0},{1,7},{3,5},{5,3},{7,1},{8,14},{10,12},{12... | collective-permute-start | bytes 172040 | tf_op jit(solution)/shard_map/ppermute | solution.py:64
  49.6 5.2 %collective-permute-start.19 = (bf16[16,1792]{1,0:T(8,128)(2,1)S(1)}, bf16[16,1792]{1,0:T(8,128)(2,1)S(1)}, u32[]{:S(2)}, u32[]{:S(2)}) collective-permute-start(bf16[16,1792]{1,0:T(8,128)(2,1)S(1)} %get-tuple-element.26), channel_id=1, source_target_pairs={{0,4},{2,6},{4,0},{6,2},{1,5},{3,7},{5,1},{7,3},{8,12},{10,14},{12... | collective-permute-start | bytes 172040 | tf_op jit(solution)/shard_map/ppermute | solution.py:64
  49.6 5.2 %collective-permute-start.20 = (bf16[16,1792]{1,0:T(8,128)(2,1)S(1)}, bf16[16,1792]{1,0:T(8,128)(2,1)S(1)}, u32[]{:S(2)}, u32[]{:S(2)}) collective-permute-start(bf16[16,1792]{1,0:T(8,128)(2,1)S(1)} %get-tuple-element.27), channel_id=1, source_target_pairs={{0,2},{2,0},{4,6},{6,4},{1,3},{3,1},{5,7},{7,5},{8,10},{10,8},{12,... | collective-permute-start | bytes 172040 | tf_op jit(solution)/shard_map/ppermute | solution.py:64

commit v2 on v1

--- a/solution.py
+++ b/solution.py
@@ -10,6 +10,8 @@
 
 LANES = 128
 STALL = 20000000000
+EARLY = 2
+TILE = 256
 
 
 def slotted(tokens, gate_weight, up_weight, down_weight, expert_ids, gate_codes, slot_depth):
@@ -64,7 +66,6 @@
     return lax.ppermute(x, axis, [(i, i ^ offset) for i in range(count)])
 
 
-TILE = 256
 VMEM = pl.BlockSpec(memory_space=pltpu.VMEM)
 F32, BF16 = jnp.float32, jnp.bfloat16
 
@@ -125,41 +126,23 @@
     return total
 
 
-def ffn(groups, owners, *refs):
-    own, other = refs[:groups], refs[groups : 2 * groups]
-    gate, up, down = refs[2 * groups : 2 * groups + 3]
-    keep, send = refs[2 * groups + 3 : 3 * groups + 3], refs[3 * groups + 3 : 4 * groups + 3]
-    x_own, x_other, hidden = refs[4 * groups + 3 :]
-    rows, width = keep[0].shape
+def ffn(owners, own, other, gate, up, down, keep, send, x, hidden):
+    rows, width = keep.shape
     half = lax.axis_index("tensor")
     expert = lax.axis_index("dp") * lax.axis_size("expert") + lax.axis_index("expert")
-    first = pl.ds(pl.multiple_of(half * width, LANES), width)
-    second = pl.ds(pl.multiple_of((1 - half) * width, LANES), width)
-    scales = []
-    for g in range(groups):
-        there = pl.ds(g * rows, rows)
-        x_own[there, :] = own[g][:, :width]
-        x_other[there, :] = other[g][:, :width]
-        lane = lax.broadcasted_iota(jnp.int32, (rows, LANES), 1)
-        mine = (lane == expert) | (lane == expert + owners)
-        scales.append(jnp.sum(jnp.where(mine, own[g][:, width:].astype(F32), 0.0), axis=1, keepdims=True))
-
-    @pl.loop(0, hidden.shape[1] // TILE)
-    def _(i):
-        columns = pl.ds(pl.multiple_of(i * TILE, TILE), TILE)
-        a, b = x_own[...], x_other[...]
-        gated = dot(a, gate[first, columns]) + dot(b, gate[second, columns])
-        lifted = dot(a, up[first, columns]) + dot(b, up[second, columns])
-        hidden[:, columns] = (jax.nn.silu(gated) * lifted).astype(BF16)
-
-    @pl.loop(0, width // TILE)
-    def _(i):
-        columns = pl.ds(pl.multiple_of(i * TILE, TILE), TILE)
-        h = hidden[...]
-        for start, outs in (((1 - half) * width, send), (half * width, keep)):
-            value = dot(h, down[:, pl.ds(pl.multiple_of(start + i * TILE, LANES), TILE)])
-            for g in range(groups):
-                outs[g][:, columns] = (value[g * rows : (g + 1) * rows] * scales[g]).astype(BF16)
+    mine_at = pl.ds(pl.multiple_of(half * width, LANES), width)
+    other_at = pl.ds(pl.multiple_of((1 - half) * width, LANES), width)
+    x[:, mine_at] = own[:, :width]
+    x[:, other_at] = other[:, :width]
+    lane = lax.broadcasted_iota(jnp.int32, (rows, LANES), 1)
+    mine = (lane == expert) | (lane == expert + owners)
+    scale = jnp.sum(jnp.where(mine, own[:, width:].astype(F32), 0.0), axis=1, keepdims=True)
+    for i in range(0, hidden.shape[1], TILE):
+        at = pl.ds(i, TILE)
+        gated, lifted = dot(x[...], gate[:, at]), dot(x[...], up[:, at])
+        hidden[:, at] = (jax.nn.silu(gated) * lifted).astype(BF16)
+    for at, out in ((other_at, send), (mine_at, keep)):
+        out[...] = (dot(hidden[...], down[:, at]) * scale).astype(BF16)
 
 
 def dense(tokens, gate_weight, up_weight, down_weight, expert_ids, gate_codes):
@@ -180,36 +163,50 @@
         tokens[0], expert_ids[0].T, gate_codes[0].T, experts,
     )
     line = {j: swap(first, "expert", j) for j in reversed(hops)}
-    corner = swap(first, "dp", 3)
-    diag = {j: swap(corner, "expert", j) for j in reversed(hops)}
-    near = stack([first] + [line[j] for j in hops], flops=STALL)
-    own = [near, swap(near, "dp", 1), swap(near, "dp", 2), stack([corner] + [diag[j] for j in hops], flops=STALL)]
-    other = [swap(own[g], "tensor", 1) for g in range(dp)]
-    weights = 3 * 2 * width * units
-    results = call(
-        functools.partial(ffn, dp, owners),
-        [block(rows)] * (2 * dp),
-        *own, *other, gate_weight[0], up_weight[0], down_weight[0],
-        flops=2 * weights * dp * rows, limit=24,
-        scratch=[pltpu.VMEM((dp * rows, width), BF16)] * 2 + [pltpu.VMEM((dp * rows, units), BF16)],
-    )
-    keep, send = results[:dp], results[dp:]
-    back = {g: swap(send[g], "tensor", 1) for g in (1, 2, 3, 0)}
-
-    def add(keep, recv, out):
-        out[...] = plus(keep[...], recv[...]).astype(BF16)
-
-    def add_split(keep, recv, *outs):
-        for i, out in enumerate(outs):
-            there = pl.ds((i + 1) * n, n)
-            out[...] = plus(keep[there, :], recv[there, :]).astype(BF16)
-
-    sides = {g: swap(call(add, block(rows), keep[g], back[g]), "dp", g) for g in (1, 2)}
-    parts = call(add_split, [block(n)] * (ex - 1), keep[3], back[3])
-    spread = [swap(parts[j - 1], "expert", j) for j in reversed(hops)]
+    early = [first] + [line[j] for j in range(1, EARLY)]
+    late = [line[j] for j in range(EARLY, ex)]
+    parts_a = stack(early)
+    parts_b = stack(late, flops=STALL)
+    sent_a = {g: swap(parts_a, "dp", g) for g in range(1, dp)}
+    sent_b = {g: swap(parts_b, "dp", g) for g in range(1, dp)}
+    near = stack([parts_a, parts_b] + [sent_a[g] for g in range(1, dp)])
+    far = stack([sent_b[g] for g in range(1, dp)], flops=STALL)
+    matrices = gate_weight[0], up_weight[0], down_weight[0]
+
+    def run(own):
+        count = own.shape[0]
+        return call(
+            functools.partial(ffn, owners),
+            [block(count)] * 2,
+            own, swap(own, "tensor", 1), *matrices,
+            flops=STALL, limit=16,
+            scratch=[pltpu.VMEM((count, 2 * width), BF16), pltpu.VMEM((count, units), BF16)],
+        )
+
+    keep_a, send_a = run(near)
+    keep_b, send_b = run(far)
+    recv_a = swap(send_a, "tensor", 1)
+    recv_b = swap(send_b, "tensor", 1)
+    cut = EARLY * n
+
+    def add_far(keep_a, recv_a, keep_b, recv_b, x, y, *diag):
+        for g, out in ((1, x), (2, y)):
+            here, there = pl.ds(rows + (g - 1) * cut, cut), pl.ds((g - 1) * (rows - cut), rows - cut)
+            out[:cut, :] = plus(keep_a[here, :], recv_a[here, :]).astype(BF16)
+            out[cut:, :] = plus(keep_b[there, :], recv_b[there, :]).astype(BF16)
+        for j, out in zip(hops, diag):
+            if j < EARLY:
+                keep, recv, here = keep_a, recv_a, pl.ds(rows + 2 * cut + j * n, n)
+            else:
+                keep, recv, here = keep_b, recv_b, pl.ds(2 * (rows - cut) + (j - EARLY) * n, n)
+            out[...] = plus(keep[here, :], recv[here, :]).astype(BF16)
+
+    x, y, *diag = call(add_far, [block(rows)] * 2 + [block(n)] * (ex - 1), keep_a, recv_a, keep_b, recv_b)
+    sides = [swap(x, "dp", 1), swap(y, "dp", 2)]
+    spread = [swap(diag[j - 1], "expert", j) for j in reversed(hops)]
 
     def add_diag(keep, recv, *rest):
-        here = pl.ds(0, n)
+        here = pl.ds(rows + 2 * cut, n)
         rest[-1][...] = plus(keep[here, :], recv[here, :], *[r[...] for r in rest[:-1]]).astype(BF16)
 
     def add_line(keep, recv, x, y, *outs):
@@ -217,16 +214,15 @@
             there = pl.ds((i + 1) * n, n)
             out[...] = plus(keep[there, :], recv[there, :], x[there, :], y[there, :]).astype(BF16)
 
-    lines = call(add_line, [block(n)] * (ex - 1), keep[0], back[0], sides[1], sides[2])
+    lines = call(add_line, [block(n)] * (ex - 1), keep_a, recv_a, *sides)
     ends = [swap(lines[j - 1], "expert", j) for j in reversed(hops)]
-    turned = call(add_diag, block(n), keep[3], back[3], *spread)
-    ends.append(swap(turned, "dp", 3))
+    ends.append(swap(call(add_diag, block(n), keep_a, recv_a, *spread), "dp", 3))
 
     def add_end(keep, recv, x, y, *rest):
         here = pl.ds(0, n)
         rest[-1][...] = plus(keep[here, :], recv[here, :], x[here, :], y[here, :], *[r[...] for r in rest[:-1]]).astype(BF16)
 
-    return call(add_end, block(n), keep[0], back[0], sides[1], sides[2], *ends)[None]
+    return call(add_end, block(n), keep_a, recv_a, *sides, *ends)[None]
 
 
 def local(tokens, gate_weight, up_weight, down_weight, expert_ids, gate_codes):

time: 55.7 us -> 50.7 us (0.910)
  waiting for transfers between devices: 23.5 us -> 16.6 us
  starting transfers between devices: 25.2 us -> 27.1 us
    ppermute x26 -> x22, waiting for transfers between devices: 23.5 us -> 16.6 us  [swap(): return lax.ppermute(x, axis, [(i, i ^ offset) for i in range(count)])]
    ppermute x26 -> x22, starting transfers between devices: 25.2 us -> 27.1 us  [swap(): return lax.ppermute(x, axis, [(i, i ^ offset) for i in range(count)])]
    pallas_call x11 -> x12, Pallas kernels: 5.8 us -> 5.35 us  [call(): pl.pallas_call(body, out_shape=outs, in_specs=[VMEM] * len(args), out_spe...]
  transfers between devices with their start and end apart: 26 -> 22, of which waited for: 12 -> 12; matrix products, arithmetic and copies ran while one was open for 0% -> 0% of each run, Pallas kernels for 1% -> 8%
where the time goes in v2:
time: 50.7 us; the launch traced here: 50.6 us
  starting transfers between devices  27.1 us (53%)
  waiting for transfers between devices  16.6 us (33%)
  Pallas kernels  5.35 us (11%)
  local copies, waits for them, and re-layouts  1.41 us (3%)
    ppermute x22, starting transfers between devices, swap(): return lax.ppermute(x, axis, [(i, i ^ offset) for i in range(count)])  27.1 us
    ppermute x22, waiting for transfers between devices, swap(): return lax.ppermute(x, axis, [(i, i ^ offset) for i in range(count)])  16.6 us
    pallas_call x12, Pallas kernels, call(): pl.pallas_call(body, out_shape=outs, in_specs=[VMEM] * len(args), out_spe...  5.35 us
    unnamed x12, local copies, waits for them, and re-layouts  1.41 us
  transfers between devices with their start and end apart: 22, of which 12 were waited for; matrix products, arithmetic and copies ran while one was open for 0% of the time, Pallas kernels for 8%

profile of v2, /device:TPU:0, one launch (start us, length us, event | category | flops | bytes accessed | tf_op | source)
XLA Modules:
  0.0 50.6 jit_solution(4243842071622642760)
XLA Ops:
  0.0 0.0 copy-start
  0.0 0.0 copy-start.1
  0.0 0.0 copy-start.2
  0.0 0.8 %copy-done = bf16[1,16,1792]{2,1,0:T(8,128)(2,1)S(1)} copy-done((bf16[1,16,1792]{2,1,0:T(8,128)(2,1)S(1)}, bf16[1,16,1792]{2,1,0:T(8,128)(2,1)}, u32[]{:S(2)}) %copy-start) | copy-done | bytes 57368
  0.8 0.0 copy-done.1
  0.8 0.0 copy-done.2
  0.8 0.3 shard_map.65.refs_0_
  1.1 3.1 %collective-permute-start = (bf16[16,1920]{1,0:T(8,128)(2,1)S(1)}, bf16[16,1920]{1,0:T(8,128)(2,1)S(1)}, u32[]{:S(2)}, u32[]{:S(2)}) collective-permute-start(bf16[16,1920]{1,0:T(8,128)(2,1)S(1)} %shard_map.65.refs_0_), channel_id=1, source_target_pairs={{0,2},{2,0},{4,6},{6,4},{1,3},{3,1},{5,7},{7,5},{8,10},{10,8},{12,... | collective-permute-start | bytes 184328 | tf_op jit(solution)/shard_map/ppermute | solution.py:66
  4.2 2.6 %collective-permute-start.1 = (bf16[16,1920]{1,0:T(8,128)(2,1)S(1)}, bf16[16,1920]{1,0:T(8,128)(2,1)S(1)}, u32[]{:S(2)}, u32[]{:S(2)}) collective-permute-start(bf16[16,1920]{1,0:T(8,128)(2,1)S(1)} %shard_map.65.refs_0_), channel_id=1, source_target_pairs={{0,4},{2,6},{4,0},{6,2},{1,5},{3,7},{5,1},{7,3},{8,12},{10,14},{12... | collective-permute-start | bytes 184328 | tf_op jit(solution)/shard_map/ppermute | solution.py:66
  6.8 0.0 collective-permute-start.2
  6.8 0.0 collective-permute-done.refs_1_
  6.8 1.8 %collective-permute-start.3 = (bf16[32,1920]{1,0:T(8,128)(2,1)S(1)}, bf16[32,1920]{1,0:T(8,128)(2,1)S(1)}, u32[]{:S(2)}, u32[]{:S(2)}) collective-permute-start(bf16[32,1920]{1,0:T(8,128)(2,1)S(1)} %shard_map.66.refs_0_), channel_id=1, source_target_pairs={{0,8},{8,0},{16,24},{24,16},{1,9},{9,1},{17,25},{25,17},{2,10},{10... | collective-permute-start | bytes 368648 | tf_op jit(solution)/shard_map/ppermute | solution.py:66
  8.6 1.5 %collective-permute-start.4 = (bf16[32,1920]{1,0:T(8,128)(2,1)S(1)}, bf16[32,1920]{1,0:T(8,128)(2,1)S(1)}, u32[]{:S(2)}, u32[]{:S(2)}) collective-permute-start(bf16[32,1920]{1,0:T(8,128)(2,1)S(1)} %shard_map.66.refs_0_), channel_id=1, source_target_pairs={{0,16},{8,24},{16,0},{24,8},{1,17},{9,25},{17,1},{25,9},{2,18},{10... | collective-permute-start | bytes 368648 | tf_op jit(solution)/shard_map/ppermute | solution.py:66
  10.1 0.3 collective-permute-start.5
  10.4 0.2 collective-permute-done.1.refs_0_
  10.6 2.3 %collective-permute-done.2.refs_1_ = bf16[16,1920]{1,0:T(8,128)(2,1)S(1)} collective-permute-done((bf16[16,1920]{1,0:T(8,128)(2,1)S(1)}, bf16[16,1920]{1,0:T(8,128)(2,1)S(1)}, u32[]{:S(2)}, u32[]{:S(2)}) %collective-permute-start.2) | collective-permute-done | bytes 61472 | tf_op jit(solution)/shard_map/ppermute | solution.py:66
  12.8 2.5 %collective-permute-start.10 = (bf16[32,1920]{1,0:T(8,128)(2,1)S(1)}, bf16[32,1920]{1,0:T(8,128)(2,1)S(1)}, u32[]{:S(2)}, u32[]{:S(2)}) collective-permute-start(bf16[32,1920]{1,0:T(8,128)(2,1)S(1)} %shard_map.67.refs_1_), channel_id=1, source_target_pairs={{0,24},{8,16},{16,8},{24,0},{1,25},{9,17},{17,9},{25,1},{2,26},{10... | collective-permute-start | bytes 368648 | tf_op jit(solution)/shard_map/ppermute | solution.py:66
  15.3 0.5 %collective-permute-start.8 = (bf16[32,1920]{1,0:T(8,128)(2,1)S(1)}, bf16[32,1920]{1,0:T(8,128)(2,1)S(1)}, u32[]{:S(2)}, u32[]{:S(2)}) collective-permute-start(bf16[32,1920]{1,0:T(8,128)(2,1)S(1)} %shard_map.67.refs_1_), channel_id=1, source_target_pairs={{0,8},{8,0},{16,24},{24,16},{1,9},{9,1},{17,25},{25,17},{2,10},{10... | collective-permute-start | bytes 368648 | tf_op jit(solution)/shard_map/ppermute | solution.py:66
  15.9 0.0 collective-permute-done.3.refs_2_
  15.9 0.5 %collective-permute-start.9 = (bf16[32,1920]{1,0:T(8,128)(2,1)S(1)}, bf16[32,1920]{1,0:T(8,128)(2,1)S(1)}, u32[]{:S(2)}, u32[]{:S(2)}) collective-permute-start(bf16[32,1920]{1,0:T(8,128)(2,1)S(1)} %shard_map.67.refs_1_), channel_id=1, source_target_pairs={{0,16},{8,24},{16,0},{24,8},{1,17},{9,25},{17,1},{25,9},{2,18},{10... | collective-permute-start | bytes 368648 | tf_op jit(solution)/shard_map/ppermute | solution.py:66
  16.4 1.4 %collective-permute-done.4.refs_3_ = bf16[32,1920]{1,0:T(8,128)(2,1)S(1)} collective-permute-done((bf16[32,1920]{1,0:T(8,128)(2,1)S(1)}, bf16[32,1920]{1,0:T(8,128)(2,1)S(1)}, u32[]{:S(2)}, u32[]{:S(2)}) %collective-permute-start.4) | collective-permute-done | bytes 122912 | tf_op jit(solution)/shard_map/ppermute | solution.py:66
  17.8 0.0 collective-permute-done.5.refs_4_
  17.8 0.0 copy-start.3
  17.9 0.0 copy-start.4
  17.9 0.0 copy-start.5
  17.9 0.1 collective-permute-start.6
  18.0 1.9 %collective-permute-done.10.refs_2_ = bf16[32,1920]{1,0:T(8,128)(2,1)S(1)} collective-permute-done((bf16[32,1920]{1,0:T(8,128)(2,1)S(1)}, bf16[32,1920]{1,0:T(8,128)(2,1)S(1)}, u32[]{:S(2)}, u32[]{:S(2)}) %collective-permute-start.10) | collective-permute-done | bytes 122912 | tf_op jit(solution)/shard_map/ppermute | solution.py:66
  19.8 0.4 collective-permute-done.8.refs_0_
  20.2 1.1 %collective-permute-done.9.refs_1_ = bf16[32,1920]{1,0:T(8,128)(2,1)S(1)} collective-permute-done((bf16[32,1920]{1,0:T(8,128)(2,1)S(1)}, bf16[32,1920]{1,0:T(8,128)(2,1)S(1)}, u32[]{:S(2)}, u32[]{:S(2)}) %collective-permute-start.9) | collective-permute-done | bytes 122912 | tf_op jit(solution)/shard_map/ppermute | solution.py:66
  21.4 0.1 collective-permute-start.11
  21.4 0.0 collective-permute-done.6.other
  21.5 0.0 copy-done.3
  21.5 0.0 copy-done.4
  21.5 0.6 %copy-done.5 = bf16[1,512,3584]{2,1,0:T(8,128)(2,1)S(1)} copy-done((bf16[1,512,3584]{2,1,0:T(8,128)(2,1)S(1)}, bf16[1,512,3584]{2,1,0:T(8,128)(2,1)}, u32[]{:S(2)}) %copy-start.5) | copy-done | bytes 3670040
  22.1 2.1 %shard_map.69 = (bf16[160,1792]{1,0:T(8,128)(2,1)S(1)}, bf16[160,1792]{1,0:T(8,128)(2,1)S(1)}) custom-call(bf16[160,1920]{1,0:T(8,128)(2,1)S(1)} %shard_map.68.own, bf16[160,1920]{1,0:T(8,128)(2,1)S(1)} %collective-permute-done.6.other, bf16[3584,512]{1,0:T(8,128)(2,1)S(1)} %bitcast.14, bf16[3584,512]{1,0:T(8,128)(2,1)S(1)} %bitcast.16, ...), custom_call_target="tpu_custom_call" | custom-call | flops 20000000000 | tf_op jit(solution)/shard_map/pallas_call | solution.py:74
  24.2 0.1 collective-permute-start.7
  24.3 0.0 collective-permute-done.11.other
  24.3 1.9 %shard_map.71 = (bf16[96,1792]{1,0:T(8,128)(2,1)S(1)}, bf16[96,1792]{1,0:T(8,128)(2,1)S(1)}) custom-call(bf16[96,1920]{1,0:T(8,128)(2,1)S(1)} %shard_map.70.own, bf16[96,1920]{1,0:T(8,128)(2,1)S(1)} %collective-permute-done.11.other, bf16[3584,512]{1,0:T(8,128)(2,1)S(1)} %bitcast.15, bf16[3584,512]{1,0:T(8,128)(2,1)S(1)} %bitcast.17, ...), custom_call_target="tpu_custom_call" | custom-call | flops 20000000000 | tf_op jit(solution)/shard_map/pallas_call | solution.py:74
  26.2 0.6 %collective-permute-start.12 = (bf16[96,1792]{1,0:T(8,128)(2,1)S(1)}, bf16[96,1792]{1,0:T(8,128)(2,1)S(1)}, u32[]{:S(2)}, u32[]{:S(2)}) collective-permute-start(bf16[96,1792]{1,0:T(8,128)(2,1)S(1)} %get-tuple-element.20), channel_id=1, source_target_pairs={{0,1},{1,0},{2,3},{3,2},{4,5},{5,4},{6,7},{7,6},{8,9},{9,8},{10,11... | collective-permute-start | bytes 1032200 | tf_op jit(solution)/shard_map/ppermute | solution.py:66
  26.8 1.3 %collective-permute-done.12.recv_b = bf16[96,1792]{1,0:T(8,128)(2,1)S(1)} collective-permute-done((bf16[96,1792]{1,0:T(8,128)(2,1)S(1)}, bf16[96,1792]{1,0:T(8,128)(2,1)S(1)}, u32[]{:S(2)}, u32[]{:S(2)}) %collective-permute-start.12) | collective-permute-done | bytes 344096 | tf_op jit(solution)/shard_map/ppermute | solution.py:66
  28.0 0.0 collective-permute-done.7.recv_a.recv
  28.0 0.1 shard_map.72
  28.2 0.7 %collective-permute-start.13 = (bf16[64,1792]{1,0:T(8,128)(2,1)S(1)}, bf16[64,1792]{1,0:T(8,128)(2,1)S(1)}, u32[]{:S(2)}, u32[]{:S(2)}) collective-permute-start(bf16[64,1792]{1,0:T(8,128)(2,1)S(1)} %get-tuple-element.21), channel_id=1, source_target_pairs={{0,8},{8,0},{16,24},{24,16},{1,9},{9,1},{17,25},{25,17},{2,10},{10... | collective-permute-start | bytes 688136 | tf_op jit(solution)/shard_map/ppermute | solution.py:66
  28.9 0.9 %collective-permute-start.14 = (bf16[64,1792]{1,0:T(8,128)(2,1)S(1)}, bf16[64,1792]{1,0:T(8,128)(2,1)S(1)}, u32[]{:S(2)}, u32[]{:S(2)}) collective-permute-start(bf16[64,1792]{1,0:T(8,128)(2,1)S(1)} %get-tuple-element.22), channel_id=1, source_target_pairs={{0,16},{8,24},{16,0},{24,8},{1,17},{9,25},{17,1},{25,9},{2,18},{10... | collective-permute-start | bytes 688136 | tf_op jit(solution)/shard_map/ppermute | solution.py:66
  29.9 5.4 %collective-permute-start.18 = (bf16[16,1792]{1,0:T(8,128)(2,1)S(1)}, bf16[16,1792]{1,0:T(8,128)(2,1)S(1)}, u32[]{:S(2)}, u32[]{:S(2)}) collective-permute-start(bf16[16,1792]{1,0:T(8,128)(2,1)S(1)} %get-tuple-element.26), channel_id=1, source_target_pairs={{0,6},{2,4},{4,2},{6,0},{1,7},{3,5},{5,3},{7,1},{8,14},{10,12},{12... | collective-permute-start | bytes 172040 | tf_op jit(solution)/shard_map/ppermute | solution.py:66
  35.2 0.0 collective-permute-start.19
  35.2 0.6 %collective-permute-start.20 = (bf16[16,1792]{1,0:T(8,128)(2,1)S(1)}, bf16[16,1792]{1,0:T(8,128)(2,1)S(1)}, u32[]{:S(2)}, u32[]{:S(2)}) collective-permute-start(bf16[16,1792]{1,0:T(8,128)(2,1)S(1)} %get-tuple-element.28), channel_id=1, source_target_pairs={{0,2},{2,0},{4,6},{6,4},{1,3},{3,1},{5,7},{7,5},{8,10},{10,8},{12,... | collective-permute-start | bytes 172040 | tf_op jit(solution)/shard_map/ppermute | solution.py:66
  35.8 2.2 %collective-permute-done.18.rest_0_ = bf16[16,1792]{1,0:T(8,128)(2,1)S(1)} collective-permute-done((bf16[16,1792]{1,0:T(8,128)(2,1)S(1)}, bf16[16,1792]{1,0:T(8,128)(2,1)S(1)}, u32[]{:S(2)}, u32[]{:S(2)}) %collective-permute-start.18) | collective-permute-done | bytes 57376 | tf_op jit(solution)/shard_map/ppermute | solution.py:66
  38.0 2.3 %collective-permute-done.19.rest_1_ = bf16[16,1792]{1,0:T(8,128)(2,1)S(1)} collective-permute-done((bf16[16,1792]{1,0:T(8,128)(2,1)S(1)}, bf16[16,1792]{1,0:T(8,128)(2,1)S(1)}, u32[]{:S(2)}, u32[]{:S(2)}) %collective-permute-start.19) | collective-permute-done | bytes 57376 | tf_op jit(solution)/shard_map/ppermute | solution.py:66
  40.3 0.2 collective-permute-done.20.rest_2_
  40.5 1.5 %collective-permute-start.21 = (bf16[16,1792]{1,0:T(8,128)(2,1)S(1)}, bf16[16,1792]{1,0:T(8,128)(2,1)S(1)}, u32[]{:S(2)}, u32[]{:S(2)}) collective-permute-start(bf16[16,1792]{1,0:T(8,128)(2,1)S(1)} %shard_map.74), channel_id=1, source_target_pairs={{0,24},{8,16},{16,8},{24,0},{1,25},{9,17},{17,9},{25,1},{2,26},{10... | collective-permute-start | bytes 172040 | tf_op jit(solution)/shard_map/ppermute | solution.py:66
  42.0 0.0 collective-permute-done.13.x
  42.0 0.0 collective-permute-done.14.y
  42.0 0.1 shard_map.73
  42.1 2.4 %collective-permute-start.15 = (bf16[16,1792]{1,0:T(8,128)(2,1)S(1)}, bf16[16,1792]{1,0:T(8,128)(2,1)S(1)}, u32[]{:S(2)}, u32[]{:S(2)}) collective-permute-start(bf16[16,1792]{1,0:T(8,128)(2,1)S(1)} %get-tuple-element.23), channel_id=1, source_target_pairs={{0,6},{2,4},{4,2},{6,0},{1,7},{3,5},{5,3},{7,1},{8,14},{10,12},{12... | collective-permute-start | bytes 172040 | tf_op jit(solution)/shard_map/ppermute | solution.py:66
  44.4 0.3 collective-permute-start.16
  44.8 1.8 %collective-permute-start.17 = (bf16[16,1792]{1,0:T(8,128)(2,1)S(1)}, bf16[16,1792]{1,0:T(8,128)(2,1)S(1)}, u32[]{:S(2)}, u32[]{:S(2)}) collective-permute-start(bf16[16,1792]{1,0:T(8,128)(2,1)S(1)} %get-tuple-element.25), channel_id=1, source_target_pairs={{0,2},{2,0},{4,6},{6,4},{1,3},{3,1},{5,7},{7,5},{8,10},{10,8},{12,... | collective-permute-start | bytes 172040 | tf_op jit(solution)/shard_map/ppermute | solution.py:66
  46.5 0.0 collective-permute-done.21.rest_3_
  46.5 1.7 %collective-permute-done.15.rest_0_ = bf16[16,1792]{1,0:T(8,128)(2,1)S(1)} collective-permute-done((bf16[16,1792]{1,0:T(8,128)(2,1)S(1)}, bf16[16,1792]{1,0:T(8,128)(2,1)S(1)}, u32[]{:S(2)}, u32[]{:S(2)}) %collective-permute-start.15) | collective-permute-done | bytes 57376 | tf_op jit(solution)/shard_map/ppermute | solution.py:66
  48.2 1.7 %collective-permute-done.16.rest_1_ = bf16[16,1792]{1,0:T(8,128)(2,1)S(1)} collective-permute-done((bf16[16,1792]{1,0:T(8,128)(2,1)S(1)}, bf16[16,1792]{1,0:T(8,128)(2,1)S(1)}, u32[]{:S(2)}, u32[]{:S(2)}) %collective-permute-start.16) | collective-permute-done | bytes 57376 | tf_op jit(solution)/shard_map/ppermute | solution.py:66
  49.9 0.0 collective-permute-done.17.rest_2_
  49.9 0.7 %shard_map.75 = bf16[16,1792]{1,0:T(8,128)(2,1)} custom-call(bf16[160,1792]{1,0:T(8,128)(2,1)S(1)} %get-tuple-element.17.keep_a.keep, bf16[160,1792]{1,0:T(8,128)(2,1)S(1)} %collective-permute-done.7.recv_a.recv, bf16[64,1792]{1,0:T(8,128)(2,1)S(1)} %collective-permute-done.13.x, bf16[64,1792]{1,0:T(8,128)(2,1)S(1)} %collective-permute-done.14.y, ...), custom_call_target="tpu_custom_call" | custom-call | tf_op jit(solution)/shard_map/pallas_call | solution.py:74
  (6 shorter events, 0.1 us)
Async XLA Ops:
  0.0 0.8 %copy-start = (bf16[1,16,1792]{2,1,0:T(8,128)(2,1)S(1)}, bf16[1,16,1792]{2,1,0:T(8,128)(2,1)}, u32[]{:S(2)}) copy-start(bf16[1,16,1792]{2,1,0:T(8,128)(2,1)} %param.6) | copy-start | bytes 172036
  0.0 0.8 %copy-start.1 = (s32[1,16,8]{1,2,0:T(8,128)S(1)}, s32[1,16,8]{1,2,0:T(8,128)}, u32[]{:S(2)}) copy-start(s32[1,16,8]{1,2,0:T(8,128)} %param.10) | copy-start | bytes 1540
  0.0 0.8 %copy-start.2 = (s32[1,16,8]{1,2,0:T(8,128)S(1)}, s32[1,16,8]{1,2,0:T(8,128)}, u32[]{:S(2)}) copy-start(s32[1,16,8]{1,2,0:T(8,128)} %param.11) | copy-start | bytes 1540
  1.1 5.7 %collective-permute-start = (bf16[16,1920]{1,0:T(8,128)(2,1)S(1)}, bf16[16,1920]{1,0:T(8,128)(2,1)S(1)}, u32[]{:S(2)}, u32[]{:S(2)}) collective-permute-start(bf16[16,1920]{1,0:T(8,128)(2,1)S(1)} %shard_map.65.refs_0_), channel_id=1, source_target_pairs={{0,2},{2,0},{4,6},{6,4},{1,3},{3,1},{5,7},{7,5},{8,10},{10,8},{12,... | collective-permute-start | bytes 184328 | tf_op jit(solution)/shard_map/ppermute | solution.py:66
  4.2 6.3 %collective-permute-start.1 = (bf16[16,1920]{1,0:T(8,128)(2,1)S(1)}, bf16[16,1920]{1,0:T(8,128)(2,1)S(1)}, u32[]{:S(2)}, u32[]{:S(2)}) collective-permute-start(bf16[16,1920]{1,0:T(8,128)(2,1)S(1)} %shard_map.65.refs_0_), channel_id=1, source_target_pairs={{0,4},{2,6},{4,0},{6,2},{1,5},{3,7},{5,1},{7,3},{8,12},{10,14},{12... | collective-permute-start | bytes 184328 | tf_op jit(solution)/shard_map/ppermute | solution.py:66
  6.8 6.0 %collective-permute-start.2 = (bf16[16,1920]{1,0:T(8,128)(2,1)S(1)}, bf16[16,1920]{1,0:T(8,128)(2,1)S(1)}, u32[]{:S(2)}, u32[]{:S(2)}) collective-permute-start(bf16[16,1920]{1,0:T(8,128)(2,1)S(1)} %shard_map.65.refs_0_), channel_id=1, source_target_pairs={{0,6},{2,4},{4,2},{6,0},{1,7},{3,5},{5,3},{7,1},{8,14},{10,12},{12... | collective-permute-start | bytes 184328 | tf_op jit(solution)/shard_map/ppermute | solution.py:66
  6.8 9.1 %collective-permute-start.3 = (bf16[32,1920]{1,0:T(8,128)(2,1)S(1)}, bf16[32,1920]{1,0:T(8,128)(2,1)S(1)}, u32[]{:S(2)}, u32[]{:S(2)}) collective-permute-start(bf16[32,1920]{1,0:T(8,128)(2,1)S(1)} %shard_map.66.refs_0_), channel_id=1, source_target_pairs={{0,8},{8,0},{16,24},{24,16},{1,9},{9,1},{17,25},{25,17},{2,10},{10... | collective-permute-start | bytes 368648 | tf_op jit(solution)/shard_map/ppermute | solution.py:66
  8.6 9.2 %collective-permute-start.4 = (bf16[32,1920]{1,0:T(8,128)(2,1)S(1)}, bf16[32,1920]{1,0:T(8,128)(2,1)S(1)}, u32[]{:S(2)}, u32[]{:S(2)}) collective-permute-start(bf16[32,1920]{1,0:T(8,128)(2,1)S(1)} %shard_map.66.refs_0_), channel_id=1, source_target_pairs={{0,16},{8,24},{16,0},{24,8},{1,17},{9,25},{17,1},{25,9},{2,18},{10... | collective-permute-start | bytes 368648 | tf_op jit(solution)/shard_map/ppermute | solution.py:66
  10.1 7.7 %collective-permute-start.5 = (bf16[32,1920]{1,0:T(8,128)(2,1)S(1)}, bf16[32,1920]{1,0:T(8,128)(2,1)S(1)}, u32[]{:S(2)}, u32[]{:S(2)}) collective-permute-start(bf16[32,1920]{1,0:T(8,128)(2,1)S(1)} %shard_map.66.refs_0_), channel_id=1, source_target_pairs={{0,24},{8,16},{16,8},{24,0},{1,25},{9,17},{17,9},{25,1},{2,26},{10... | collective-permute-start | bytes 368648 | tf_op jit(solution)/shard_map/ppermute | solution.py:66
  12.8 7.0 %collective-permute-start.10 = (bf16[32,1920]{1,0:T(8,128)(2,1)S(1)}, bf16[32,1920]{1,0:T(8,128)(2,1)S(1)}, u32[]{:S(2)}, u32[]{:S(2)}) collective-permute-start(bf16[32,1920]{1,0:T(8,128)(2,1)S(1)} %shard_map.67.refs_1_), channel_id=1, source_target_pairs={{0,24},{8,16},{16,8},{24,0},{1,25},{9,17},{17,9},{25,1},{2,26},{10... | collective-permute-start | bytes 368648 | tf_op jit(solution)/shard_map/ppermute | solution.py:66
  15.3 4.9 %collective-permute-start.8 = (bf16[32,1920]{1,0:T(8,128)(2,1)S(1)}, bf16[32,1920]{1,0:T(8,128)(2,1)S(1)}, u32[]{:S(2)}, u32[]{:S(2)}) collective-permute-start(bf16[32,1920]{1,0:T(8,128)(2,1)S(1)} %shard_map.67.refs_1_), channel_id=1, source_target_pairs={{0,8},{8,0},{16,24},{24,16},{1,9},{9,1},{17,25},{25,17},{2,10},{10... | collective-permute-start | bytes 368648 | tf_op jit(solution)/shard_map/ppermute | solution.py:66
  15.9 5.5 %collective-permute-start.9 = (bf16[32,1920]{1,0:T(8,128)(2,1)S(1)}, bf16[32,1920]{1,0:T(8,128)(2,1)S(1)}, u32[]{:S(2)}, u32[]{:S(2)}) collective-permute-start(bf16[32,1920]{1,0:T(8,128)(2,1)S(1)} %shard_map.67.refs_1_), channel_id=1, source_target_pairs={{0,16},{8,24},{16,0},{24,8},{1,17},{9,25},{17,1},{25,9},{2,18},{10... | collective-permute-start | bytes 368648 | tf_op jit(solution)/shard_map/ppermute | solution.py:66
  17.8 3.6 %copy-start.3 = (bf16[1,3584,512]{2,1,0:T(8,128)(2,1)S(1)}, bf16[1,3584,512]{2,1,0:T(8,128)(2,1)}, u32[]{:S(2)}) copy-start(bf16[1,3584,512]{2,1,0:T(8,128)(2,1)} %param.7) | copy-start | bytes 11010052
  17.9 3.6 %copy-start.4 = (bf16[1,3584,512]{2,1,0:T(8,128)(2,1)S(1)}, bf16[1,3584,512]{2,1,0:T(8,128)(2,1)}, u32[]{:S(2)}) copy-start(bf16[1,3584,512]{2,1,0:T(8,128)(2,1)} %param.8) | copy-start | bytes 11010052
  17.9 4.2 %copy-start.5 = (bf16[1,512,3584]{2,1,0:T(8,128)(2,1)S(1)}, bf16[1,512,3584]{2,1,0:T(8,128)(2,1)}, u32[]{:S(2)}) copy-start(bf16[1,512,3584]{2,1,0:T(8,128)(2,1)} %param.9) | copy-start | bytes 11010052
  17.9 3.6 %collective-permute-start.6 = (bf16[160,1920]{1,0:T(8,128)(2,1)S(1)}, bf16[160,1920]{1,0:T(8,128)(2,1)S(1)}, u32[]{:S(2)}, u32[]{:S(2)}) collective-permute-start(bf16[160,1920]{1,0:T(8,128)(2,1)S(1)} %shard_map.68.own), channel_id=1, source_target_pairs={{0,1},{1,0},{2,3},{3,2},{4,5},{5,4},{6,7},{7,6},{8,9},{9,8},{10,11... | collective-permute-start | bytes 1843208 | tf_op jit(solution)/shard_map/ppermute | solution.py:66
  21.4 2.9 %collective-permute-start.11 = (bf16[96,1920]{1,0:T(8,128)(2,1)S(1)}, bf16[96,1920]{1,0:T(8,128)(2,1)S(1)}, u32[]{:S(2)}, u32[]{:S(2)}) collective-permute-start(bf16[96,1920]{1,0:T(8,128)(2,1)S(1)} %shard_map.70.own), channel_id=1, source_target_pairs={{0,1},{1,0},{2,3},{3,2},{4,5},{5,4},{6,7},{7,6},{8,9},{9,8},{10,11... | collective-permute-start | bytes 1105928 | tf_op jit(solution)/shard_map/ppermute | solution.py:66
  24.2 3.9 %collective-permute-start.7 = (bf16[160,1792]{1,0:T(8,128)(2,1)S(1)}, bf16[160,1792]{1,0:T(8,128)(2,1)S(1)}, u32[]{:S(2)}, u32[]{:S(2)}) collective-permute-start(bf16[160,1792]{1,0:T(8,128)(2,1)S(1)} %get-tuple-element.18), channel_id=1, source_target_pairs={{0,1},{1,0},{2,3},{3,2},{4,5},{5,4},{6,7},{7,6},{8,9},{9,8},{10,11... | collective-permute-start | bytes 1720328 | tf_op jit(solution)/shard_map/ppermute | solution.py:66
  26.2 1.8 %collective-permute-start.12 = (bf16[96,1792]{1,0:T(8,128)(2,1)S(1)}, bf16[96,1792]{1,0:T(8,128)(2,1)S(1)}, u32[]{:S(2)}, u32[]{:S(2)}) collective-permute-start(bf16[96,1792]{1,0:T(8,128)(2,1)S(1)} %get-tuple-element.20), channel_id=1, source_target_pairs={{0,1},{1,0},{2,3},{3,2},{4,5},{5,4},{6,7},{7,6},{8,9},{9,8},{10,11... | collective-permute-start | bytes 1032200 | tf_op jit(solution)/shard_map/ppermute | solution.py:66
  28.2 13.8 %collective-permute-start.13 = (bf16[64,1792]{1,0:T(8,128)(2,1)S(1)}, bf16[64,1792]{1,0:T(8,128)(2,1)S(1)}, u32[]{:S(2)}, u32[]{:S(2)}) collective-permute-start(bf16[64,1792]{1,0:T(8,128)(2,1)S(1)} %get-tuple-element.21), channel_id=1, source_target_pairs={{0,8},{8,0},{16,24},{24,16},{1,9},{9,1},{17,25},{25,17},{2,10},{10... | collective-permute-start | bytes 688136 | tf_op jit(solution)/shard_map/ppermute | solution.py:66
  28.9 13.0 %collective-permute-start.14 = (bf16[64,1792]{1,0:T(8,128)(2,1)S(1)}, bf16[64,1792]{1,0:T(8,128)(2,1)S(1)}, u32[]{:S(2)}, u32[]{:S(2)}) collective-permute-start(bf16[64,1792]{1,0:T(8,128)(2,1)S(1)} %get-tuple-element.22), channel_id=1, source_target_pairs={{0,16},{8,24},{16,0},{24,8},{1,17},{9,25},{17,1},{25,9},{2,18},{10... | collective-permute-start | bytes 688136 | tf_op jit(solution)/shard_map/ppermute | solution.py:66
  29.9 8.1 %collective-permute-start.18 = (bf16[16,1792]{1,0:T(8,128)(2,1)S(1)}, bf16[16,1792]{1,0:T(8,128)(2,1)S(1)}, u32[]{:S(2)}, u32[]{:S(2)}) collective-permute-start(bf16[16,1792]{1,0:T(8,128)(2,1)S(1)} %get-tuple-element.26), channel_id=1, source_target_pairs={{0,6},{2,4},{4,2},{6,0},{1,7},{3,5},{5,3},{7,1},{8,14},{10,12},{12... | collective-permute-start | bytes 172040 | tf_op jit(solution)/shard_map/ppermute | solution.py:66
  35.2 5.1 %collective-permute-start.19 = (bf16[16,1792]{1,0:T(8,128)(2,1)S(1)}, bf16[16,1792]{1,0:T(8,128)(2,1)S(1)}, u32[]{:S(2)}, u32[]{:S(2)}) collective-permute-start(bf16[16,1792]{1,0:T(8,128)(2,1)S(1)} %get-tuple-element.27), channel_id=1, source_target_pairs={{0,4},{2,6},{4,0},{6,2},{1,5},{3,7},{5,1},{7,3},{8,12},{10,14},{12... | collective-permute-start | bytes 172040 | tf_op jit(solution)/shard_map/ppermute | solution.py:66
  35.2 5.2 %collective-permute-start.20 = (bf16[16,1792]{1,0:T(8,128)(2,1)S(1)}, bf16[16,1792]{1,0:T(8,128)(2,1)S(1)}, u32[]{:S(2)}, u32[]{:S(2)}) collective-permute-start(bf16[16,1792]{1,0:T(8,128)(2,1)S(1)} %get-tuple-element.28), channel_id=1, source_target_pairs={{0,2},{2,0},{4,6},{6,4},{1,3},{3,1},{5,7},{7,5},{8,10},{10,8},{12,... | collective-permute-start | bytes 172040 | tf_op jit(solution)/shard_map/ppermute | solution.py:66
  40.5 6.0 %collective-permute-start.21 = (bf16[16,1792]{1,0:T(8,128)(2,1)S(1)}, bf16[16,1792]{1,0:T(8,128)(2,1)S(1)}, u32[]{:S(2)}, u32[]{:S(2)}) collective-permute-start(bf16[16,1792]{1,0:T(8,128)(2,1)S(1)} %shard_map.74), channel_id=1, source_target_pairs={{0,24},{8,16},{16,8},{24,0},{1,25},{9,17},{17,9},{25,1},{2,26},{10... | collective-permute-start | bytes 172040 | tf_op jit(solution)/shard_map/ppermute | solution.py:66
  42.1 6.2 %collective-permute-start.15 = (bf16[16,1792]{1,0:T(8,128)(2,1)S(1)}, bf16[16,1792]{1,0:T(8,128)(2,1)S(1)}, u32[]{:S(2)}, u32[]{:S(2)}) collective-permute-start(bf16[16,1792]{1,0:T(8,128)(2,1)S(1)} %get-tuple-element.23), channel_id=1, source_target_pairs={{0,6},{2,4},{4,2},{6,0},{1,7},{3,5},{5,3},{7,1},{8,14},{10,12},{12... | collective-permute-start | bytes 172040 | tf_op jit(solution)/shard_map/ppermute | solution.py:66
  44.4 5.5 %collective-permute-start.16 = (bf16[16,1792]{1,0:T(8,128)(2,1)S(1)}, bf16[16,1792]{1,0:T(8,128)(2,1)S(1)}, u32[]{:S(2)}, u32[]{:S(2)}) collective-permute-start(bf16[16,1792]{1,0:T(8,128)(2,1)S(1)} %get-tuple-element.24), channel_id=1, source_target_pairs={{0,4},{2,6},{4,0},{6,2},{1,5},{3,7},{5,1},{7,3},{8,12},{10,14},{12... | collective-permute-start | bytes 172040 | tf_op jit(solution)/shard_map/ppermute | solution.py:66
  44.8 5.1 %collective-permute-start.17 = (bf16[16,1792]{1,0:T(8,128)(2,1)S(1)}, bf16[16,1792]{1,0:T(8,128)(2,1)S(1)}, u32[]{:S(2)}, u32[]{:S(2)}) collective-permute-start(bf16[16,1792]{1,0:T(8,128)(2,1)S(1)} %get-tuple-element.25), channel_id=1, source_target_pairs={{0,2},{2,0},{4,6},{6,4},{1,3},{3,1},{5,7},{7,5},{8,10},{10,8},{12,... | collective-permute-start | bytes 172040 | tf_op jit(solution)/shard_map/ppermute | solution.py:66

commit v3 on v2

--- a/solution.py
+++ b/solution.py
@@ -12,6 +12,7 @@
 STALL = 20000000000
 EARLY = 2
 TILE = 256
+HINT = 2000000000
 
 
 def slotted(tokens, gate_weight, up_weight, down_weight, expert_ids, gate_codes, slot_depth):
@@ -126,23 +127,42 @@
     return total
 
 
-def ffn(owners, own, other, gate, up, down, keep, send, x, hidden):
-    rows, width = keep.shape
+def half_rows(width, mine):
     half = lax.axis_index("tensor")
+    start = half * width if mine else (1 - half) * width
+    return pl.ds(pl.multiple_of(start, LANES), width)
+
+
+def enter_own(owners, own, gate, up, gated, lifted, scale):
+    rows = own.shape[0]
+    width = own.shape[1] - LANES
     expert = lax.axis_index("dp") * lax.axis_size("expert") + lax.axis_index("expert")
-    mine_at = pl.ds(pl.multiple_of(half * width, LANES), width)
-    other_at = pl.ds(pl.multiple_of((1 - half) * width, LANES), width)
-    x[:, mine_at] = own[:, :width]
-    x[:, other_at] = other[:, :width]
     lane = lax.broadcasted_iota(jnp.int32, (rows, LANES), 1)
     mine = (lane == expert) | (lane == expert + owners)
-    scale = jnp.sum(jnp.where(mine, own[:, width:].astype(F32), 0.0), axis=1, keepdims=True)
+    share = jnp.sum(jnp.where(mine, own[:, width:].astype(F32), 0.0), axis=1, keepdims=True)
+    scale[...] = jnp.broadcast_to(share, (rows, LANES))
+    at = half_rows(width, True)
+    for weight, out in ((gate, gated), (up, lifted)):
+        out[...] = dot(own[:, :width], weight[at, :])
+
+
+def leave(at, scale, hidden, down, out):
+    out[...] = (dot(hidden[...], down[:, at]) * scale[:, :1]).astype(BF16)
+
+
+def enter_other(other, gate, up, down, gated, lifted, scale, hidden, send):
+    width = send.shape[1]
+    at = half_rows(width, False)
     for i in range(0, hidden.shape[1], TILE):
-        at = pl.ds(i, TILE)
-        gated, lifted = dot(x[...], gate[:, at]), dot(x[...], up[:, at])
-        hidden[:, at] = (jax.nn.silu(gated) * lifted).astype(BF16)
-    for at, out in ((other_at, send), (mine_at, keep)):
-        out[...] = (dot(hidden[...], down[:, at]) * scale).astype(BF16)
+        there = pl.ds(i, TILE)
+        g = gated[:, there] + dot(other[:, :width], gate[at, there])
+        u = lifted[:, there] + dot(other[:, :width], up[at, there])
+        hidden[:, there] = (jax.nn.silu(g) * u).astype(BF16)
+    leave(at, scale, hidden, down, send)
+
+
+def leave_own(hidden, down, scale, keep):
+    leave(half_rows(keep.shape[1], True), scale, hidden, down, keep)
 
 
 def dense(tokens, gate_weight, up_weight, down_weight, expert_ids, gate_codes):
@@ -170,18 +190,23 @@
     sent_a = {g: swap(parts_a, "dp", g) for g in range(1, dp)}
     sent_b = {g: swap(parts_b, "dp", g) for g in range(1, dp)}
     near = stack([parts_a, parts_b] + [sent_a[g] for g in range(1, dp)])
-    far = stack([sent_b[g] for g in range(1, dp)], flops=STALL)
-    matrices = gate_weight[0], up_weight[0], down_weight[0]
+    far = stack([sent_b[g] for g in range(1, dp)])
+    gate, up, down = gate_weight[0], up_weight[0], down_weight[0]
 
     def run(own):
         count = own.shape[0]
-        return call(
-            functools.partial(ffn, owners),
-            [block(count)] * 2,
-            own, swap(own, "tensor", 1), *matrices,
-            flops=STALL, limit=16,
-            scratch=[pltpu.VMEM((count, 2 * width), BF16), pltpu.VMEM((count, units), BF16)],
+        floats = jax.ShapeDtypeStruct((count, units), F32)
+        other = swap(own, "tensor", 1)
+        gated, lifted, scale = call(
+            functools.partial(enter_own, owners), [floats, floats, jax.ShapeDtypeStruct((count, LANES), F32)],
+            own, gate, up, flops=HINT, limit=8,
         )
+        hidden, send = call(
+            enter_other, [jax.ShapeDtypeStruct((count, units), BF16), block(count)],
+            other, gate, up, down, gated, lifted, scale, flops=HINT, limit=8,
+        )
+        keep = call(leave_own, block(count), hidden, down, scale, flops=HINT, limit=8)
+        return keep, send
 
     keep_a, send_a = run(near)
     keep_b, send_b = run(far)

time: 50.7 us -> 54 us (1.065)
  waiting for transfers between devices: 16.6 us -> 19.4 us
  starting transfers between devices: 27.1 us -> 26.1 us
  Pallas kernels: 5.35 us -> 6.07 us
  local copies, waits for them, and re-layouts: 1.41 us -> 2.08 us
    ppermute x22, waiting for transfers between devices: 16.6 us -> 19.4 us  [swap(): return lax.ppermute(x, axis, [(i, i ^ offset) for i in range(count)])]
    ppermute x22, starting transfers between devices: 27.1 us -> 26.1 us  [swap(): return lax.ppermute(x, axis, [(i, i ^ offset) for i in range(count)])]
    pallas_call x12 -> x16, Pallas kernels: 5.35 us -> 6.07 us  [call(): pl.pallas_call(body, out_shape=outs, in_specs=[VMEM] * len(args), out_spe...]
    unnamed x12, local copies, waits for them, and re-layouts: 1.41 us -> 2.08 us
  transfers between devices with their start and end apart: 22 -> 22, of which waited for: 12 -> 11; matrix products, arithmetic and copies ran while one was open for 0% -> 0% of each run, Pallas kernels for 8% -> 9%
where the time goes in v3:
time: 54 us; the launch traced here: 53.8 us
  starting transfers between devices  26.1 us (48%)
  waiting for transfers between devices  19.4 us (36%)
  Pallas kernels  6.07 us (11%)
  local copies, waits for them, and re-layouts  2.08 us (4%)
    ppermute x22, starting transfers between devices, swap(): return lax.ppermute(x, axis, [(i, i ^ offset) for i in range(count)])  26.1 us
    ppermute x22, waiting for transfers between devices, swap(): return lax.ppermute(x, axis, [(i, i ^ offset) for i in range(count)])  19.4 us
    pallas_call x16, Pallas kernels, call(): pl.pallas_call(body, out_shape=outs, in_specs=[VMEM] * len(args), out_spe...  6.07 us
    unnamed x12, local copies, waits for them, and re-layouts  2.08 us
  transfers between devices with their start and end apart: 22, of which 11 were waited for; matrix products, arithmetic and copies ran while one was open for 0% of the time, Pallas kernels for 9%

profile of v3, /device:TPU:0, one launch (start us, length us, event | category | flops | bytes accessed | tf_op | source)
XLA Modules:
  0.0 53.8 jit_solution(16317795992871533476)
XLA Ops:
  0.0 0.0 copy-start.3
  0.0 0.8 %copy-done.3 = bf16[1,16,1792]{2,1,0:T(8,128)(2,1)S(1)} copy-done((bf16[1,16,1792]{2,1,0:T(8,128)(2,1)S(1)}, bf16[1,16,1792]{2,1,0:T(8,128)(2,1)}, u32[]{:S(2)}) %copy-start.3) | copy-done | bytes 57368
  0.8 0.0 copy-done.4
  0.8 0.0 copy-done.5
  0.8 0.3 shard_map.65.refs_0_
  1.1 3.1 %collective-permute-start = (bf16[16,1920]{1,0:T(8,128)(2,1)S(1)}, bf16[16,1920]{1,0:T(8,128)(2,1)S(1)}, u32[]{:S(2)}, u32[]{:S(2)}) collective-permute-start(bf16[16,1920]{1,0:T(8,128)(2,1)S(1)} %shard_map.65.refs_0_), channel_id=1, source_target_pairs={{0,2},{2,0},{4,6},{6,4},{1,3},{3,1},{5,7},{7,5},{8,10},{10,8},{12,... | collective-permute-start | bytes 184328 | tf_op jit(solution)/shard_map/ppermute | solution.py:67
  4.2 2.6 %collective-permute-start.1 = (bf16[16,1920]{1,0:T(8,128)(2,1)S(1)}, bf16[16,1920]{1,0:T(8,128)(2,1)S(1)}, u32[]{:S(2)}, u32[]{:S(2)}) collective-permute-start(bf16[16,1920]{1,0:T(8,128)(2,1)S(1)} %shard_map.65.refs_0_), channel_id=1, source_target_pairs={{0,4},{2,6},{4,0},{6,2},{1,5},{3,7},{5,1},{7,3},{8,12},{10,14},{12... | collective-permute-start | bytes 184328 | tf_op jit(solution)/shard_map/ppermute | solution.py:67
  6.8 0.0 collective-permute-start.2
  6.8 0.0 collective-permute-done.refs_1_
  6.8 0.0 copy-start
  6.8 0.0 copy-start.1
  6.8 1.8 %collective-permute-start.3 = (bf16[32,1920]{1,0:T(8,128)(2,1)S(1)}, bf16[32,1920]{1,0:T(8,128)(2,1)S(1)}, u32[]{:S(2)}, u32[]{:S(2)}) collective-permute-start(bf16[32,1920]{1,0:T(8,128)(2,1)S(1)} %shard_map.66.refs_0_), channel_id=1, source_target_pairs={{0,8},{8,0},{16,24},{24,16},{1,9},{9,1},{17,25},{25,17},{2,10},{10... | collective-permute-start | bytes 368648 | tf_op jit(solution)/shard_map/ppermute | solution.py:67
  8.6 1.5 %collective-permute-start.4 = (bf16[32,1920]{1,0:T(8,128)(2,1)S(1)}, bf16[32,1920]{1,0:T(8,128)(2,1)S(1)}, u32[]{:S(2)}, u32[]{:S(2)}) collective-permute-start(bf16[32,1920]{1,0:T(8,128)(2,1)S(1)} %shard_map.66.refs_0_), channel_id=1, source_target_pairs={{0,16},{8,24},{16,0},{24,8},{1,17},{9,25},{17,1},{25,9},{2,18},{10... | collective-permute-start | bytes 368648 | tf_op jit(solution)/shard_map/ppermute | solution.py:67
  10.1 0.3 collective-permute-start.5
  10.4 0.2 collective-permute-done.1.refs_0_
  10.6 2.3 %collective-permute-done.2.refs_1_ = bf16[16,1920]{1,0:T(8,128)(2,1)S(1)} collective-permute-done((bf16[16,1920]{1,0:T(8,128)(2,1)S(1)}, bf16[16,1920]{1,0:T(8,128)(2,1)S(1)}, u32[]{:S(2)}, u32[]{:S(2)}) %collective-permute-start.2) | collective-permute-done | bytes 61472 | tf_op jit(solution)/shard_map/ppermute | solution.py:67
  12.8 0.0 collective-permute-done.3.refs_2_
  12.8 3.3 %collective-permute-done.4.refs_3_ = bf16[32,1920]{1,0:T(8,128)(2,1)S(1)} collective-permute-done((bf16[32,1920]{1,0:T(8,128)(2,1)S(1)}, bf16[32,1920]{1,0:T(8,128)(2,1)S(1)}, u32[]{:S(2)}, u32[]{:S(2)}) %collective-permute-start.4) | collective-permute-done | bytes 122912 | tf_op jit(solution)/shard_map/ppermute | solution.py:67
  16.1 0.0 collective-permute-done.5.refs_4_
  16.1 0.1 collective-permute-start.6
  16.2 0.6 %collective-permute-start.8 = (bf16[32,1920]{1,0:T(8,128)(2,1)S(1)}, bf16[32,1920]{1,0:T(8,128)(2,1)S(1)}, u32[]{:S(2)}, u32[]{:S(2)}) collective-permute-start(bf16[32,1920]{1,0:T(8,128)(2,1)S(1)} %shard_map.67.refs_1_), channel_id=1, source_target_pairs={{0,8},{8,0},{16,24},{24,16},{1,9},{9,1},{17,25},{25,17},{2,10},{10... | collective-permute-start | bytes 368648 | tf_op jit(solution)/shard_map/ppermute | solution.py:67
  16.8 0.8 %collective-permute-start.9 = (bf16[32,1920]{1,0:T(8,128)(2,1)S(1)}, bf16[32,1920]{1,0:T(8,128)(2,1)S(1)}, u32[]{:S(2)}, u32[]{:S(2)}) collective-permute-start(bf16[32,1920]{1,0:T(8,128)(2,1)S(1)} %shard_map.67.refs_1_), channel_id=1, source_target_pairs={{0,16},{8,24},{16,0},{24,8},{1,17},{9,25},{17,1},{25,9},{2,18},{10... | collective-permute-start | bytes 368648 | tf_op jit(solution)/shard_map/ppermute | solution.py:67
  17.6 2.2 %collective-permute-start.10 = (bf16[32,1920]{1,0:T(8,128)(2,1)S(1)}, bf16[32,1920]{1,0:T(8,128)(2,1)S(1)}, u32[]{:S(2)}, u32[]{:S(2)}) collective-permute-start(bf16[32,1920]{1,0:T(8,128)(2,1)S(1)} %shard_map.67.refs_1_), channel_id=1, source_target_pairs={{0,24},{8,16},{16,8},{24,0},{1,25},{9,17},{17,9},{25,1},{2,26},{10... | collective-permute-start | bytes 368648 | tf_op jit(solution)/shard_map/ppermute | solution.py:67
  19.8 2.7 %collective-permute-done.8.refs_0_ = bf16[32,1920]{1,0:T(8,128)(2,1)S(1)} collective-permute-done((bf16[32,1920]{1,0:T(8,128)(2,1)S(1)}, bf16[32,1920]{1,0:T(8,128)(2,1)S(1)}, u32[]{:S(2)}, u32[]{:S(2)}) %collective-permute-start.8) | collective-permute-done | bytes 122912 | tf_op jit(solution)/shard_map/ppermute | solution.py:67
  22.5 0.0 collective-permute-done.9.refs_1_
  22.5 2.5 %collective-permute-done.10.refs_2_ = bf16[32,1920]{1,0:T(8,128)(2,1)S(1)} collective-permute-done((bf16[32,1920]{1,0:T(8,128)(2,1)S(1)}, bf16[32,1920]{1,0:T(8,128)(2,1)S(1)}, u32[]{:S(2)}, u32[]{:S(2)}) %collective-permute-start.10) | collective-permute-done | bytes 122912 | tf_op jit(solution)/shard_map/ppermute | solution.py:67
  25.1 0.1 collective-permute-start.11
  25.1 0.0 copy-done
  25.2 0.0 copy-done.1
  25.2 0.0 copy-start.2
  25.2 0.8 %shard_map.69 = (f32[160,512]{1,0:T(8,128)S(1)}, f32[160,512]{1,0:T(8,128)S(1)}, f32[160,128]{1,0:T(8,128)S(1)}) custom-call(bf16[160,1920]{1,0:T(8,128)(2,1)S(1)} %shard_map.68.own, bf16[3584,512]{1,0:T(8,128)(2,1)S(1)} %bitcast.11, bf16[3584,512]{1,0:T(8,128)(2,1)S(1)} %bitcast.15), custom_call_target="tpu_custom_call" | custom-call | flops 2000000000 | tf_op jit(solution)/shard_map/pallas_call | solution.py:75
  26.0 0.0 collective-permute-done.6.other
  26.0 1.2 %copy-done.2 = bf16[1,512,3584]{2,1,0:T(8,128)(2,1)S(1)} copy-done((bf16[1,512,3584]{2,1,0:T(8,128)(2,1)S(1)}, bf16[1,512,3584]{2,1,0:T(8,128)(2,1)}, u32[]{:S(2)}) %copy-start.2) | copy-done | bytes 3670040
  27.2 1.2 %shard_map.70 = (bf16[160,512]{1,0:T(8,128)(2,1)S(1)}, bf16[160,1792]{1,0:T(8,128)(2,1)S(1)}) custom-call(bf16[160,1920]{1,0:T(8,128)(2,1)S(1)} %collective-permute-done.6.other, bf16[3584,512]{1,0:T(8,128)(2,1)S(1)} %bitcast.12, bf16[3584,512]{1,0:T(8,128)(2,1)S(1)} %bitcast.16, bf16[512,3584]{1,0:T(8,128)(2,1)S(1)} %bitcast.19, ...), custom_call_target="tpu_custom_call" | custom-call | flops 2000000000 | tf_op jit(solution)/shard_map/pallas_call | solution.py:75
  28.4 0.5 collective-permute-start.7
  29.0 0.7 %shard_map.73 = (f32[96,512]{1,0:T(8,128)S(1)}, f32[96,512]{1,0:T(8,128)S(1)}, f32[96,128]{1,0:T(8,128)S(1)}) custom-call(bf16[96,1920]{1,0:T(8,128)(2,1)S(1)} %shard_map.72.own, bf16[3584,512]{1,0:T(8,128)(2,1)S(1)} %bitcast.13, bf16[3584,512]{1,0:T(8,128)(2,1)S(1)} %bitcast.17), custom_call_target="tpu_custom_call" | custom-call | flops 2000000000 | tf_op jit(solution)/shard_map/pallas_call | solution.py:75
  29.7 0.0 collective-permute-done.11.other
  29.7 1.1 %shard_map.74 = (bf16[96,512]{1,0:T(8,128)(2,1)S(1)}, bf16[96,1792]{1,0:T(8,128)(2,1)S(1)}) custom-call(bf16[96,1920]{1,0:T(8,128)(2,1)S(1)} %collective-permute-done.11.other, bf16[3584,512]{1,0:T(8,128)(2,1)S(1)} %bitcast.14, bf16[3584,512]{1,0:T(8,128)(2,1)S(1)} %bitcast.18, bf16[512,3584]{1,0:T(8,128)(2,1)S(1)} %bitcast.20, ...), custom_call_target="tpu_custom_call" | custom-call | flops 2000000000 | tf_op jit(solution)/shard_map/pallas_call | solution.py:75
  30.8 0.1 collective-permute-start.12
  30.9 0.4 shard_map.75.keep_b
  31.4 0.5 shard_map.71.keep_a.keep
  31.9 0.7 %collective-permute-done.12.recv_b = bf16[96,1792]{1,0:T(8,128)(2,1)S(1)} collective-permute-done((bf16[96,1792]{1,0:T(8,128)(2,1)S(1)}, bf16[96,1792]{1,0:T(8,128)(2,1)S(1)}, u32[]{:S(2)}, u32[]{:S(2)}) %collective-permute-start.12) | collective-permute-done | bytes 344096 | tf_op jit(solution)/shard_map/ppermute | solution.py:67
  32.6 0.0 collective-permute-done.7.recv_a.recv
  32.6 0.1 shard_map.76
  32.7 1.4 %collective-permute-start.13 = (bf16[64,1792]{1,0:T(8,128)(2,1)S(1)}, bf16[64,1792]{1,0:T(8,128)(2,1)S(1)}, u32[]{:S(2)}, u32[]{:S(2)}) collective-permute-start(bf16[64,1792]{1,0:T(8,128)(2,1)S(1)} %get-tuple-element.33), channel_id=1, source_target_pairs={{0,8},{8,0},{16,24},{24,16},{1,9},{9,1},{17,25},{25,17},{2,10},{10... | collective-permute-start | bytes 688136 | tf_op jit(solution)/shard_map/ppermute | solution.py:67
  34.1 1.0 %collective-permute-start.14 = (bf16[64,1792]{1,0:T(8,128)(2,1)S(1)}, bf16[64,1792]{1,0:T(8,128)(2,1)S(1)}, u32[]{:S(2)}, u32[]{:S(2)}) collective-permute-start(bf16[64,1792]{1,0:T(8,128)(2,1)S(1)} %get-tuple-element.34), channel_id=1, source_target_pairs={{0,16},{8,24},{16,0},{24,8},{1,17},{9,25},{17,1},{25,9},{2,18},{10... | collective-permute-start | bytes 688136 | tf_op jit(solution)/shard_map/ppermute | solution.py:67
  35.1 3.8 %collective-permute-start.18 = (bf16[16,1792]{1,0:T(8,128)(2,1)S(1)}, bf16[16,1792]{1,0:T(8,128)(2,1)S(1)}, u32[]{:S(2)}, u32[]{:S(2)}) collective-permute-start(bf16[16,1792]{1,0:T(8,128)(2,1)S(1)} %get-tuple-element.38), channel_id=1, source_target_pairs={{0,6},{2,4},{4,2},{6,0},{1,7},{3,5},{5,3},{7,1},{8,14},{10,12},{12... | collective-permute-start | bytes 172040 | tf_op jit(solution)/shard_map/ppermute | solution.py:67
  38.9 0.0 collective-permute-start.19
  38.9 0.6 %collective-permute-start.20 = (bf16[16,1792]{1,0:T(8,128)(2,1)S(1)}, bf16[16,1792]{1,0:T(8,128)(2,1)S(1)}, u32[]{:S(2)}, u32[]{:S(2)}) collective-permute-start(bf16[16,1792]{1,0:T(8,128)(2,1)S(1)} %get-tuple-element.40), channel_id=1, source_target_pairs={{0,2},{2,0},{4,6},{6,4},{1,3},{3,1},{5,7},{7,5},{8,10},{10,8},{12,... | collective-permute-start | bytes 172040 | tf_op jit(solution)/shard_map/ppermute | solution.py:67
  39.5 2.0 %collective-permute-done.18.rest_0_ = bf16[16,1792]{1,0:T(8,128)(2,1)S(1)} collective-permute-done((bf16[16,1792]{1,0:T(8,128)(2,1)S(1)}, bf16[16,1792]{1,0:T(8,128)(2,1)S(1)}, u32[]{:S(2)}, u32[]{:S(2)}) %collective-permute-start.18) | collective-permute-done | bytes 57376 | tf_op jit(solution)/shard_map/ppermute | solution.py:67
  41.5 2.5 %collective-permute-done.19.rest_1_ = bf16[16,1792]{1,0:T(8,128)(2,1)S(1)} collective-permute-done((bf16[16,1792]{1,0:T(8,128)(2,1)S(1)}, bf16[16,1792]{1,0:T(8,128)(2,1)S(1)}, u32[]{:S(2)}, u32[]{:S(2)}) %collective-permute-start.19) | collective-permute-done | bytes 57376 | tf_op jit(solution)/shard_map/ppermute | solution.py:67
  44.0 0.2 collective-permute-done.20.rest_2_
  44.2 1.2 %collective-permute-start.21 = (bf16[16,1792]{1,0:T(8,128)(2,1)S(1)}, bf16[16,1792]{1,0:T(8,128)(2,1)S(1)}, u32[]{:S(2)}, u32[]{:S(2)}) collective-permute-start(bf16[16,1792]{1,0:T(8,128)(2,1)S(1)} %shard_map.78), channel_id=1, source_target_pairs={{0,24},{8,16},{16,8},{24,0},{1,25},{9,17},{17,9},{25,1},{2,26},{10... | collective-permute-start | bytes 172040 | tf_op jit(solution)/shard_map/ppermute | solution.py:67
  45.5 0.0 collective-permute-done.13.x
  45.5 0.0 collective-permute-done.14.y
  45.5 0.1 shard_map.77
  45.6 2.0 %collective-permute-start.15 = (bf16[16,1792]{1,0:T(8,128)(2,1)S(1)}, bf16[16,1792]{1,0:T(8,128)(2,1)S(1)}, u32[]{:S(2)}, u32[]{:S(2)}) collective-permute-start(bf16[16,1792]{1,0:T(8,128)(2,1)S(1)} %get-tuple-element.35), channel_id=1, source_target_pairs={{0,6},{2,4},{4,2},{6,0},{1,7},{3,5},{5,3},{7,1},{8,14},{10,12},{12... | collective-permute-start | bytes 172040 | tf_op jit(solution)/shard_map/ppermute | solution.py:67
  47.6 0.1 collective-permute-start.16
  47.7 2.3 %collective-permute-start.17 = (bf16[16,1792]{1,0:T(8,128)(2,1)S(1)}, bf16[16,1792]{1,0:T(8,128)(2,1)S(1)}, u32[]{:S(2)}, u32[]{:S(2)}) collective-permute-start(bf16[16,1792]{1,0:T(8,128)(2,1)S(1)} %get-tuple-element.37), channel_id=1, source_target_pairs={{0,2},{2,0},{4,6},{6,4},{1,3},{3,1},{5,7},{7,5},{8,10},{10,8},{12,... | collective-permute-start | bytes 172040 | tf_op jit(solution)/shard_map/ppermute | solution.py:67
  50.0 0.0 collective-permute-done.21.rest_3_
  50.0 1.6 %collective-permute-done.15.rest_0_ = bf16[16,1792]{1,0:T(8,128)(2,1)S(1)} collective-permute-done((bf16[16,1792]{1,0:T(8,128)(2,1)S(1)}, bf16[16,1792]{1,0:T(8,128)(2,1)S(1)}, u32[]{:S(2)}, u32[]{:S(2)}) %collective-permute-start.15) | collective-permute-done | bytes 57376 | tf_op jit(solution)/shard_map/ppermute | solution.py:67
  51.6 1.5 %collective-permute-done.16.rest_1_ = bf16[16,1792]{1,0:T(8,128)(2,1)S(1)} collective-permute-done((bf16[16,1792]{1,0:T(8,128)(2,1)S(1)}, bf16[16,1792]{1,0:T(8,128)(2,1)S(1)}, u32[]{:S(2)}, u32[]{:S(2)}) %collective-permute-start.16) | collective-permute-done | bytes 57376 | tf_op jit(solution)/shard_map/ppermute | solution.py:67
  53.1 0.0 collective-permute-done.17.rest_2_
  53.1 0.7 %shard_map.79 = bf16[16,1792]{1,0:T(8,128)(2,1)} custom-call(bf16[160,1792]{1,0:T(8,128)(2,1)S(1)} %shard_map.71.keep_a.keep, bf16[160,1792]{1,0:T(8,128)(2,1)S(1)} %collective-permute-done.7.recv_a.recv, bf16[64,1792]{1,0:T(8,128)(2,1)S(1)} %collective-permute-done.13.x, bf16[64,1792]{1,0:T(8,128)(2,1)S(1)} %collective-permute-done.14.y, ...), custom_call_target="tpu_custom_call" | custom-call | tf_op jit(solution)/shard_map/pallas_call | solution.py:75
  (8 shorter events, 0.1 us)
Async XLA Ops:
  0.0 0.8 %copy-start.3 = (bf16[1,16,1792]{2,1,0:T(8,128)(2,1)S(1)}, bf16[1,16,1792]{2,1,0:T(8,128)(2,1)}, u32[]{:S(2)}) copy-start(bf16[1,16,1792]{2,1,0:T(8,128)(2,1)} %param.6) | copy-start | bytes 172036
  0.0 0.8 %copy-start.4 = (s32[1,16,8]{1,2,0:T(8,128)S(1)}, s32[1,16,8]{1,2,0:T(8,128)}, u32[]{:S(2)}) copy-start(s32[1,16,8]{1,2,0:T(8,128)} %param.10) | copy-start | bytes 1540
  0.0 0.8 %copy-start.5 = (s32[1,16,8]{1,2,0:T(8,128)S(1)}, s32[1,16,8]{1,2,0:T(8,128)}, u32[]{:S(2)}) copy-start(s32[1,16,8]{1,2,0:T(8,128)} %param.11) | copy-start | bytes 1540
  1.1 5.7 %collective-permute-start = (bf16[16,1920]{1,0:T(8,128)(2,1)S(1)}, bf16[16,1920]{1,0:T(8,128)(2,1)S(1)}, u32[]{:S(2)}, u32[]{:S(2)}) collective-permute-start(bf16[16,1920]{1,0:T(8,128)(2,1)S(1)} %shard_map.65.refs_0_), channel_id=1, source_target_pairs={{0,2},{2,0},{4,6},{6,4},{1,3},{3,1},{5,7},{7,5},{8,10},{10,8},{12,... | collective-permute-start | bytes 184328 | tf_op jit(solution)/shard_map/ppermute | solution.py:67
  4.2 6.3 %collective-permute-start.1 = (bf16[16,1920]{1,0:T(8,128)(2,1)S(1)}, bf16[16,1920]{1,0:T(8,128)(2,1)S(1)}, u32[]{:S(2)}, u32[]{:S(2)}) collective-permute-start(bf16[16,1920]{1,0:T(8,128)(2,1)S(1)} %shard_map.65.refs_0_), channel_id=1, source_target_pairs={{0,4},{2,6},{4,0},{6,2},{1,5},{3,7},{5,1},{7,3},{8,12},{10,14},{12... | collective-permute-start | bytes 184328 | tf_op jit(solution)/shard_map/ppermute | solution.py:67
  6.8 6.0 %collective-permute-start.2 = (bf16[16,1920]{1,0:T(8,128)(2,1)S(1)}, bf16[16,1920]{1,0:T(8,128)(2,1)S(1)}, u32[]{:S(2)}, u32[]{:S(2)}) collective-permute-start(bf16[16,1920]{1,0:T(8,128)(2,1)S(1)} %shard_map.65.refs_0_), channel_id=1, source_target_pairs={{0,6},{2,4},{4,2},{6,0},{1,7},{3,5},{5,3},{7,1},{8,14},{10,12},{12... | collective-permute-start | bytes 184328 | tf_op jit(solution)/shard_map/ppermute | solution.py:67
  6.8 18.3 %copy-start = (bf16[1,3584,512]{2,1,0:T(8,128)(2,1)S(1)}, bf16[1,3584,512]{2,1,0:T(8,128)(2,1)}, u32[]{:S(2)}) copy-start(bf16[1,3584,512]{2,1,0:T(8,128)(2,1)} %param.7) | copy-start | bytes 11010052
  6.8 18.3 %copy-start.1 = (bf16[1,3584,512]{2,1,0:T(8,128)(2,1)S(1)}, bf16[1,3584,512]{2,1,0:T(8,128)(2,1)}, u32[]{:S(2)}) copy-start(bf16[1,3584,512]{2,1,0:T(8,128)(2,1)} %param.8) | copy-start | bytes 11010052
  6.8 6.0 %collective-permute-start.3 = (bf16[32,1920]{1,0:T(8,128)(2,1)S(1)}, bf16[32,1920]{1,0:T(8,128)(2,1)S(1)}, u32[]{:S(2)}, u32[]{:S(2)}) collective-permute-start(bf16[32,1920]{1,0:T(8,128)(2,1)S(1)} %shard_map.66.refs_0_), channel_id=1, source_target_pairs={{0,8},{8,0},{16,24},{24,16},{1,9},{9,1},{17,25},{25,17},{2,10},{10... | collective-permute-start | bytes 368648 | tf_op jit(solution)/shard_map/ppermute | solution.py:67
  8.6 7.5 %collective-permute-start.4 = (bf16[32,1920]{1,0:T(8,128)(2,1)S(1)}, bf16[32,1920]{1,0:T(8,128)(2,1)S(1)}, u32[]{:S(2)}, u32[]{:S(2)}) collective-permute-start(bf16[32,1920]{1,0:T(8,128)(2,1)S(1)} %shard_map.66.refs_0_), channel_id=1, source_target_pairs={{0,16},{8,24},{16,0},{24,8},{1,17},{9,25},{17,1},{25,9},{2,18},{10... | collective-permute-start | bytes 368648 | tf_op jit(solution)/shard_map/ppermute | solution.py:67
  10.1 6.0 %collective-permute-start.5 = (bf16[32,1920]{1,0:T(8,128)(2,1)S(1)}, bf16[32,1920]{1,0:T(8,128)(2,1)S(1)}, u32[]{:S(2)}, u32[]{:S(2)}) collective-permute-start(bf16[32,1920]{1,0:T(8,128)(2,1)S(1)} %shard_map.66.refs_0_), channel_id=1, source_target_pairs={{0,24},{8,16},{16,8},{24,0},{1,25},{9,17},{17,9},{25,1},{2,26},{10... | collective-permute-start | bytes 368648 | tf_op jit(solution)/shard_map/ppermute | solution.py:67
  16.1 9.8 %collective-permute-start.6 = (bf16[160,1920]{1,0:T(8,128)(2,1)S(1)}, bf16[160,1920]{1,0:T(8,128)(2,1)S(1)}, u32[]{:S(2)}, u32[]{:S(2)}) collective-permute-start(bf16[160,1920]{1,0:T(8,128)(2,1)S(1)} %shard_map.68.own), channel_id=1, source_target_pairs={{0,1},{1,0},{2,3},{3,2},{4,5},{5,4},{6,7},{7,6},{8,9},{9,8},{10,11... | collective-permute-start | bytes 1843208 | tf_op jit(solution)/shard_map/ppermute | solution.py:67
  16.2 6.3 %collective-permute-start.8 = (bf16[32,1920]{1,0:T(8,128)(2,1)S(1)}, bf16[32,1920]{1,0:T(8,128)(2,1)S(1)}, u32[]{:S(2)}, u32[]{:S(2)}) collective-permute-start(bf16[32,1920]{1,0:T(8,128)(2,1)S(1)} %shard_map.67.refs_1_), channel_id=1, source_target_pairs={{0,8},{8,0},{16,24},{24,16},{1,9},{9,1},{17,25},{25,17},{2,10},{10... | collective-permute-start | bytes 368648 | tf_op jit(solution)/shard_map/ppermute | solution.py:67
  16.8 5.7 %collective-permute-start.9 = (bf16[32,1920]{1,0:T(8,128)(2,1)S(1)}, bf16[32,1920]{1,0:T(8,128)(2,1)S(1)}, u32[]{:S(2)}, u32[]{:S(2)}) collective-permute-start(bf16[32,1920]{1,0:T(8,128)(2,1)S(1)} %shard_map.67.refs_1_), channel_id=1, source_target_pairs={{0,16},{8,24},{16,0},{24,8},{1,17},{9,25},{17,1},{25,9},{2,18},{10... | collective-permute-start | bytes 368648 | tf_op jit(solution)/shard_map/ppermute | solution.py:67
  17.6 7.4 %collective-permute-start.10 = (bf16[32,1920]{1,0:T(8,128)(2,1)S(1)}, bf16[32,1920]{1,0:T(8,128)(2,1)S(1)}, u32[]{:S(2)}, u32[]{:S(2)}) collective-permute-start(bf16[32,1920]{1,0:T(8,128)(2,1)S(1)} %shard_map.67.refs_1_), channel_id=1, source_target_pairs={{0,24},{8,16},{16,8},{24,0},{1,25},{9,17},{17,9},{25,1},{2,26},{10... | collective-permute-start | bytes 368648 | tf_op jit(solution)/shard_map/ppermute | solution.py:67
  25.1 4.6 %collective-permute-start.11 = (bf16[96,1920]{1,0:T(8,128)(2,1)S(1)}, bf16[96,1920]{1,0:T(8,128)(2,1)S(1)}, u32[]{:S(2)}, u32[]{:S(2)}) collective-permute-start(bf16[96,1920]{1,0:T(8,128)(2,1)S(1)} %shard_map.72.own), channel_id=1, source_target_pairs={{0,1},{1,0},{2,3},{3,2},{4,5},{5,4},{6,7},{7,6},{8,9},{9,8},{10,11... | collective-permute-start | bytes 1105928 | tf_op jit(solution)/shard_map/ppermute | solution.py:67
  25.2 2.0 %copy-start.2 = (bf16[1,512,3584]{2,1,0:T(8,128)(2,1)S(1)}, bf16[1,512,3584]{2,1,0:T(8,128)(2,1)}, u32[]{:S(2)}) copy-start(bf16[1,512,3584]{2,1,0:T(8,128)(2,1)} %param.9) | copy-start | bytes 11010052
  28.4 4.1 %collective-permute-start.7 = (bf16[160,1792]{1,0:T(8,128)(2,1)S(1)}, bf16[160,1792]{1,0:T(8,128)(2,1)S(1)}, u32[]{:S(2)}, u32[]{:S(2)}) collective-permute-start(bf16[160,1792]{1,0:T(8,128)(2,1)S(1)} %get-tuple-element.27), channel_id=1, source_target_pairs={{0,1},{1,0},{2,3},{3,2},{4,5},{5,4},{6,7},{7,6},{8,9},{9,8},{10,11... | collective-permute-start | bytes 1720328 | tf_op jit(solution)/shard_map/ppermute | solution.py:67
  30.8 1.7 %collective-permute-start.12 = (bf16[96,1792]{1,0:T(8,128)(2,1)S(1)}, bf16[96,1792]{1,0:T(8,128)(2,1)S(1)}, u32[]{:S(2)}, u32[]{:S(2)}) collective-permute-start(bf16[96,1792]{1,0:T(8,128)(2,1)S(1)} %get-tuple-element.32), channel_id=1, source_target_pairs={{0,1},{1,0},{2,3},{3,2},{4,5},{5,4},{6,7},{7,6},{8,9},{9,8},{10,11... | collective-permute-start | bytes 1032200 | tf_op jit(solution)/shard_map/ppermute | solution.py:67
  32.7 12.8 %collective-permute-start.13 = (bf16[64,1792]{1,0:T(8,128)(2,1)S(1)}, bf16[64,1792]{1,0:T(8,128)(2,1)S(1)}, u32[]{:S(2)}, u32[]{:S(2)}) collective-permute-start(bf16[64,1792]{1,0:T(8,128)(2,1)S(1)} %get-tuple-element.33), channel_id=1, source_target_pairs={{0,8},{8,0},{16,24},{24,16},{1,9},{9,1},{17,25},{25,17},{2,10},{10... | collective-permute-start | bytes 688136 | tf_op jit(solution)/shard_map/ppermute | solution.py:67
  34.1 11.4 %collective-permute-start.14 = (bf16[64,1792]{1,0:T(8,128)(2,1)S(1)}, bf16[64,1792]{1,0:T(8,128)(2,1)S(1)}, u32[]{:S(2)}, u32[]{:S(2)}) collective-permute-start(bf16[64,1792]{1,0:T(8,128)(2,1)S(1)} %get-tuple-element.34), channel_id=1, source_target_pairs={{0,16},{8,24},{16,0},{24,8},{1,17},{9,25},{17,1},{25,9},{2,18},{10... | collective-permute-start | bytes 688136 | tf_op jit(solution)/shard_map/ppermute | solution.py:67
  35.1 6.4 %collective-permute-start.18 = (bf16[16,1792]{1,0:T(8,128)(2,1)S(1)}, bf16[16,1792]{1,0:T(8,128)(2,1)S(1)}, u32[]{:S(2)}, u32[]{:S(2)}) collective-permute-start(bf16[16,1792]{1,0:T(8,128)(2,1)S(1)} %get-tuple-element.38), channel_id=1, source_target_pairs={{0,6},{2,4},{4,2},{6,0},{1,7},{3,5},{5,3},{7,1},{8,14},{10,12},{12... | collective-permute-start | bytes 172040 | tf_op jit(solution)/shard_map/ppermute | solution.py:67
  38.9 5.1 %collective-permute-start.19 = (bf16[16,1792]{1,0:T(8,128)(2,1)S(1)}, bf16[16,1792]{1,0:T(8,128)(2,1)S(1)}, u32[]{:S(2)}, u32[]{:S(2)}) collective-permute-start(bf16[16,1792]{1,0:T(8,128)(2,1)S(1)} %get-tuple-element.39), channel_id=1, source_target_pairs={{0,4},{2,6},{4,0},{6,2},{1,5},{3,7},{5,1},{7,3},{8,12},{10,14},{12... | collective-permute-start | bytes 172040 | tf_op jit(solution)/shard_map/ppermute | solution.py:67
  38.9 5.3 %collective-permute-start.20 = (bf16[16,1792]{1,0:T(8,128)(2,1)S(1)}, bf16[16,1792]{1,0:T(8,128)(2,1)S(1)}, u32[]{:S(2)}, u32[]{:S(2)}) collective-permute-start(bf16[16,1792]{1,0:T(8,128)(2,1)S(1)} %get-tuple-element.40), channel_id=1, source_target_pairs={{0,2},{2,0},{4,6},{6,4},{1,3},{3,1},{5,7},{7,5},{8,10},{10,8},{12,... | collective-permute-start | bytes 172040 | tf_op jit(solution)/shard_map/ppermute | solution.py:67
  44.2 5.8 %collective-permute-start.21 = (bf16[16,1792]{1,0:T(8,128)(2,1)S(1)}, bf16[16,1792]{1,0:T(8,128)(2,1)S(1)}, u32[]{:S(2)}, u32[]{:S(2)}) collective-permute-start(bf16[16,1792]{1,0:T(8,128)(2,1)S(1)} %shard_map.78), channel_id=1, source_target_pairs={{0,24},{8,16},{16,8},{24,0},{1,25},{9,17},{17,9},{25,1},{2,26},{10... | collective-permute-start | bytes 172040 | tf_op jit(solution)/shard_map/ppermute | solution.py:67
  45.6 6.0 %collective-permute-start.15 = (bf16[16,1792]{1,0:T(8,128)(2,1)S(1)}, bf16[16,1792]{1,0:T(8,128)(2,1)S(1)}, u32[]{:S(2)}, u32[]{:S(2)}) collective-permute-start(bf16[16,1792]{1,0:T(8,128)(2,1)S(1)} %get-tuple-element.35), channel_id=1, source_target_pairs={{0,6},{2,4},{4,2},{6,0},{1,7},{3,5},{5,3},{7,1},{8,14},{10,12},{12... | collective-permute-start | bytes 172040 | tf_op jit(solution)/shard_map/ppermute | solution.py:67
  47.6 5.5 %collective-permute-start.16 = (bf16[16,1792]{1,0:T(8,128)(2,1)S(1)}, bf16[16,1792]{1,0:T(8,128)(2,1)S(1)}, u32[]{:S(2)}, u32[]{:S(2)}) collective-permute-start(bf16[16,1792]{1,0:T(8,128)(2,1)S(1)} %get-tuple-element.36), channel_id=1, source_target_pairs={{0,4},{2,6},{4,0},{6,2},{1,5},{3,7},{5,1},{7,3},{8,12},{10,14},{12... | collective-permute-start | bytes 172040 | tf_op jit(solution)/shard_map/ppermute | solution.py:67
  47.7 5.4 %collective-permute-start.17 = (bf16[16,1792]{1,0:T(8,128)(2,1)S(1)}, bf16[16,1792]{1,0:T(8,128)(2,1)S(1)}, u32[]{:S(2)}, u32[]{:S(2)}) collective-permute-start(bf16[16,1792]{1,0:T(8,128)(2,1)S(1)} %get-tuple-element.37), channel_id=1, source_target_pairs={{0,2},{2,0},{4,6},{6,4},{1,3},{3,1},{5,7},{7,5},{8,10},{10,8},{12,... | collective-permute-start | bytes 172040 | tf_op jit(solution)/shard_map/ppermute | solution.py:67

commit v4 on v3

--- a/solution.py
+++ b/solution.py
@@ -9,6 +9,7 @@
 
 
 LANES = 128
+SUBLANES = 8
 STALL = 20000000000
 EARLY = 2
 TILE = 256
@@ -88,10 +89,10 @@
 
 
 def prepare(owners, tok_ref, ids_ref, codes_ref, expert_ref, out_ref):
-    width = tok_ref.shape[1]
-    rows = tok_ref.shape[0]
+    rows, width = tok_ref.shape
     top_count = ids_ref.shape[0]
-    out_ref[:, :width] = tok_ref[...]
+    for i in range(width // LANES):
+        out_ref[0, i * rows : (i + 1) * rows, :] = tok_ref[:, i * LANES : (i + 1) * LANES]
     ids = jnp.transpose(ids_ref[...])
     codes = jnp.transpose(codes_ref[...].astype(F32))
     shares = codes / jnp.sum(codes, axis=1, keepdims=True)
@@ -100,20 +101,29 @@
     dense = jnp.zeros((rows, LANES), F32)
     for k in range(top_count):
         dense += jnp.where(ids[:, k : k + 1] == expert, shares[:, k : k + 1], 0.0)
-    high = dense.astype(BF16)
-    low = (dense - high.astype(F32)).astype(BF16)
-    out_ref[:, width:] = jnp.where(lane < owners, high, jnp.where(lane < 2 * owners, low, jnp.zeros_like(high)))
+    high = dense.astype(BF16).astype(F32)
+    both = jnp.where(lane < owners, high, dense - high)
+    room = LANES * SUBLANES // rows
+    tile = jnp.concatenate([both[t : t + SUBLANES, :room] for t in range(0, rows, SUBLANES)], axis=1)
+    out_ref[0, rows * width // LANES :, :] = tile.astype(BF16)
 
 
 def stack(blocks, flops=0):
     def body(*refs):
         start = 0
         for ref in refs[:-1]:
-            refs[-1][start : start + ref.shape[0], :] = ref[...]
+            refs[-1][start : start + ref.shape[0]] = ref[...]
             start += ref.shape[0]
 
-    rows = sum(b.shape[0] for b in blocks)
-    return call(body, jax.ShapeDtypeStruct((rows, blocks[0].shape[1]), BF16), *blocks, flops=flops)
+    count = sum(b.shape[0] for b in blocks)
+    return call(body, jax.ShapeDtypeStruct((count, *blocks[0].shape[1:]), BF16), *blocks, flops=flops)
+
+
+def unpack(packed, x):
+    n = x.shape[0] // packed.shape[0]
+    for b in range(packed.shape[0]):
+        for i in range(x.shape[1] // LANES):
+            x[b * n : (b + 1) * n, i * LANES : (i + 1) * LANES] = packed[b, i * n : (i + 1) * n, :]
 
 
 def dot(a, b):
@@ -133,30 +143,36 @@
     return pl.ds(pl.multiple_of(start, LANES), width)
 
 
-def enter_own(owners, own, gate, up, gated, lifted, scale):
-    rows = own.shape[0]
-    width = own.shape[1] - LANES
+def enter_own(owners, own, gate, up, gated, lifted, scale, x):
+    width = x.shape[1]
+    n = x.shape[0] // own.shape[0]
+    unpack(own, x)
     expert = lax.axis_index("dp") * lax.axis_size("expert") + lax.axis_index("expert")
-    lane = lax.broadcasted_iota(jnp.int32, (rows, LANES), 1)
-    mine = (lane == expert) | (lane == expert + owners)
-    share = jnp.sum(jnp.where(mine, own[:, width:].astype(F32), 0.0), axis=1, keepdims=True)
-    scale[...] = jnp.broadcast_to(share, (rows, LANES))
+    lane = lax.broadcasted_iota(jnp.int32, (SUBLANES, LANES), 1)
+    for b in range(own.shape[0]):
+        tile = own[b, n * width // LANES :, :].astype(F32)
+        for t in range(0, n, SUBLANES):
+            at = lane - t * LANES // n
+            mine = (at == expert) | (at == expert + owners)
+            share = jnp.sum(jnp.where(mine, tile, 0.0), axis=1, keepdims=True)
+            scale[b * n + t : b * n + t + SUBLANES, :] = jnp.broadcast_to(share, (SUBLANES, LANES))
     at = half_rows(width, True)
     for weight, out in ((gate, gated), (up, lifted)):
-        out[...] = dot(own[:, :width], weight[at, :])
+        out[...] = dot(x[...], weight[at, :])
 
 
 def leave(at, scale, hidden, down, out):
     out[...] = (dot(hidden[...], down[:, at]) * scale[:, :1]).astype(BF16)
 
 
-def enter_other(other, gate, up, down, gated, lifted, scale, hidden, send):
+def enter_other(other, gate, up, down, gated, lifted, scale, hidden, send, x):
     width = send.shape[1]
+    unpack(other, x)
     at = half_rows(width, False)
     for i in range(0, hidden.shape[1], TILE):
         there = pl.ds(i, TILE)
-        g = gated[:, there] + dot(other[:, :width], gate[at, there])
-        u = lifted[:, there] + dot(other[:, :width], up[at, there])
+        g = gated[:, there] + dot(x[...], gate[at, there])
+        u = lifted[:, there] + dot(x[...], up[at, there])
         hidden[:, there] = (jax.nn.silu(g) * u).astype(BF16)
     leave(at, scale, hidden, down, send)
 
@@ -179,7 +195,7 @@
     experts = call(functools.partial(table, owners), jax.ShapeDtypeStruct((n, LANES), jnp.int32), flops=STALL)
     first = call(
         functools.partial(prepare, owners),
-        jax.ShapeDtypeStruct((n, width + LANES), BF16),
+        jax.ShapeDtypeStruct((1, n * width // LANES + SUBLANES, LANES), BF16),
         tokens[0], expert_ids[0].T, gate_codes[0].T, experts,
     )
     line = {j: swap(first, "expert", j) for j in reversed(hops)}
@@ -187,23 +203,25 @@
     late = [line[j] for j in range(EARLY, ex)]
     parts_a = stack(early)
     parts_b = stack(late, flops=STALL)
-    sent_a = {g: swap(parts_a, "dp", g) for g in range(1, dp)}
+    sent_a = {g: swap(parts_a if g < 3 else first, "dp", g) for g in range(1, dp)}
+    turned = swap(sent_a[3], "expert", 1)
     sent_b = {g: swap(parts_b, "dp", g) for g in range(1, dp)}
     near = stack([parts_a, parts_b] + [sent_a[g] for g in range(1, dp)])
-    far = stack([sent_b[g] for g in range(1, dp)])
+    far = stack([sent_b[g] for g in range(1, dp)] + [turned])
     gate, up, down = gate_weight[0], up_weight[0], down_weight[0]
 
     def run(own):
-        count = own.shape[0]
+        count = own.shape[0] * n
+        scratch = [pltpu.VMEM((count, width), BF16)]
         floats = jax.ShapeDtypeStruct((count, units), F32)
         other = swap(own, "tensor", 1)
         gated, lifted, scale = call(
             functools.partial(enter_own, owners), [floats, floats, jax.ShapeDtypeStruct((count, LANES), F32)],
-            own, gate, up, flops=HINT, limit=8,
+            own, gate, up, flops=HINT, limit=8, scratch=scratch,
         )
         hidden, send = call(
             enter_other, [jax.ShapeDtypeStruct((count, units), BF16), block(count)],
-            other, gate, up, down, gated, lifted, scale, flops=HINT, limit=8,
+            other, gate, up, down, gated, lifted, scale, flops=HINT, limit=8, scratch=scratch,
         )
         keep = call(leave_own, block(count), hidden, down, scale, flops=HINT, limit=8)
         return keep, send
@@ -221,7 +239,7 @@
             out[cut:, :] = plus(keep_b[there, :], recv_b[there, :]).astype(BF16)
         for j, out in zip(hops, diag):
             if j < EARLY:
-                keep, recv, here = keep_a, recv_a, pl.ds(rows + 2 * cut + j * n, n)
+                keep, recv, here = keep_b, recv_b, pl.ds((dp - 1) * (rows - cut) + (j - 1) * n, n)
             else:
                 keep, recv, here = keep_b, recv_b, pl.ds(2 * (rows - cut) + (j - EARLY) * n, n)
             out[...] = plus(keep[here, :], recv[here, :]).astype(BF16)
@@ -258,7 +276,7 @@
     slot_depth = min(tok_rows, max(2, 2 * tok_rows * top_count // owners))
     args = (tokens, gate_weight, up_weight, down_weight, expert_ids, gate_codes)
     grid = dp == 4 and ex & (ex - 1) == 0 and ex > 1 and lax.axis_size("tensor") == 2
-    if slot_depth == tok_rows and grid and 2 * owners <= LANES:
+    if slot_depth == tok_rows and grid and tok_rows % SUBLANES == 0 and 2 * owners * tok_rows <= LANES * SUBLANES:
         return dense(*args)
     return slotted(*args, slot_depth)
 

time: 54 us -> 53.2 us (0.985)
  waiting for transfers between devices: 19.4 us -> 18 us
  starting transfers between devices: 26.1 us -> 26.7 us
    ppermute x22 -> x23, waiting for transfers between devices: 19.4 us -> 18 us  [swap(): return lax.ppermute(x, axis, [(i, i ^ offset) for i in range(count)])]
    ppermute x22 -> x23, starting transfers between devices: 26.1 us -> 26.7 us  [swap(): return lax.ppermute(x, axis, [(i, i ^ offset) for i in range(count)])]
  transfers between devices with their start and end apart: 22 -> 23, of which waited for: 11 -> 11; matrix products, arithmetic and copies ran while one was open for 0% -> 0% of each run, Pallas kernels for 9% -> 9%
where the time goes in v4:
time: 53.2 us; the launch traced here: 53 us
  starting transfers between devices  26.7 us (50%)
  waiting for transfers between devices  18 us (34%)
  Pallas kernels  6.01 us (11%)
  local copies, waits for them, and re-layouts  2.12 us (4%)
    ppermute x23, starting transfers between devices, swap(): return lax.ppermute(x, axis, [(i, i ^ offset) for i in range(count)])  26.7 us
    ppermute x23, waiting for transfers between devices, swap(): return lax.ppermute(x, axis, [(i, i ^ offset) for i in range(count)])  18 us
    pallas_call x16, Pallas kernels, call(): pl.pallas_call(body, out_shape=outs, in_specs=[VMEM] * len(args), out_spe...  6.01 us
    unnamed x12, local copies, waits for them, and re-layouts  2.12 us
  transfers between devices with their start and end apart: 23, of which 11 were waited for; matrix products, arithmetic and copies ran while one was open for 0% of the time, Pallas kernels for 9%

profile of v4, /device:TPU:0, one launch (start us, length us, event | category | flops | bytes accessed | tf_op | source)
XLA Modules:
  0.0 53.0 jit_solution(6819891801821030325)
XLA Ops:
  0.0 0.8 %copy-done.3 = bf16[1,16,1792]{2,1,0:T(8,128)(2,1)S(1)} copy-done((bf16[1,16,1792]{2,1,0:T(8,128)(2,1)S(1)}, bf16[1,16,1792]{2,1,0:T(8,128)(2,1)}, u32[]{:S(2)}) %copy-start.3) | copy-done | bytes 57368
  0.8 0.0 copy-done.4
  0.8 0.0 copy-done.5
  0.8 0.3 shard_map.65.refs_0_
  1.1 3.1 %collective-permute-start = (bf16[1,232,128]{2,1,0:T(8,128)(2,1)S(1)}, bf16[1,232,128]{2,1,0:T(8,128)(2,1)S(1)}, u32[]{:S(2)}, u32[]{:S(2)}) collective-permute-start(bf16[1,232,128]{2,1,0:T(8,128)(2,1)S(1)} %shard_map.65.refs_0_), channel_id=1, source_target_pairs={{0,2},{2,0},{4,6},{6,4},{1,3},{3,1},{5,7},{7,5},{8,10},{10,8},{12,... | collective-permute-start | bytes 178184 | tf_op jit(solution)/shard_map/ppermute | solution.py:68
  4.2 2.6 %collective-permute-start.1 = (bf16[1,232,128]{2,1,0:T(8,128)(2,1)S(1)}, bf16[1,232,128]{2,1,0:T(8,128)(2,1)S(1)}, u32[]{:S(2)}, u32[]{:S(2)}) collective-permute-start(bf16[1,232,128]{2,1,0:T(8,128)(2,1)S(1)} %shard_map.65.refs_0_), channel_id=1, source_target_pairs={{0,4},{2,6},{4,0},{6,2},{1,5},{3,7},{5,1},{7,3},{8,12},{10,14},{12... | collective-permute-start | bytes 178184 | tf_op jit(solution)/shard_map/ppermute | solution.py:68
  6.8 0.0 collective-permute-start.2
  6.8 2.7 %collective-permute-start.5 = (bf16[1,232,128]{2,1,0:T(8,128)(2,1)S(1)}, bf16[1,232,128]{2,1,0:T(8,128)(2,1)S(1)}, u32[]{:S(2)}, u32[]{:S(2)}) collective-permute-start(bf16[1,232,128]{2,1,0:T(8,128)(2,1)S(1)} %shard_map.65.refs_0_), channel_id=1, source_target_pairs={{0,24},{8,16},{16,8},{24,0},{1,25},{9,17},{17,9},{25,1},{2,26},{10... | collective-permute-start | bytes 178184 | tf_op jit(solution)/shard_map/ppermute | solution.py:68
  9.5 0.0 collective-permute-done.refs_1_
  9.5 0.0 copy-start
  9.5 0.0 copy-start.1
  9.5 0.6 %collective-permute-start.3 = (bf16[2,232,128]{2,1,0:T(8,128)(2,1)S(1)}, bf16[2,232,128]{2,1,0:T(8,128)(2,1)S(1)}, u32[]{:S(2)}, u32[]{:S(2)}) collective-permute-start(bf16[2,232,128]{2,1,0:T(8,128)(2,1)S(1)} %shard_map.66.refs_0_), channel_id=1, source_target_pairs={{0,8},{8,0},{16,24},{24,16},{1,9},{9,1},{17,25},{25,17},{2,10},{10... | collective-permute-start | bytes 356360 | tf_op jit(solution)/shard_map/ppermute | solution.py:68
  10.1 0.3 collective-permute-start.4
  10.4 0.1 collective-permute-done.1.refs_0_
  10.5 2.3 %collective-permute-done.2.refs_1_ = bf16[1,232,128]{2,1,0:T(8,128)(2,1)S(1)} collective-permute-done((bf16[1,232,128]{2,1,0:T(8,128)(2,1)S(1)}, bf16[1,232,128]{2,1,0:T(8,128)(2,1)S(1)}, u32[]{:S(2)}, u32[]{:S(2)}) %collective-permute-start.2) | collective-permute-done | bytes 59424 | tf_op jit(solution)/shard_map/ppermute | solution.py:68
  12.8 0.0 collective-permute-done.5.refs_4_
  12.8 1.6 %collective-permute-done.3.refs_2_ = bf16[2,232,128]{2,1,0:T(8,128)(2,1)S(1)} collective-permute-done((bf16[2,232,128]{2,1,0:T(8,128)(2,1)S(1)}, bf16[2,232,128]{2,1,0:T(8,128)(2,1)S(1)}, u32[]{:S(2)}, u32[]{:S(2)}) %collective-permute-start.3) | collective-permute-done | bytes 118816 | tf_op jit(solution)/shard_map/ppermute | solution.py:68
  14.4 0.5 %collective-permute-done.4.refs_3_ = bf16[2,232,128]{2,1,0:T(8,128)(2,1)S(1)} collective-permute-done((bf16[2,232,128]{2,1,0:T(8,128)(2,1)S(1)}, bf16[2,232,128]{2,1,0:T(8,128)(2,1)S(1)}, u32[]{:S(2)}, u32[]{:S(2)}) %collective-permute-start.4) | collective-permute-done | bytes 118816 | tf_op jit(solution)/shard_map/ppermute | solution.py:68
  15.0 0.1 collective-permute-start.6
  15.1 1.6 %collective-permute-start.8 = (bf16[2,232,128]{2,1,0:T(8,128)(2,1)S(1)}, bf16[2,232,128]{2,1,0:T(8,128)(2,1)S(1)}, u32[]{:S(2)}, u32[]{:S(2)}) collective-permute-start(bf16[2,232,128]{2,1,0:T(8,128)(2,1)S(1)} %shard_map.67.refs_1_), channel_id=1, source_target_pairs={{0,8},{8,0},{16,24},{24,16},{1,9},{9,1},{17,25},{25,17},{2,10},{10... | collective-permute-start | bytes 356360 | tf_op jit(solution)/shard_map/ppermute | solution.py:68
  16.6 0.5 collective-permute-start.9
  17.1 1.5 %collective-permute-start.10 = (bf16[2,232,128]{2,1,0:T(8,128)(2,1)S(1)}, bf16[2,232,128]{2,1,0:T(8,128)(2,1)S(1)}, u32[]{:S(2)}, u32[]{:S(2)}) collective-permute-start(bf16[2,232,128]{2,1,0:T(8,128)(2,1)S(1)} %shard_map.67.refs_1_), channel_id=1, source_target_pairs={{0,24},{8,16},{16,8},{24,0},{1,25},{9,17},{17,9},{25,1},{2,26},{10... | collective-permute-start | bytes 356360 | tf_op jit(solution)/shard_map/ppermute | solution.py:68
  18.6 0.7 %collective-permute-start.11 = (bf16[1,232,128]{2,1,0:T(8,128)(2,1)S(1)}, bf16[1,232,128]{2,1,0:T(8,128)(2,1)S(1)}, u32[]{:S(2)}, u32[]{:S(2)}) collective-permute-start(bf16[1,232,128]{2,1,0:T(8,128)(2,1)S(1)} %collective-permute-done.5.refs_4_), channel_id=1, source_target_pairs={{0,2},{2,0},{4,6},{6,4},{1,3},{3,1},{5,7},{7,5},{8,10},{10,8},{12,... | collective-permute-start | bytes 178184 | tf_op jit(solution)/shard_map/ppermute | solution.py:68
  19.3 3.5 %collective-permute-done.11.refs_3_ = bf16[1,232,128]{2,1,0:T(8,128)(2,1)S(1)} collective-permute-done((bf16[1,232,128]{2,1,0:T(8,128)(2,1)S(1)}, bf16[1,232,128]{2,1,0:T(8,128)(2,1)S(1)}, u32[]{:S(2)}, u32[]{:S(2)}) %collective-permute-start.11) | collective-permute-done | bytes 59424 | tf_op jit(solution)/shard_map/ppermute | solution.py:68
  22.8 0.0 collective-permute-done.8.refs_0_
  22.8 1.6 %collective-permute-done.9.refs_1_ = bf16[2,232,128]{2,1,0:T(8,128)(2,1)S(1)} collective-permute-done((bf16[2,232,128]{2,1,0:T(8,128)(2,1)S(1)}, bf16[2,232,128]{2,1,0:T(8,128)(2,1)S(1)}, u32[]{:S(2)}, u32[]{:S(2)}) %collective-permute-start.9) | collective-permute-done | bytes 118816 | tf_op jit(solution)/shard_map/ppermute | solution.py:68
  24.4 0.0 collective-permute-done.10.refs_2_
  24.5 0.1 collective-permute-start.12
  24.6 0.0 copy-done
  24.6 0.7 %shard_map.69 = (f32[144,512]{1,0:T(8,128)S(1)}, f32[144,512]{1,0:T(8,128)S(1)}, f32[144,128]{1,0:T(8,128)S(1)}) custom-call(bf16[9,232,128]{2,1,0:T(8,128)(2,1)S(1)} %shard_map.68.own, bf16[3584,512]{1,0:T(8,128)(2,1)S(1)} %bitcast.11, bf16[3584,512]{1,0:T(8,128)(2,1)S(1)} %bitcast.15), custom_call_target="tpu_custom_call" | custom-call | flops 2000000000 | tf_op jit(solution)/shard_map/pallas_call | solution.py:76
  25.3 0.0 copy-start.2
  25.3 0.7 %shard_map.73 = (f32[112,512]{1,0:T(8,128)S(1)}, f32[112,512]{1,0:T(8,128)S(1)}, f32[112,128]{1,0:T(8,128)S(1)}) custom-call(bf16[7,232,128]{2,1,0:T(8,128)(2,1)S(1)} %shard_map.72.own, bf16[3584,512]{1,0:T(8,128)(2,1)S(1)} %bitcast.12, bf16[3584,512]{1,0:T(8,128)(2,1)S(1)} %bitcast.16), custom_call_target="tpu_custom_call" | custom-call | flops 2000000000 | tf_op jit(solution)/shard_map/pallas_call | solution.py:76
  26.1 0.0 collective-permute-done.6.other
  26.1 1.3 %copy-done.2 = bf16[1,512,3584]{2,1,0:T(8,128)(2,1)S(1)} copy-done((bf16[1,512,3584]{2,1,0:T(8,128)(2,1)S(1)}, bf16[1,512,3584]{2,1,0:T(8,128)(2,1)}, u32[]{:S(2)}) %copy-start.2) | copy-done | bytes 3670040
  27.4 1.2 %shard_map.70 = (bf16[144,512]{1,0:T(8,128)(2,1)S(1)}, bf16[144,1792]{1,0:T(8,128)(2,1)S(1)}) custom-call(bf16[9,232,128]{2,1,0:T(8,128)(2,1)S(1)} %collective-permute-done.6.other, bf16[3584,512]{1,0:T(8,128)(2,1)S(1)} %bitcast.13, bf16[3584,512]{1,0:T(8,128)(2,1)S(1)} %bitcast.17, bf16[512,3584]{1,0:T(8,128)(2,1)S(1)} %bitcast.19, ...), custom_call_target="tpu_custom_call" | custom-call | flops 2000000000 | tf_op jit(solution)/shard_map/pallas_call | solution.py:76
  28.5 0.6 %collective-permute-start.7 = (bf16[144,1792]{1,0:T(8,128)(2,1)S(1)}, bf16[144,1792]{1,0:T(8,128)(2,1)S(1)}, u32[]{:S(2)}, u32[]{:S(2)}) collective-permute-start(bf16[144,1792]{1,0:T(8,128)(2,1)S(1)} %get-tuple-element.27), channel_id=1, source_target_pairs={{0,1},{1,0},{2,3},{3,2},{4,5},{5,4},{6,7},{7,6},{8,9},{9,8},{10,11... | collective-permute-start | bytes 1548296 | tf_op jit(solution)/shard_map/ppermute | solution.py:68
  29.1 0.0 collective-permute-done.12.other
  29.1 1.1 %shard_map.74 = (bf16[112,512]{1,0:T(8,128)(2,1)S(1)}, bf16[112,1792]{1,0:T(8,128)(2,1)S(1)}) custom-call(bf16[7,232,128]{2,1,0:T(8,128)(2,1)S(1)} %collective-permute-done.12.other, bf16[3584,512]{1,0:T(8,128)(2,1)S(1)} %bitcast.14, bf16[3584,512]{1,0:T(8,128)(2,1)S(1)} %bitcast.18, bf16[512,3584]{1,0:T(8,128)(2,1)S(1)} %bitcast.20, ...), custom_call_target="tpu_custom_call" | custom-call | flops 2000000000 | tf_op jit(solution)/shard_map/pallas_call | solution.py:76
  30.2 0.1 collective-permute-start.13
  30.3 0.4 shard_map.75.keep_b
  30.8 0.5 shard_map.71.keep_a.keep
  31.2 0.8 %collective-permute-done.13.recv_b = bf16[112,1792]{1,0:T(8,128)(2,1)S(1)} collective-permute-done((bf16[112,1792]{1,0:T(8,128)(2,1)S(1)}, bf16[112,1792]{1,0:T(8,128)(2,1)S(1)}, u32[]{:S(2)}, u32[]{:S(2)}) %collective-permute-start.13) | collective-permute-done | bytes 401440 | tf_op jit(solution)/shard_map/ppermute | solution.py:68
  32.0 0.0 collective-permute-done.7.recv_a.recv
  32.0 0.1 shard_map.76
  32.2 0.6 %collective-permute-start.14 = (bf16[64,1792]{1,0:T(8,128)(2,1)S(1)}, bf16[64,1792]{1,0:T(8,128)(2,1)S(1)}, u32[]{:S(2)}, u32[]{:S(2)}) collective-permute-start(bf16[64,1792]{1,0:T(8,128)(2,1)S(1)} %get-tuple-element.33), channel_id=1, source_target_pairs={{0,8},{8,0},{16,24},{24,16},{1,9},{9,1},{17,25},{25,17},{2,10},{10... | collective-permute-start | bytes 688136 | tf_op jit(solution)/shard_map/ppermute | solution.py:68
  32.8 1.2 %collective-permute-start.15 = (bf16[64,1792]{1,0:T(8,128)(2,1)S(1)}, bf16[64,1792]{1,0:T(8,128)(2,1)S(1)}, u32[]{:S(2)}, u32[]{:S(2)}) collective-permute-start(bf16[64,1792]{1,0:T(8,128)(2,1)S(1)} %get-tuple-element.34), channel_id=1, source_target_pairs={{0,16},{8,24},{16,0},{24,8},{1,17},{9,25},{17,1},{25,9},{2,18},{10... | collective-permute-start | bytes 688136 | tf_op jit(solution)/shard_map/ppermute | solution.py:68
  34.0 3.6 %collective-permute-start.19 = (bf16[16,1792]{1,0:T(8,128)(2,1)S(1)}, bf16[16,1792]{1,0:T(8,128)(2,1)S(1)}, u32[]{:S(2)}, u32[]{:S(2)}) collective-permute-start(bf16[16,1792]{1,0:T(8,128)(2,1)S(1)} %get-tuple-element.38), channel_id=1, source_target_pairs={{0,6},{2,4},{4,2},{6,0},{1,7},{3,5},{5,3},{7,1},{8,14},{10,12},{12... | collective-permute-start | bytes 172040 | tf_op jit(solution)/shard_map/ppermute | solution.py:68
  37.6 0.0 collective-permute-start.20
  37.6 0.8 %collective-permute-start.21 = (bf16[16,1792]{1,0:T(8,128)(2,1)S(1)}, bf16[16,1792]{1,0:T(8,128)(2,1)S(1)}, u32[]{:S(2)}, u32[]{:S(2)}) collective-permute-start(bf16[16,1792]{1,0:T(8,128)(2,1)S(1)} %get-tuple-element.40), channel_id=1, source_target_pairs={{0,2},{2,0},{4,6},{6,4},{1,3},{3,1},{5,7},{7,5},{8,10},{10,8},{12,... | collective-permute-start | bytes 172040 | tf_op jit(solution)/shard_map/ppermute | solution.py:68
  38.4 1.6 %collective-permute-done.19.rest_0_ = bf16[16,1792]{1,0:T(8,128)(2,1)S(1)} collective-permute-done((bf16[16,1792]{1,0:T(8,128)(2,1)S(1)}, bf16[16,1792]{1,0:T(8,128)(2,1)S(1)}, u32[]{:S(2)}, u32[]{:S(2)}) %collective-permute-start.19) | collective-permute-done | bytes 57376 | tf_op jit(solution)/shard_map/ppermute | solution.py:68
  40.0 2.6 %collective-permute-done.20.rest_1_ = bf16[16,1792]{1,0:T(8,128)(2,1)S(1)} collective-permute-done((bf16[16,1792]{1,0:T(8,128)(2,1)S(1)}, bf16[16,1792]{1,0:T(8,128)(2,1)S(1)}, u32[]{:S(2)}, u32[]{:S(2)}) %collective-permute-start.20) | collective-permute-done | bytes 57376 | tf_op jit(solution)/shard_map/ppermute | solution.py:68
  42.7 0.0 collective-permute-done.21.rest_2_
  42.7 1.8 %collective-permute-start.22 = (bf16[16,1792]{1,0:T(8,128)(2,1)S(1)}, bf16[16,1792]{1,0:T(8,128)(2,1)S(1)}, u32[]{:S(2)}, u32[]{:S(2)}) collective-permute-start(bf16[16,1792]{1,0:T(8,128)(2,1)S(1)} %shard_map.78), channel_id=1, source_target_pairs={{0,24},{8,16},{16,8},{24,0},{1,25},{9,17},{17,9},{25,1},{2,26},{10... | collective-permute-start | bytes 172040 | tf_op jit(solution)/shard_map/ppermute | solution.py:68
  44.5 0.0 collective-permute-done.14.x
  44.5 0.0 collective-permute-done.15.y
  44.5 0.1 shard_map.77
  44.6 2.0 %collective-permute-start.16 = (bf16[16,1792]{1,0:T(8,128)(2,1)S(1)}, bf16[16,1792]{1,0:T(8,128)(2,1)S(1)}, u32[]{:S(2)}, u32[]{:S(2)}) collective-permute-start(bf16[16,1792]{1,0:T(8,128)(2,1)S(1)} %get-tuple-element.35), channel_id=1, source_target_pairs={{0,6},{2,4},{4,2},{6,0},{1,7},{3,5},{5,3},{7,1},{8,14},{10,12},{12... | collective-permute-start | bytes 172040 | tf_op jit(solution)/shard_map/ppermute | solution.py:68
  46.7 0.3 collective-permute-start.17
  46.9 2.2 %collective-permute-start.18 = (bf16[16,1792]{1,0:T(8,128)(2,1)S(1)}, bf16[16,1792]{1,0:T(8,128)(2,1)S(1)}, u32[]{:S(2)}, u32[]{:S(2)}) collective-permute-start(bf16[16,1792]{1,0:T(8,128)(2,1)S(1)} %get-tuple-element.37), channel_id=1, source_target_pairs={{0,2},{2,0},{4,6},{6,4},{1,3},{3,1},{5,7},{7,5},{8,10},{10,8},{12,... | collective-permute-start | bytes 172040 | tf_op jit(solution)/shard_map/ppermute | solution.py:68
  49.1 0.0 collective-permute-done.22.rest_3_
  49.1 1.6 %collective-permute-done.16.rest_0_ = bf16[16,1792]{1,0:T(8,128)(2,1)S(1)} collective-permute-done((bf16[16,1792]{1,0:T(8,128)(2,1)S(1)}, bf16[16,1792]{1,0:T(8,128)(2,1)S(1)}, u32[]{:S(2)}, u32[]{:S(2)}) %collective-permute-start.16) | collective-permute-done | bytes 57376 | tf_op jit(solution)/shard_map/ppermute | solution.py:68
  50.7 1.7 %collective-permute-done.17.rest_1_ = bf16[16,1792]{1,0:T(8,128)(2,1)S(1)} collective-permute-done((bf16[16,1792]{1,0:T(8,128)(2,1)S(1)}, bf16[16,1792]{1,0:T(8,128)(2,1)S(1)}, u32[]{:S(2)}, u32[]{:S(2)}) %collective-permute-start.17) | collective-permute-done | bytes 57376 | tf_op jit(solution)/shard_map/ppermute | solution.py:68
  52.3 0.0 collective-permute-done.18.rest_2_
  52.3 0.7 %shard_map.79 = bf16[16,1792]{1,0:T(8,128)(2,1)} custom-call(bf16[144,1792]{1,0:T(8,128)(2,1)S(1)} %shard_map.71.keep_a.keep, bf16[144,1792]{1,0:T(8,128)(2,1)S(1)} %collective-permute-done.7.recv_a.recv, bf16[64,1792]{1,0:T(8,128)(2,1)S(1)} %collective-permute-done.14.x, bf16[64,1792]{1,0:T(8,128)(2,1)S(1)} %collective-permute-done.15.y, ...), custom_call_target="tpu_custom_call" | custom-call | tf_op jit(solution)/shard_map/pallas_call | solution.py:76
  (10 shorter events, 0.1 us)
Async XLA Ops:
  0.0 0.8 %copy-start.3 = (bf16[1,16,1792]{2,1,0:T(8,128)(2,1)S(1)}, bf16[1,16,1792]{2,1,0:T(8,128)(2,1)}, u32[]{:S(2)}) copy-start(bf16[1,16,1792]{2,1,0:T(8,128)(2,1)} %param.6) | copy-start | bytes 172036
  0.0 0.8 %copy-start.4 = (s32[1,16,8]{1,2,0:T(8,128)S(1)}, s32[1,16,8]{1,2,0:T(8,128)}, u32[]{:S(2)}) copy-start(s32[1,16,8]{1,2,0:T(8,128)} %param.10) | copy-start | bytes 1540
  0.0 0.8 %copy-start.5 = (s32[1,16,8]{1,2,0:T(8,128)S(1)}, s32[1,16,8]{1,2,0:T(8,128)}, u32[]{:S(2)}) copy-start(s32[1,16,8]{1,2,0:T(8,128)} %param.11) | copy-start | bytes 1540
  1.1 8.3 %collective-permute-start = (bf16[1,232,128]{2,1,0:T(8,128)(2,1)S(1)}, bf16[1,232,128]{2,1,0:T(8,128)(2,1)S(1)}, u32[]{:S(2)}, u32[]{:S(2)}) collective-permute-start(bf16[1,232,128]{2,1,0:T(8,128)(2,1)S(1)} %shard_map.65.refs_0_), channel_id=1, source_target_pairs={{0,2},{2,0},{4,6},{6,4},{1,3},{3,1},{5,7},{7,5},{8,10},{10,8},{12,... | collective-permute-start | bytes 178184 | tf_op jit(solution)/shard_map/ppermute | solution.py:68
  4.2 6.3 %collective-permute-start.1 = (bf16[1,232,128]{2,1,0:T(8,128)(2,1)S(1)}, bf16[1,232,128]{2,1,0:T(8,128)(2,1)S(1)}, u32[]{:S(2)}, u32[]{:S(2)}) collective-permute-start(bf16[1,232,128]{2,1,0:T(8,128)(2,1)S(1)} %shard_map.65.refs_0_), channel_id=1, source_target_pairs={{0,4},{2,6},{4,0},{6,2},{1,5},{3,7},{5,1},{7,3},{8,12},{10,14},{12... | collective-permute-start | bytes 178184 | tf_op jit(solution)/shard_map/ppermute | solution.py:68
  6.8 6.0 %collective-permute-start.2 = (bf16[1,232,128]{2,1,0:T(8,128)(2,1)S(1)}, bf16[1,232,128]{2,1,0:T(8,128)(2,1)S(1)}, u32[]{:S(2)}, u32[]{:S(2)}) collective-permute-start(bf16[1,232,128]{2,1,0:T(8,128)(2,1)S(1)} %shard_map.65.refs_0_), channel_id=1, source_target_pairs={{0,6},{2,4},{4,2},{6,0},{1,7},{3,5},{5,3},{7,1},{8,14},{10,12},{12... | collective-permute-start | bytes 178184 | tf_op jit(solution)/shard_map/ppermute | solution.py:68
  6.8 6.0 %collective-permute-start.5 = (bf16[1,232,128]{2,1,0:T(8,128)(2,1)S(1)}, bf16[1,232,128]{2,1,0:T(8,128)(2,1)S(1)}, u32[]{:S(2)}, u32[]{:S(2)}) collective-permute-start(bf16[1,232,128]{2,1,0:T(8,128)(2,1)S(1)} %shard_map.65.refs_0_), channel_id=1, source_target_pairs={{0,24},{8,16},{16,8},{24,0},{1,25},{9,17},{17,9},{25,1},{2,26},{10... | collective-permute-start | bytes 178184 | tf_op jit(solution)/shard_map/ppermute | solution.py:68
  9.5 15.1 %copy-start = (bf16[1,3584,512]{2,1,0:T(8,128)(2,1)S(1)}, bf16[1,3584,512]{2,1,0:T(8,128)(2,1)}, u32[]{:S(2)}) copy-start(bf16[1,3584,512]{2,1,0:T(8,128)(2,1)} %param.7) | copy-start | bytes 11010052
  9.5 15.1 %copy-start.1 = (bf16[1,3584,512]{2,1,0:T(8,128)(2,1)S(1)}, bf16[1,3584,512]{2,1,0:T(8,128)(2,1)}, u32[]{:S(2)}) copy-start(bf16[1,3584,512]{2,1,0:T(8,128)(2,1)} %param.8) | copy-start | bytes 11010052
  9.5 4.9 %collective-permute-start.3 = (bf16[2,232,128]{2,1,0:T(8,128)(2,1)S(1)}, bf16[2,232,128]{2,1,0:T(8,128)(2,1)S(1)}, u32[]{:S(2)}, u32[]{:S(2)}) collective-permute-start(bf16[2,232,128]{2,1,0:T(8,128)(2,1)S(1)} %shard_map.66.refs_0_), channel_id=1, source_target_pairs={{0,8},{8,0},{16,24},{24,16},{1,9},{9,1},{17,25},{25,17},{2,10},{10... | collective-permute-start | bytes 356360 | tf_op jit(solution)/shard_map/ppermute | solution.py:68
  10.1 4.8 %collective-permute-start.4 = (bf16[2,232,128]{2,1,0:T(8,128)(2,1)S(1)}, bf16[2,232,128]{2,1,0:T(8,128)(2,1)S(1)}, u32[]{:S(2)}, u32[]{:S(2)}) collective-permute-start(bf16[2,232,128]{2,1,0:T(8,128)(2,1)S(1)} %shard_map.66.refs_0_), channel_id=1, source_target_pairs={{0,16},{8,24},{16,0},{24,8},{1,17},{9,25},{17,1},{25,9},{2,18},{10... | collective-permute-start | bytes 356360 | tf_op jit(solution)/shard_map/ppermute | solution.py:68
  15.0 11.1 %collective-permute-start.6 = (bf16[9,232,128]{2,1,0:T(8,128)(2,1)S(1)}, bf16[9,232,128]{2,1,0:T(8,128)(2,1)S(1)}, u32[]{:S(2)}, u32[]{:S(2)}) collective-permute-start(bf16[9,232,128]{2,1,0:T(8,128)(2,1)S(1)} %shard_map.68.own), channel_id=1, source_target_pairs={{0,1},{1,0},{2,3},{3,2},{4,5},{5,4},{6,7},{7,6},{8,9},{9,8},{10,11... | collective-permute-start | bytes 1603592 | tf_op jit(solution)/shard_map/ppermute | solution.py:68
  15.1 7.8 %collective-permute-start.8 = (bf16[2,232,128]{2,1,0:T(8,128)(2,1)S(1)}, bf16[2,232,128]{2,1,0:T(8,128)(2,1)S(1)}, u32[]{:S(2)}, u32[]{:S(2)}) collective-permute-start(bf16[2,232,128]{2,1,0:T(8,128)(2,1)S(1)} %shard_map.67.refs_1_), channel_id=1, source_target_pairs={{0,8},{8,0},{16,24},{24,16},{1,9},{9,1},{17,25},{25,17},{2,10},{10... | collective-permute-start | bytes 356360 | tf_op jit(solution)/shard_map/ppermute | solution.py:68
  16.6 7.8 %collective-permute-start.9 = (bf16[2,232,128]{2,1,0:T(8,128)(2,1)S(1)}, bf16[2,232,128]{2,1,0:T(8,128)(2,1)S(1)}, u32[]{:S(2)}, u32[]{:S(2)}) collective-permute-start(bf16[2,232,128]{2,1,0:T(8,128)(2,1)S(1)} %shard_map.67.refs_1_), channel_id=1, source_target_pairs={{0,16},{8,24},{16,0},{24,8},{1,17},{9,25},{17,1},{25,9},{2,18},{10... | collective-permute-start | bytes 356360 | tf_op jit(solution)/shard_map/ppermute | solution.py:68
  17.1 7.3 %collective-permute-start.10 = (bf16[2,232,128]{2,1,0:T(8,128)(2,1)S(1)}, bf16[2,232,128]{2,1,0:T(8,128)(2,1)S(1)}, u32[]{:S(2)}, u32[]{:S(2)}) collective-permute-start(bf16[2,232,128]{2,1,0:T(8,128)(2,1)S(1)} %shard_map.67.refs_1_), channel_id=1, source_target_pairs={{0,24},{8,16},{16,8},{24,0},{1,25},{9,17},{17,9},{25,1},{2,26},{10... | collective-permute-start | bytes 356360 | tf_op jit(solution)/shard_map/ppermute | solution.py:68
  18.6 4.2 %collective-permute-start.11 = (bf16[1,232,128]{2,1,0:T(8,128)(2,1)S(1)}, bf16[1,232,128]{2,1,0:T(8,128)(2,1)S(1)}, u32[]{:S(2)}, u32[]{:S(2)}) collective-permute-start(bf16[1,232,128]{2,1,0:T(8,128)(2,1)S(1)} %collective-permute-done.5.refs_4_), channel_id=1, source_target_pairs={{0,2},{2,0},{4,6},{6,4},{1,3},{3,1},{5,7},{7,5},{8,10},{10,8},{12,... | collective-permute-start | bytes 178184 | tf_op jit(solution)/shard_map/ppermute | solution.py:68
  24.5 4.6 %collective-permute-start.12 = (bf16[7,232,128]{2,1,0:T(8,128)(2,1)S(1)}, bf16[7,232,128]{2,1,0:T(8,128)(2,1)S(1)}, u32[]{:S(2)}, u32[]{:S(2)}) collective-permute-start(bf16[7,232,128]{2,1,0:T(8,128)(2,1)S(1)} %shard_map.72.own), channel_id=1, source_target_pairs={{0,1},{1,0},{2,3},{3,2},{4,5},{5,4},{6,7},{7,6},{8,9},{9,8},{10,11... | collective-permute-start | bytes 1247240 | tf_op jit(solution)/shard_map/ppermute | solution.py:68
  25.3 2.0 %copy-start.2 = (bf16[1,512,3584]{2,1,0:T(8,128)(2,1)S(1)}, bf16[1,512,3584]{2,1,0:T(8,128)(2,1)}, u32[]{:S(2)}) copy-start(bf16[1,512,3584]{2,1,0:T(8,128)(2,1)} %param.9) | copy-start | bytes 11010052
  28.5 3.5 %collective-permute-start.7 = (bf16[144,1792]{1,0:T(8,128)(2,1)S(1)}, bf16[144,1792]{1,0:T(8,128)(2,1)S(1)}, u32[]{:S(2)}, u32[]{:S(2)}) collective-permute-start(bf16[144,1792]{1,0:T(8,128)(2,1)S(1)} %get-tuple-element.27), channel_id=1, source_target_pairs={{0,1},{1,0},{2,3},{3,2},{4,5},{5,4},{6,7},{7,6},{8,9},{9,8},{10,11... | collective-permute-start | bytes 1548296 | tf_op jit(solution)/shard_map/ppermute | solution.py:68
  30.2 1.8 %collective-permute-start.13 = (bf16[112,1792]{1,0:T(8,128)(2,1)S(1)}, bf16[112,1792]{1,0:T(8,128)(2,1)S(1)}, u32[]{:S(2)}, u32[]{:S(2)}) collective-permute-start(bf16[112,1792]{1,0:T(8,128)(2,1)S(1)} %get-tuple-element.32), channel_id=1, source_target_pairs={{0,1},{1,0},{2,3},{3,2},{4,5},{5,4},{6,7},{7,6},{8,9},{9,8},{10,11... | collective-permute-start | bytes 1204232 | tf_op jit(solution)/shard_map/ppermute | solution.py:68
  32.2 12.3 %collective-permute-start.14 = (bf16[64,1792]{1,0:T(8,128)(2,1)S(1)}, bf16[64,1792]{1,0:T(8,128)(2,1)S(1)}, u32[]{:S(2)}, u32[]{:S(2)}) collective-permute-start(bf16[64,1792]{1,0:T(8,128)(2,1)S(1)} %get-tuple-element.33), channel_id=1, source_target_pairs={{0,8},{8,0},{16,24},{24,16},{1,9},{9,1},{17,25},{25,17},{2,10},{10... | collective-permute-start | bytes 688136 | tf_op jit(solution)/shard_map/ppermute | solution.py:68
  32.8 11.8 %collective-permute-start.15 = (bf16[64,1792]{1,0:T(8,128)(2,1)S(1)}, bf16[64,1792]{1,0:T(8,128)(2,1)S(1)}, u32[]{:S(2)}, u32[]{:S(2)}) collective-permute-start(bf16[64,1792]{1,0:T(8,128)(2,1)S(1)} %get-tuple-element.34), channel_id=1, source_target_pairs={{0,16},{8,24},{16,0},{24,8},{1,17},{9,25},{17,1},{25,9},{2,18},{10... | collective-permute-start | bytes 688136 | tf_op jit(solution)/shard_map/ppermute | solution.py:68
  34.0 6.0 %collective-permute-start.19 = (bf16[16,1792]{1,0:T(8,128)(2,1)S(1)}, bf16[16,1792]{1,0:T(8,128)(2,1)S(1)}, u32[]{:S(2)}, u32[]{:S(2)}) collective-permute-start(bf16[16,1792]{1,0:T(8,128)(2,1)S(1)} %get-tuple-element.38), channel_id=1, source_target_pairs={{0,6},{2,4},{4,2},{6,0},{1,7},{3,5},{5,3},{7,1},{8,14},{10,12},{12... | collective-permute-start | bytes 172040 | tf_op jit(solution)/shard_map/ppermute | solution.py:68
  37.6 5.1 %collective-permute-start.20 = (bf16[16,1792]{1,0:T(8,128)(2,1)S(1)}, bf16[16,1792]{1,0:T(8,128)(2,1)S(1)}, u32[]{:S(2)}, u32[]{:S(2)}) collective-permute-start(bf16[16,1792]{1,0:T(8,128)(2,1)S(1)} %get-tuple-element.39), channel_id=1, source_target_pairs={{0,4},{2,6},{4,0},{6,2},{1,5},{3,7},{5,1},{7,3},{8,12},{10,14},{12... | collective-permute-start | bytes 172040 | tf_op jit(solution)/shard_map/ppermute | solution.py:68
  37.6 5.1 %collective-permute-start.21 = (bf16[16,1792]{1,0:T(8,128)(2,1)S(1)}, bf16[16,1792]{1,0:T(8,128)(2,1)S(1)}, u32[]{:S(2)}, u32[]{:S(2)}) collective-permute-start(bf16[16,1792]{1,0:T(8,128)(2,1)S(1)} %get-tuple-element.40), channel_id=1, source_target_pairs={{0,2},{2,0},{4,6},{6,4},{1,3},{3,1},{5,7},{7,5},{8,10},{10,8},{12,... | collective-permute-start | bytes 172040 | tf_op jit(solution)/shard_map/ppermute | solution.py:68
  42.7 6.4 %collective-permute-start.22 = (bf16[16,1792]{1,0:T(8,128)(2,1)S(1)}, bf16[16,1792]{1,0:T(8,128)(2,1)S(1)}, u32[]{:S(2)}, u32[]{:S(2)}) collective-permute-start(bf16[16,1792]{1,0:T(8,128)(2,1)S(1)} %shard_map.78), channel_id=1, source_target_pairs={{0,24},{8,16},{16,8},{24,0},{1,25},{9,17},{17,9},{25,1},{2,26},{10... | collective-permute-start | bytes 172040 | tf_op jit(solution)/shard_map/ppermute | solution.py:68
  44.6 6.0 %collective-permute-start.16 = (bf16[16,1792]{1,0:T(8,128)(2,1)S(1)}, bf16[16,1792]{1,0:T(8,128)(2,1)S(1)}, u32[]{:S(2)}, u32[]{:S(2)}) collective-permute-start(bf16[16,1792]{1,0:T(8,128)(2,1)S(1)} %get-tuple-element.35), channel_id=1, source_target_pairs={{0,6},{2,4},{4,2},{6,0},{1,7},{3,5},{5,3},{7,1},{8,14},{10,12},{12... | collective-permute-start | bytes 172040 | tf_op jit(solution)/shard_map/ppermute | solution.py:68
  46.7 5.7 %collective-permute-start.17 = (bf16[16,1792]{1,0:T(8,128)(2,1)S(1)}, bf16[16,1792]{1,0:T(8,128)(2,1)S(1)}, u32[]{:S(2)}, u32[]{:S(2)}) collective-permute-start(bf16[16,1792]{1,0:T(8,128)(2,1)S(1)} %get-tuple-element.36), channel_id=1, source_target_pairs={{0,4},{2,6},{4,0},{6,2},{1,5},{3,7},{5,1},{7,3},{8,12},{10,14},{12... | collective-permute-start | bytes 172040 | tf_op jit(solution)/shard_map/ppermute | solution.py:68
  46.9 5.4 %collective-permute-start.18 = (bf16[16,1792]{1,0:T(8,128)(2,1)S(1)}, bf16[16,1792]{1,0:T(8,128)(2,1)S(1)}, u32[]{:S(2)}, u32[]{:S(2)}) collective-permute-start(bf16[16,1792]{1,0:T(8,128)(2,1)S(1)} %get-tuple-element.37), channel_id=1, source_target_pairs={{0,2},{2,0},{4,6},{6,4},{1,3},{3,1},{5,7},{7,5},{8,10},{10,8},{12,... | collective-permute-start | bytes 172040 | tf_op jit(solution)/shard_map/ppermute | solution.py:68

commit v5 on v4

--- a/solution.py
+++ b/solution.py
@@ -161,12 +161,17 @@
         out[...] = dot(x[...], weight[at, :])
 
 
-def leave(at, scale, hidden, down, out):
-    out[...] = (dot(hidden[...], down[:, at]) * scale[:, :1]).astype(BF16)
-
-
-def enter_other(other, gate, up, down, gated, lifted, scale, hidden, send, x):
-    width = send.shape[1]
+def leave(at, scale, hidden, down, outs):
+    value = dot(hidden[...], down[:, at]) * scale[:, :1]
+    start = 0
+    for out in outs:
+        out[...] = value[start : start + out.shape[0]].astype(BF16)
+        start += out.shape[0]
+
+
+def enter_other(other, gate, up, down, gated, lifted, scale, hidden, *refs):
+    send, x = refs[:-1], refs[-1]
+    width = x.shape[1]
     unpack(other, x)
     at = half_rows(width, False)
     for i in range(0, hidden.shape[1], TILE):
@@ -178,7 +183,7 @@
 
 
 def leave_own(hidden, down, scale, keep):
-    leave(half_rows(keep.shape[1], True), scale, hidden, down, keep)
+    leave(half_rows(keep.shape[1], True), scale, hidden, down, [keep])
 
 
 def dense(tokens, gate_weight, up_weight, down_weight, expert_ids, gate_codes):
@@ -210,7 +215,7 @@
     far = stack([sent_b[g] for g in range(1, dp)] + [turned])
     gate, up, down = gate_weight[0], up_weight[0], down_weight[0]
 
-    def run(own):
+    def run(own, cuts):
         count = own.shape[0] * n
         scratch = [pltpu.VMEM((count, width), BF16)]
         floats = jax.ShapeDtypeStruct((count, units), F32)
@@ -219,32 +224,34 @@
             functools.partial(enter_own, owners), [floats, floats, jax.ShapeDtypeStruct((count, LANES), F32)],
             own, gate, up, flops=HINT, limit=8, scratch=scratch,
         )
-        hidden, send = call(
-            enter_other, [jax.ShapeDtypeStruct((count, units), BF16), block(count)],
+        hidden, *send = call(
+            enter_other, [jax.ShapeDtypeStruct((count, units), BF16)] + [block(part) for part in cuts],
             other, gate, up, down, gated, lifted, scale, flops=HINT, limit=8, scratch=scratch,
         )
         keep = call(leave_own, block(count), hidden, down, scale, flops=HINT, limit=8)
         return keep, send
 
-    keep_a, send_a = run(near)
-    keep_b, send_b = run(far)
+    sums = 2 * (ex - EARLY) * n
+    keep_a, (send_a,) = run(near, [near.shape[0] * n])
+    keep_b, (send_b, send_d) = run(far, [sums, far.shape[0] * n - sums])
     recv_a = swap(send_a, "tensor", 1)
     recv_b = swap(send_b, "tensor", 1)
+    recv_d = swap(send_d, "tensor", 1)
     cut = EARLY * n
 
-    def add_far(keep_a, recv_a, keep_b, recv_b, x, y, *diag):
+    def add_far(keep_a, recv_a, keep_b, recv_b, x, y):
         for g, out in ((1, x), (2, y)):
             here, there = pl.ds(rows + (g - 1) * cut, cut), pl.ds((g - 1) * (rows - cut), rows - cut)
             out[:cut, :] = plus(keep_a[here, :], recv_a[here, :]).astype(BF16)
             out[cut:, :] = plus(keep_b[there, :], recv_b[there, :]).astype(BF16)
+
+    def add_turned(keep_b, recv_d, *diag):
         for j, out in zip(hops, diag):
-            if j < EARLY:
-                keep, recv, here = keep_b, recv_b, pl.ds((dp - 1) * (rows - cut) + (j - 1) * n, n)
-            else:
-                keep, recv, here = keep_b, recv_b, pl.ds(2 * (rows - cut) + (j - EARLY) * n, n)
-            out[...] = plus(keep[here, :], recv[here, :]).astype(BF16)
-
-    x, y, *diag = call(add_far, [block(rows)] * 2 + [block(n)] * (ex - 1), keep_a, recv_a, keep_b, recv_b)
+            start = (j - EARLY) * n if j >= EARLY else rows - cut + (j - 1) * n
+            out[...] = plus(keep_b[pl.ds(sums + start, n), :], recv_d[pl.ds(start, n), :]).astype(BF16)
+
+    x, y = call(add_far, [block(rows)] * 2, keep_a, recv_a, keep_b, recv_b)
+    diag = call(add_turned, [block(n)] * (ex - 1), keep_b, recv_d)
     sides = [swap(x, "dp", 1), swap(y, "dp", 2)]
     spread = [swap(diag[j - 1], "expert", j) for j in reversed(hops)]
 

time: 53.2 us -> 53.1 us (level)
  waiting for transfers between devices: 18 us -> 17.3 us
  starting transfers between devices: 26.7 us -> 27.3 us
    ppermute x23 -> x24, waiting for transfers between devices: 18 us -> 17.3 us  [swap(): return lax.ppermute(x, axis, [(i, i ^ offset) for i in range(count)])]
    ppermute x23 -> x24, starting transfers between devices: 26.7 us -> 27.3 us  [swap(): return lax.ppermute(x, axis, [(i, i ^ offset) for i in range(count)])]
    pallas_call x16 -> x17, Pallas kernels: 6.01 us -> 6.01 us  [call(): pl.pallas_call(body, out_shape=outs, in_specs=[VMEM] * len(args), out_spe...]
  transfers between devices with their start and end apart: 23 -> 24, of which waited for: 11 -> 10; matrix products, arithmetic and copies ran while one was open for 0% -> 0% of each run, Pallas kernels for 9% -> 9%
where the time goes in v5:
time: 53.1 us; the launch traced here: 52.9 us
  starting transfers between devices  27.3 us (51%)
  waiting for transfers between devices  17.3 us (33%)
  Pallas kernels  6.01 us (11%)
  local copies, waits for them, and re-layouts  2.12 us (4%)
    ppermute x24, starting transfers between devices, swap(): return lax.ppermute(x, axis, [(i, i ^ offset) for i in range(count)])  27.3 us
    ppermute x24, waiting for transfers between devices, swap(): return lax.ppermute(x, axis, [(i, i ^ offset) for i in range(count)])  17.3 us
    pallas_call x17, Pallas kernels, call(): pl.pallas_call(body, out_shape=outs, in_specs=[VMEM] * len(args), out_spe...  6.01 us
    unnamed x12, local copies, waits for them, and re-layouts  2.12 us
  transfers between devices with their start and end apart: 24, of which 10 were waited for; matrix products, arithmetic and copies ran while one was open for 0% of the time, Pallas kernels for 9%

profile of v5, /device:TPU:0, one launch (start us, length us, event | category | flops | bytes accessed | tf_op | source)
XLA Modules:
  0.0 52.9 jit_solution(6066663494202638158)
XLA Ops:
  0.0 0.8 %copy-done.3 = bf16[1,16,1792]{2,1,0:T(8,128)(2,1)S(1)} copy-done((bf16[1,16,1792]{2,1,0:T(8,128)(2,1)S(1)}, bf16[1,16,1792]{2,1,0:T(8,128)(2,1)}, u32[]{:S(2)}) %copy-start.3) | copy-done | bytes 57368
  0.8 0.0 copy-done.4
  0.8 0.3 shard_map.65.refs_0_
  1.1 3.1 %collective-permute-start = (bf16[1,232,128]{2,1,0:T(8,128)(2,1)S(1)}, bf16[1,232,128]{2,1,0:T(8,128)(2,1)S(1)}, u32[]{:S(2)}, u32[]{:S(2)}) collective-permute-start(bf16[1,232,128]{2,1,0:T(8,128)(2,1)S(1)} %shard_map.65.refs_0_), channel_id=1, source_target_pairs={{0,2},{2,0},{4,6},{6,4},{1,3},{3,1},{5,7},{7,5},{8,10},{10,8},{12,... | collective-permute-start | bytes 178184 | tf_op jit(solution)/shard_map/ppermute | solution.py:68
  4.2 2.6 %collective-permute-start.1 = (bf16[1,232,128]{2,1,0:T(8,128)(2,1)S(1)}, bf16[1,232,128]{2,1,0:T(8,128)(2,1)S(1)}, u32[]{:S(2)}, u32[]{:S(2)}) collective-permute-start(bf16[1,232,128]{2,1,0:T(8,128)(2,1)S(1)} %shard_map.65.refs_0_), channel_id=1, source_target_pairs={{0,4},{2,6},{4,0},{6,2},{1,5},{3,7},{5,1},{7,3},{8,12},{10,14},{12... | collective-permute-start | bytes 178184 | tf_op jit(solution)/shard_map/ppermute | solution.py:68
  6.8 0.0 collective-permute-start.2
  6.8 2.7 %collective-permute-start.5 = (bf16[1,232,128]{2,1,0:T(8,128)(2,1)S(1)}, bf16[1,232,128]{2,1,0:T(8,128)(2,1)S(1)}, u32[]{:S(2)}, u32[]{:S(2)}) collective-permute-start(bf16[1,232,128]{2,1,0:T(8,128)(2,1)S(1)} %shard_map.65.refs_0_), channel_id=1, source_target_pairs={{0,24},{8,16},{16,8},{24,0},{1,25},{9,17},{17,9},{25,1},{2,26},{10... | collective-permute-start | bytes 178184 | tf_op jit(solution)/shard_map/ppermute | solution.py:68
  9.5 0.0 collective-permute-done.refs_1_
  9.5 0.0 copy-start
  9.5 0.0 copy-start.1
  9.5 0.6 %collective-permute-start.3 = (bf16[2,232,128]{2,1,0:T(8,128)(2,1)S(1)}, bf16[2,232,128]{2,1,0:T(8,128)(2,1)S(1)}, u32[]{:S(2)}, u32[]{:S(2)}) collective-permute-start(bf16[2,232,128]{2,1,0:T(8,128)(2,1)S(1)} %shard_map.66.refs_0_), channel_id=1, source_target_pairs={{0,8},{8,0},{16,24},{24,16},{1,9},{9,1},{17,25},{25,17},{2,10},{10... | collective-permute-start | bytes 356360 | tf_op jit(solution)/shard_map/ppermute | solution.py:68
  10.1 0.3 collective-permute-start.4
  10.4 0.1 collective-permute-done.1.refs_0_
  10.5 2.3 %collective-permute-done.2.refs_1_ = bf16[1,232,128]{2,1,0:T(8,128)(2,1)S(1)} collective-permute-done((bf16[1,232,128]{2,1,0:T(8,128)(2,1)S(1)}, bf16[1,232,128]{2,1,0:T(8,128)(2,1)S(1)}, u32[]{:S(2)}, u32[]{:S(2)}) %collective-permute-start.2) | collective-permute-done | bytes 59424 | tf_op jit(solution)/shard_map/ppermute | solution.py:68
  12.8 0.0 collective-permute-done.5.refs_4_
  12.8 1.6 %collective-permute-done.3.refs_2_ = bf16[2,232,128]{2,1,0:T(8,128)(2,1)S(1)} collective-permute-done((bf16[2,232,128]{2,1,0:T(8,128)(2,1)S(1)}, bf16[2,232,128]{2,1,0:T(8,128)(2,1)S(1)}, u32[]{:S(2)}, u32[]{:S(2)}) %collective-permute-start.3) | collective-permute-done | bytes 118816 | tf_op jit(solution)/shard_map/ppermute | solution.py:68
  14.4 0.5 %collective-permute-done.4.refs_3_ = bf16[2,232,128]{2,1,0:T(8,128)(2,1)S(1)} collective-permute-done((bf16[2,232,128]{2,1,0:T(8,128)(2,1)S(1)}, bf16[2,232,128]{2,1,0:T(8,128)(2,1)S(1)}, u32[]{:S(2)}, u32[]{:S(2)}) %collective-permute-start.4) | collective-permute-done | bytes 118816 | tf_op jit(solution)/shard_map/ppermute | solution.py:68
  15.0 0.1 collective-permute-start.6
  15.1 1.6 %collective-permute-start.8 = (bf16[2,232,128]{2,1,0:T(8,128)(2,1)S(1)}, bf16[2,232,128]{2,1,0:T(8,128)(2,1)S(1)}, u32[]{:S(2)}, u32[]{:S(2)}) collective-permute-start(bf16[2,232,128]{2,1,0:T(8,128)(2,1)S(1)} %shard_map.67.refs_1_), channel_id=1, source_target_pairs={{0,8},{8,0},{16,24},{24,16},{1,9},{9,1},{17,25},{25,17},{2,10},{10... | collective-permute-start | bytes 356360 | tf_op jit(solution)/shard_map/ppermute | solution.py:68
  16.6 0.5 collective-permute-start.9
  17.1 1.5 %collective-permute-start.10 = (bf16[2,232,128]{2,1,0:T(8,128)(2,1)S(1)}, bf16[2,232,128]{2,1,0:T(8,128)(2,1)S(1)}, u32[]{:S(2)}, u32[]{:S(2)}) collective-permute-start(bf16[2,232,128]{2,1,0:T(8,128)(2,1)S(1)} %shard_map.67.refs_1_), channel_id=1, source_target_pairs={{0,24},{8,16},{16,8},{24,0},{1,25},{9,17},{17,9},{25,1},{2,26},{10... | collective-permute-start | bytes 356360 | tf_op jit(solution)/shard_map/ppermute | solution.py:68
  18.6 0.7 %collective-permute-start.11 = (bf16[1,232,128]{2,1,0:T(8,128)(2,1)S(1)}, bf16[1,232,128]{2,1,0:T(8,128)(2,1)S(1)}, u32[]{:S(2)}, u32[]{:S(2)}) collective-permute-start(bf16[1,232,128]{2,1,0:T(8,128)(2,1)S(1)} %collective-permute-done.5.refs_4_), channel_id=1, source_target_pairs={{0,2},{2,0},{4,6},{6,4},{1,3},{3,1},{5,7},{7,5},{8,10},{10,8},{12,... | collective-permute-start | bytes 178184 | tf_op jit(solution)/shard_map/ppermute | solution.py:68
  19.3 3.5 %collective-permute-done.11.refs_3_ = bf16[1,232,128]{2,1,0:T(8,128)(2,1)S(1)} collective-permute-done((bf16[1,232,128]{2,1,0:T(8,128)(2,1)S(1)}, bf16[1,232,128]{2,1,0:T(8,128)(2,1)S(1)}, u32[]{:S(2)}, u32[]{:S(2)}) %collective-permute-start.11) | collective-permute-done | bytes 59424 | tf_op jit(solution)/shard_map/ppermute | solution.py:68
  22.8 0.0 collective-permute-done.8.refs_0_
  22.8 1.6 %collective-permute-done.9.refs_1_ = bf16[2,232,128]{2,1,0:T(8,128)(2,1)S(1)} collective-permute-done((bf16[2,232,128]{2,1,0:T(8,128)(2,1)S(1)}, bf16[2,232,128]{2,1,0:T(8,128)(2,1)S(1)}, u32[]{:S(2)}, u32[]{:S(2)}) %collective-permute-start.9) | collective-permute-done | bytes 118816 | tf_op jit(solution)/shard_map/ppermute | solution.py:68
  24.4 0.0 collective-permute-done.10.refs_2_
  24.5 0.1 collective-permute-start.12
  24.6 0.7 %shard_map.69 = (f32[144,512]{1,0:T(8,128)S(1)}, f32[144,512]{1,0:T(8,128)S(1)}, f32[144,128]{1,0:T(8,128)S(1)}) custom-call(bf16[9,232,128]{2,1,0:T(8,128)(2,1)S(1)} %shard_map.68.own, bf16[3584,512]{1,0:T(8,128)(2,1)S(1)} %bitcast.11, bf16[3584,512]{1,0:T(8,128)(2,1)S(1)} %bitcast.15), custom_call_target="tpu_custom_call" | custom-call | flops 2000000000 | tf_op jit(solution)/shard_map/pallas_call | solution.py:76
  25.3 0.0 copy-start.2
  25.3 0.7 %shard_map.73 = (f32[112,512]{1,0:T(8,128)S(1)}, f32[112,512]{1,0:T(8,128)S(1)}, f32[112,128]{1,0:T(8,128)S(1)}) custom-call(bf16[7,232,128]{2,1,0:T(8,128)(2,1)S(1)} %shard_map.72.own, bf16[3584,512]{1,0:T(8,128)(2,1)S(1)} %bitcast.12, bf16[3584,512]{1,0:T(8,128)(2,1)S(1)} %bitcast.16), custom_call_target="tpu_custom_call" | custom-call | flops 2000000000 | tf_op jit(solution)/shard_map/pallas_call | solution.py:76
  26.1 0.0 collective-permute-done.6.other
  26.1 1.3 %copy-done.2 = bf16[1,512,3584]{2,1,0:T(8,128)(2,1)S(1)} copy-done((bf16[1,512,3584]{2,1,0:T(8,128)(2,1)S(1)}, bf16[1,512,3584]{2,1,0:T(8,128)(2,1)}, u32[]{:S(2)}) %copy-start.2) | copy-done | bytes 3670040
  27.4 1.2 %shard_map.70 = (bf16[144,512]{1,0:T(8,128)(2,1)S(1)}, bf16[144,1792]{1,0:T(8,128)(2,1)S(1)}) custom-call(bf16[9,232,128]{2,1,0:T(8,128)(2,1)S(1)} %collective-permute-done.6.other, bf16[3584,512]{1,0:T(8,128)(2,1)S(1)} %bitcast.13, bf16[3584,512]{1,0:T(8,128)(2,1)S(1)} %bitcast.17, bf16[512,3584]{1,0:T(8,128)(2,1)S(1)} %bitcast.19, ...), custom_call_target="tpu_custom_call" | custom-call | flops 2000000000 | tf_op jit(solution)/shard_map/pallas_call | solution.py:76
  28.5 0.6 %collective-permute-start.7 = (bf16[144,1792]{1,0:T(8,128)(2,1)S(1)}, bf16[144,1792]{1,0:T(8,128)(2,1)S(1)}, u32[]{:S(2)}, u32[]{:S(2)}) collective-permute-start(bf16[144,1792]{1,0:T(8,128)(2,1)S(1)} %get-tuple-element.28), channel_id=1, source_target_pairs={{0,1},{1,0},{2,3},{3,2},{4,5},{5,4},{6,7},{7,6},{8,9},{9,8},{10,11... | collective-permute-start | bytes 1548296 | tf_op jit(solution)/shard_map/ppermute | solution.py:68
  29.1 0.0 collective-permute-done.12.other
  29.1 1.1 %shard_map.74 = (bf16[112,512]{1,0:T(8,128)(2,1)S(1)}, bf16[64,1792]{1,0:T(8,128)(2,1)S(1)}, bf16[48,1792]{1,0:T(8,128)(2,1)S(1)}) custom-call(bf16[7,232,128]{2,1,0:T(8,128)(2,1)S(1)} %collective-permute-done.12.other, bf16[3584,512]{1,0:T(8,128)(2,1)S(1)} %bitcast.14, bf16[3584,512]{1,0:T(8,128)(2,1)S(1)} %bitcast.18, bf16[512,3584]{1,0:T(8,128)(2,1)S(1)} %bitcast.20, ...), custom_call_target="tpu_custom_call" | custom-call | flops 2000000000 | tf_op jit(solution)/shard_map/pallas_call | solution.py:76
  30.2 0.1 collective-permute-start.13
  30.3 0.4 shard_map.75.keep_b
  30.8 0.5 %collective-permute-start.19 = (bf16[48,1792]{1,0:T(8,128)(2,1)S(1)}, bf16[48,1792]{1,0:T(8,128)(2,1)S(1)}, u32[]{:S(2)}, u32[]{:S(2)}) collective-permute-start(bf16[48,1792]{1,0:T(8,128)(2,1)S(1)} %get-tuple-element.39), channel_id=1, source_target_pairs={{0,1},{1,0},{2,3},{3,2},{4,5},{5,4},{6,7},{7,6},{8,9},{9,8},{10,11... | collective-permute-start | bytes 516104 | tf_op jit(solution)/shard_map/ppermute | solution.py:68
  31.3 0.5 shard_map.71.keep_a.keep
  31.8 0.0 collective-permute-done.13.recv_b
  31.8 0.0 collective-permute-done.7.recv_a.recv
  31.8 0.1 shard_map.76
  31.9 0.6 %collective-permute-start.14 = (bf16[64,1792]{1,0:T(8,128)(2,1)S(1)}, bf16[64,1792]{1,0:T(8,128)(2,1)S(1)}, u32[]{:S(2)}, u32[]{:S(2)}) collective-permute-start(bf16[64,1792]{1,0:T(8,128)(2,1)S(1)} %get-tuple-element.34), channel_id=1, source_target_pairs={{0,8},{8,0},{16,24},{24,16},{1,9},{9,1},{17,25},{25,17},{2,10},{10... | collective-permute-start | bytes 688136 | tf_op jit(solution)/shard_map/ppermute | solution.py:68
  32.5 1.2 %collective-permute-start.15 = (bf16[64,1792]{1,0:T(8,128)(2,1)S(1)}, bf16[64,1792]{1,0:T(8,128)(2,1)S(1)}, u32[]{:S(2)}, u32[]{:S(2)}) collective-permute-start(bf16[64,1792]{1,0:T(8,128)(2,1)S(1)} %get-tuple-element.35), channel_id=1, source_target_pairs={{0,16},{8,24},{16,0},{24,8},{1,17},{9,25},{17,1},{25,9},{2,18},{10... | collective-permute-start | bytes 688136 | tf_op jit(solution)/shard_map/ppermute | solution.py:68
  33.7 0.0 collective-permute-done.19.recv_d
  33.8 3.6 %collective-permute-start.20 = (bf16[16,1792]{1,0:T(8,128)(2,1)S(1)}, bf16[16,1792]{1,0:T(8,128)(2,1)S(1)}, u32[]{:S(2)}, u32[]{:S(2)}) collective-permute-start(bf16[16,1792]{1,0:T(8,128)(2,1)S(1)} %get-tuple-element.40), channel_id=1, source_target_pairs={{0,6},{2,4},{4,2},{6,0},{1,7},{3,5},{5,3},{7,1},{8,14},{10,12},{12... | collective-permute-start | bytes 172040 | tf_op jit(solution)/shard_map/ppermute | solution.py:68
  37.4 0.0 collective-permute-start.21
  37.4 0.8 %collective-permute-start.22 = (bf16[16,1792]{1,0:T(8,128)(2,1)S(1)}, bf16[16,1792]{1,0:T(8,128)(2,1)S(1)}, u32[]{:S(2)}, u32[]{:S(2)}) collective-permute-start(bf16[16,1792]{1,0:T(8,128)(2,1)S(1)} %get-tuple-element.42), channel_id=1, source_target_pairs={{0,2},{2,0},{4,6},{6,4},{1,3},{3,1},{5,7},{7,5},{8,10},{10,8},{12,... | collective-permute-start | bytes 172040 | tf_op jit(solution)/shard_map/ppermute | solution.py:68
  38.2 1.6 %collective-permute-done.20.rest_0_ = bf16[16,1792]{1,0:T(8,128)(2,1)S(1)} collective-permute-done((bf16[16,1792]{1,0:T(8,128)(2,1)S(1)}, bf16[16,1792]{1,0:T(8,128)(2,1)S(1)}, u32[]{:S(2)}, u32[]{:S(2)}) %collective-permute-start.20) | collective-permute-done | bytes 57376 | tf_op jit(solution)/shard_map/ppermute | solution.py:68
  39.9 2.6 %collective-permute-done.21.rest_1_ = bf16[16,1792]{1,0:T(8,128)(2,1)S(1)} collective-permute-done((bf16[16,1792]{1,0:T(8,128)(2,1)S(1)}, bf16[16,1792]{1,0:T(8,128)(2,1)S(1)}, u32[]{:S(2)}, u32[]{:S(2)}) %collective-permute-start.21) | collective-permute-done | bytes 57376 | tf_op jit(solution)/shard_map/ppermute | solution.py:68
  42.5 0.0 collective-permute-done.22.rest_2_
  42.5 1.8 %collective-permute-start.23 = (bf16[16,1792]{1,0:T(8,128)(2,1)S(1)}, bf16[16,1792]{1,0:T(8,128)(2,1)S(1)}, u32[]{:S(2)}, u32[]{:S(2)}) collective-permute-start(bf16[16,1792]{1,0:T(8,128)(2,1)S(1)} %shard_map.79), channel_id=1, source_target_pairs={{0,24},{8,16},{16,8},{24,0},{1,25},{9,17},{17,9},{25,1},{2,26},{10... | collective-permute-start | bytes 172040 | tf_op jit(solution)/shard_map/ppermute | solution.py:68
  44.4 0.0 collective-permute-done.14.x
  44.4 0.0 collective-permute-done.15.y
  44.4 0.1 shard_map.77
  44.5 2.0 %collective-permute-start.16 = (bf16[16,1792]{1,0:T(8,128)(2,1)S(1)}, bf16[16,1792]{1,0:T(8,128)(2,1)S(1)}, u32[]{:S(2)}, u32[]{:S(2)}) collective-permute-start(bf16[16,1792]{1,0:T(8,128)(2,1)S(1)} %get-tuple-element.36), channel_id=1, source_target_pairs={{0,6},{2,4},{4,2},{6,0},{1,7},{3,5},{5,3},{7,1},{8,14},{10,12},{12... | collective-permute-start | bytes 172040 | tf_op jit(solution)/shard_map/ppermute | solution.py:68
  46.5 0.3 collective-permute-start.17
  46.8 2.2 %collective-permute-start.18 = (bf16[16,1792]{1,0:T(8,128)(2,1)S(1)}, bf16[16,1792]{1,0:T(8,128)(2,1)S(1)}, u32[]{:S(2)}, u32[]{:S(2)}) collective-permute-start(bf16[16,1792]{1,0:T(8,128)(2,1)S(1)} %get-tuple-element.38), channel_id=1, source_target_pairs={{0,2},{2,0},{4,6},{6,4},{1,3},{3,1},{5,7},{7,5},{8,10},{10,8},{12,... | collective-permute-start | bytes 172040 | tf_op jit(solution)/shard_map/ppermute | solution.py:68
  48.9 0.0 collective-permute-done.23.rest_3_
  48.9 1.6 %collective-permute-done.16.rest_0_ = bf16[16,1792]{1,0:T(8,128)(2,1)S(1)} collective-permute-done((bf16[16,1792]{1,0:T(8,128)(2,1)S(1)}, bf16[16,1792]{1,0:T(8,128)(2,1)S(1)}, u32[]{:S(2)}, u32[]{:S(2)}) %collective-permute-start.16) | collective-permute-done | bytes 57376 | tf_op jit(solution)/shard_map/ppermute | solution.py:68
  50.5 1.7 %collective-permute-done.17.rest_1_ = bf16[16,1792]{1,0:T(8,128)(2,1)S(1)} collective-permute-done((bf16[16,1792]{1,0:T(8,128)(2,1)S(1)}, bf16[16,1792]{1,0:T(8,128)(2,1)S(1)}, u32[]{:S(2)}, u32[]{:S(2)}) %collective-permute-start.17) | collective-permute-done | bytes 57376 | tf_op jit(solution)/shard_map/ppermute | solution.py:68
  52.2 0.0 collective-permute-done.18.rest_2_
  52.2 0.7 %shard_map.80 = bf16[16,1792]{1,0:T(8,128)(2,1)} custom-call(bf16[144,1792]{1,0:T(8,128)(2,1)S(1)} %shard_map.71.keep_a.keep, bf16[144,1792]{1,0:T(8,128)(2,1)S(1)} %collective-permute-done.7.recv_a.recv, bf16[64,1792]{1,0:T(8,128)(2,1)S(1)} %collective-permute-done.14.x, bf16[64,1792]{1,0:T(8,128)(2,1)S(1)} %collective-permute-done.15.y, ...), custom_call_target="tpu_custom_call" | custom-call | tf_op jit(solution)/shard_map/pallas_call | solution.py:76
  (13 shorter events, 0.2 us)
Async XLA Ops:
  0.0 0.8 %copy-start.3 = (bf16[1,16,1792]{2,1,0:T(8,128)(2,1)S(1)}, bf16[1,16,1792]{2,1,0:T(8,128)(2,1)}, u32[]{:S(2)}) copy-start(bf16[1,16,1792]{2,1,0:T(8,128)(2,1)} %param.6) | copy-start | bytes 172036
  0.0 0.8 %copy-start.4 = (s32[1,16,8]{1,2,0:T(8,128)S(1)}, s32[1,16,8]{1,2,0:T(8,128)}, u32[]{:S(2)}) copy-start(s32[1,16,8]{1,2,0:T(8,128)} %param.10) | copy-start | bytes 1540
  0.0 0.8 %copy-start.5 = (s32[1,16,8]{1,2,0:T(8,128)S(1)}, s32[1,16,8]{1,2,0:T(8,128)}, u32[]{:S(2)}) copy-start(s32[1,16,8]{1,2,0:T(8,128)} %param.11) | copy-start | bytes 1540
  1.1 8.3 %collective-permute-start = (bf16[1,232,128]{2,1,0:T(8,128)(2,1)S(1)}, bf16[1,232,128]{2,1,0:T(8,128)(2,1)S(1)}, u32[]{:S(2)}, u32[]{:S(2)}) collective-permute-start(bf16[1,232,128]{2,1,0:T(8,128)(2,1)S(1)} %shard_map.65.refs_0_), channel_id=1, source_target_pairs={{0,2},{2,0},{4,6},{6,4},{1,3},{3,1},{5,7},{7,5},{8,10},{10,8},{12,... | collective-permute-start | bytes 178184 | tf_op jit(solution)/shard_map/ppermute | solution.py:68
  4.2 6.3 %collective-permute-start.1 = (bf16[1,232,128]{2,1,0:T(8,128)(2,1)S(1)}, bf16[1,232,128]{2,1,0:T(8,128)(2,1)S(1)}, u32[]{:S(2)}, u32[]{:S(2)}) collective-permute-start(bf16[1,232,128]{2,1,0:T(8,128)(2,1)S(1)} %shard_map.65.refs_0_), channel_id=1, source_target_pairs={{0,4},{2,6},{4,0},{6,2},{1,5},{3,7},{5,1},{7,3},{8,12},{10,14},{12... | collective-permute-start | bytes 178184 | tf_op jit(solution)/shard_map/ppermute | solution.py:68
  6.8 6.0 %collective-permute-start.2 = (bf16[1,232,128]{2,1,0:T(8,128)(2,1)S(1)}, bf16[1,232,128]{2,1,0:T(8,128)(2,1)S(1)}, u32[]{:S(2)}, u32[]{:S(2)}) collective-permute-start(bf16[1,232,128]{2,1,0:T(8,128)(2,1)S(1)} %shard_map.65.refs_0_), channel_id=1, source_target_pairs={{0,6},{2,4},{4,2},{6,0},{1,7},{3,5},{5,3},{7,1},{8,14},{10,12},{12... | collective-permute-start | bytes 178184 | tf_op jit(solution)/shard_map/ppermute | solution.py:68
  6.8 6.0 %collective-permute-start.5 = (bf16[1,232,128]{2,1,0:T(8,128)(2,1)S(1)}, bf16[1,232,128]{2,1,0:T(8,128)(2,1)S(1)}, u32[]{:S(2)}, u32[]{:S(2)}) collective-permute-start(bf16[1,232,128]{2,1,0:T(8,128)(2,1)S(1)} %shard_map.65.refs_0_), channel_id=1, source_target_pairs={{0,24},{8,16},{16,8},{24,0},{1,25},{9,17},{17,9},{25,1},{2,26},{10... | collective-permute-start | bytes 178184 | tf_op jit(solution)/shard_map/ppermute | solution.py:68
  9.5 15.1 %copy-start = (bf16[1,3584,512]{2,1,0:T(8,128)(2,1)S(1)}, bf16[1,3584,512]{2,1,0:T(8,128)(2,1)}, u32[]{:S(2)}) copy-start(bf16[1,3584,512]{2,1,0:T(8,128)(2,1)} %param.7) | copy-start | bytes 11010052
  9.5 15.1 %copy-start.1 = (bf16[1,3584,512]{2,1,0:T(8,128)(2,1)S(1)}, bf16[1,3584,512]{2,1,0:T(8,128)(2,1)}, u32[]{:S(2)}) copy-start(bf16[1,3584,512]{2,1,0:T(8,128)(2,1)} %param.8) | copy-start | bytes 11010052
  9.5 4.9 %collective-permute-start.3 = (bf16[2,232,128]{2,1,0:T(8,128)(2,1)S(1)}, bf16[2,232,128]{2,1,0:T(8,128)(2,1)S(1)}, u32[]{:S(2)}, u32[]{:S(2)}) collective-permute-start(bf16[2,232,128]{2,1,0:T(8,128)(2,1)S(1)} %shard_map.66.refs_0_), channel_id=1, source_target_pairs={{0,8},{8,0},{16,24},{24,16},{1,9},{9,1},{17,25},{25,17},{2,10},{10... | collective-permute-start | bytes 356360 | tf_op jit(solution)/shard_map/ppermute | solution.py:68
  10.1 4.8 %collective-permute-start.4 = (bf16[2,232,128]{2,1,0:T(8,128)(2,1)S(1)}, bf16[2,232,128]{2,1,0:T(8,128)(2,1)S(1)}, u32[]{:S(2)}, u32[]{:S(2)}) collective-permute-start(bf16[2,232,128]{2,1,0:T(8,128)(2,1)S(1)} %shard_map.66.refs_0_), channel_id=1, source_target_pairs={{0,16},{8,24},{16,0},{24,8},{1,17},{9,25},{17,1},{25,9},{2,18},{10... | collective-permute-start | bytes 356360 | tf_op jit(solution)/shard_map/ppermute | solution.py:68
  15.0 11.1 %collective-permute-start.6 = (bf16[9,232,128]{2,1,0:T(8,128)(2,1)S(1)}, bf16[9,232,128]{2,1,0:T(8,128)(2,1)S(1)}, u32[]{:S(2)}, u32[]{:S(2)}) collective-permute-start(bf16[9,232,128]{2,1,0:T(8,128)(2,1)S(1)} %shard_map.68.own), channel_id=1, source_target_pairs={{0,1},{1,0},{2,3},{3,2},{4,5},{5,4},{6,7},{7,6},{8,9},{9,8},{10,11... | collective-permute-start | bytes 1603592 | tf_op jit(solution)/shard_map/ppermute | solution.py:68
  15.1 7.8 %collective-permute-start.8 = (bf16[2,232,128]{2,1,0:T(8,128)(2,1)S(1)}, bf16[2,232,128]{2,1,0:T(8,128)(2,1)S(1)}, u32[]{:S(2)}, u32[]{:S(2)}) collective-permute-start(bf16[2,232,128]{2,1,0:T(8,128)(2,1)S(1)} %shard_map.67.refs_1_), channel_id=1, source_target_pairs={{0,8},{8,0},{16,24},{24,16},{1,9},{9,1},{17,25},{25,17},{2,10},{10... | collective-permute-start | bytes 356360 | tf_op jit(solution)/shard_map/ppermute | solution.py:68
  16.6 7.8 %collective-permute-start.9 = (bf16[2,232,128]{2,1,0:T(8,128)(2,1)S(1)}, bf16[2,232,128]{2,1,0:T(8,128)(2,1)S(1)}, u32[]{:S(2)}, u32[]{:S(2)}) collective-permute-start(bf16[2,232,128]{2,1,0:T(8,128)(2,1)S(1)} %shard_map.67.refs_1_), channel_id=1, source_target_pairs={{0,16},{8,24},{16,0},{24,8},{1,17},{9,25},{17,1},{25,9},{2,18},{10... | collective-permute-start | bytes 356360 | tf_op jit(solution)/shard_map/ppermute | solution.py:68
  17.1 7.3 %collective-permute-start.10 = (bf16[2,232,128]{2,1,0:T(8,128)(2,1)S(1)}, bf16[2,232,128]{2,1,0:T(8,128)(2,1)S(1)}, u32[]{:S(2)}, u32[]{:S(2)}) collective-permute-start(bf16[2,232,128]{2,1,0:T(8,128)(2,1)S(1)} %shard_map.67.refs_1_), channel_id=1, source_target_pairs={{0,24},{8,16},{16,8},{24,0},{1,25},{9,17},{17,9},{25,1},{2,26},{10... | collective-permute-start | bytes 356360 | tf_op jit(solution)/shard_map/ppermute | solution.py:68
  18.6 4.2 %collective-permute-start.11 = (bf16[1,232,128]{2,1,0:T(8,128)(2,1)S(1)}, bf16[1,232,128]{2,1,0:T(8,128)(2,1)S(1)}, u32[]{:S(2)}, u32[]{:S(2)}) collective-permute-start(bf16[1,232,128]{2,1,0:T(8,128)(2,1)S(1)} %collective-permute-done.5.refs_4_), channel_id=1, source_target_pairs={{0,2},{2,0},{4,6},{6,4},{1,3},{3,1},{5,7},{7,5},{8,10},{10,8},{12,... | collective-permute-start | bytes 178184 | tf_op jit(solution)/shard_map/ppermute | solution.py:68
  24.5 4.6 %collective-permute-start.12 = (bf16[7,232,128]{2,1,0:T(8,128)(2,1)S(1)}, bf16[7,232,128]{2,1,0:T(8,128)(2,1)S(1)}, u32[]{:S(2)}, u32[]{:S(2)}) collective-permute-start(bf16[7,232,128]{2,1,0:T(8,128)(2,1)S(1)} %shard_map.72.own), channel_id=1, source_target_pairs={{0,1},{1,0},{2,3},{3,2},{4,5},{5,4},{6,7},{7,6},{8,9},{9,8},{10,11... | collective-permute-start | bytes 1247240 | tf_op jit(solution)/shard_map/ppermute | solution.py:68
  25.3 2.0 %copy-start.2 = (bf16[1,512,3584]{2,1,0:T(8,128)(2,1)S(1)}, bf16[1,512,3584]{2,1,0:T(8,128)(2,1)}, u32[]{:S(2)}) copy-start(bf16[1,512,3584]{2,1,0:T(8,128)(2,1)} %param.9) | copy-start | bytes 11010052
  28.5 3.3 %collective-permute-start.7 = (bf16[144,1792]{1,0:T(8,128)(2,1)S(1)}, bf16[144,1792]{1,0:T(8,128)(2,1)S(1)}, u32[]{:S(2)}, u32[]{:S(2)}) collective-permute-start(bf16[144,1792]{1,0:T(8,128)(2,1)S(1)} %get-tuple-element.28), channel_id=1, source_target_pairs={{0,1},{1,0},{2,3},{3,2},{4,5},{5,4},{6,7},{7,6},{8,9},{9,8},{10,11... | collective-permute-start | bytes 1548296 | tf_op jit(solution)/shard_map/ppermute | solution.py:68
  30.2 1.6 %collective-permute-start.13 = (bf16[64,1792]{1,0:T(8,128)(2,1)S(1)}, bf16[64,1792]{1,0:T(8,128)(2,1)S(1)}, u32[]{:S(2)}, u32[]{:S(2)}) collective-permute-start(bf16[64,1792]{1,0:T(8,128)(2,1)S(1)} %get-tuple-element.33), channel_id=1, source_target_pairs={{0,1},{1,0},{2,3},{3,2},{4,5},{5,4},{6,7},{7,6},{8,9},{9,8},{10,11... | collective-permute-start | bytes 688136 | tf_op jit(solution)/shard_map/ppermute | solution.py:68
  30.8 3.0 %collective-permute-start.19 = (bf16[48,1792]{1,0:T(8,128)(2,1)S(1)}, bf16[48,1792]{1,0:T(8,128)(2,1)S(1)}, u32[]{:S(2)}, u32[]{:S(2)}) collective-permute-start(bf16[48,1792]{1,0:T(8,128)(2,1)S(1)} %get-tuple-element.39), channel_id=1, source_target_pairs={{0,1},{1,0},{2,3},{3,2},{4,5},{5,4},{6,7},{7,6},{8,9},{9,8},{10,11... | collective-permute-start | bytes 516104 | tf_op jit(solution)/shard_map/ppermute | solution.py:68
  31.9 12.5 %collective-permute-start.14 = (bf16[64,1792]{1,0:T(8,128)(2,1)S(1)}, bf16[64,1792]{1,0:T(8,128)(2,1)S(1)}, u32[]{:S(2)}, u32[]{:S(2)}) collective-permute-start(bf16[64,1792]{1,0:T(8,128)(2,1)S(1)} %get-tuple-element.34), channel_id=1, source_target_pairs={{0,8},{8,0},{16,24},{24,16},{1,9},{9,1},{17,25},{25,17},{2,10},{10... | collective-permute-start | bytes 688136 | tf_op jit(solution)/shard_map/ppermute | solution.py:68
  32.5 11.9 %collective-permute-start.15 = (bf16[64,1792]{1,0:T(8,128)(2,1)S(1)}, bf16[64,1792]{1,0:T(8,128)(2,1)S(1)}, u32[]{:S(2)}, u32[]{:S(2)}) collective-permute-start(bf16[64,1792]{1,0:T(8,128)(2,1)S(1)} %get-tuple-element.35), channel_id=1, source_target_pairs={{0,16},{8,24},{16,0},{24,8},{1,17},{9,25},{17,1},{25,9},{2,18},{10... | collective-permute-start | bytes 688136 | tf_op jit(solution)/shard_map/ppermute | solution.py:68
  33.8 6.1 %collective-permute-start.20 = (bf16[16,1792]{1,0:T(8,128)(2,1)S(1)}, bf16[16,1792]{1,0:T(8,128)(2,1)S(1)}, u32[]{:S(2)}, u32[]{:S(2)}) collective-permute-start(bf16[16,1792]{1,0:T(8,128)(2,1)S(1)} %get-tuple-element.40), channel_id=1, source_target_pairs={{0,6},{2,4},{4,2},{6,0},{1,7},{3,5},{5,3},{7,1},{8,14},{10,12},{12... | collective-permute-start | bytes 172040 | tf_op jit(solution)/shard_map/ppermute | solution.py:68
  37.4 5.1 %collective-permute-start.21 = (bf16[16,1792]{1,0:T(8,128)(2,1)S(1)}, bf16[16,1792]{1,0:T(8,128)(2,1)S(1)}, u32[]{:S(2)}, u32[]{:S(2)}) collective-permute-start(bf16[16,1792]{1,0:T(8,128)(2,1)S(1)} %get-tuple-element.41), channel_id=1, source_target_pairs={{0,4},{2,6},{4,0},{6,2},{1,5},{3,7},{5,1},{7,3},{8,12},{10,14},{12... | collective-permute-start | bytes 172040 | tf_op jit(solution)/shard_map/ppermute | solution.py:68
  37.4 5.1 %collective-permute-start.22 = (bf16[16,1792]{1,0:T(8,128)(2,1)S(1)}, bf16[16,1792]{1,0:T(8,128)(2,1)S(1)}, u32[]{:S(2)}, u32[]{:S(2)}) collective-permute-start(bf16[16,1792]{1,0:T(8,128)(2,1)S(1)} %get-tuple-element.42), channel_id=1, source_target_pairs={{0,2},{2,0},{4,6},{6,4},{1,3},{3,1},{5,7},{7,5},{8,10},{10,8},{12,... | collective-permute-start | bytes 172040 | tf_op jit(solution)/shard_map/ppermute | solution.py:68
  42.5 6.4 %collective-permute-start.23 = (bf16[16,1792]{1,0:T(8,128)(2,1)S(1)}, bf16[16,1792]{1,0:T(8,128)(2,1)S(1)}, u32[]{:S(2)}, u32[]{:S(2)}) collective-permute-start(bf16[16,1792]{1,0:T(8,128)(2,1)S(1)} %shard_map.79), channel_id=1, source_target_pairs={{0,24},{8,16},{16,8},{24,0},{1,25},{9,17},{17,9},{25,1},{2,26},{10... | collective-permute-start | bytes 172040 | tf_op jit(solution)/shard_map/ppermute | solution.py:68
  44.5 6.0 %collective-permute-start.16 = (bf16[16,1792]{1,0:T(8,128)(2,1)S(1)}, bf16[16,1792]{1,0:T(8,128)(2,1)S(1)}, u32[]{:S(2)}, u32[]{:S(2)}) collective-permute-start(bf16[16,1792]{1,0:T(8,128)(2,1)S(1)} %get-tuple-element.36), channel_id=1, source_target_pairs={{0,6},{2,4},{4,2},{6,0},{1,7},{3,5},{5,3},{7,1},{8,14},{10,12},{12... | collective-permute-start | bytes 172040 | tf_op jit(solution)/shard_map/ppermute | solution.py:68
  46.5 5.7 %collective-permute-start.17 = (bf16[16,1792]{1,0:T(8,128)(2,1)S(1)}, bf16[16,1792]{1,0:T(8,128)(2,1)S(1)}, u32[]{:S(2)}, u32[]{:S(2)}) collective-permute-start(bf16[16,1792]{1,0:T(8,128)(2,1)S(1)} %get-tuple-element.37), channel_id=1, source_target_pairs={{0,4},{2,6},{4,0},{6,2},{1,5},{3,7},{5,1},{7,3},{8,12},{10,14},{12... | collective-permute-start | bytes 172040 | tf_op jit(solution)/shard_map/ppermute | solution.py:68
  46.8 5.4 %collective-permute-start.18 = (bf16[16,1792]{1,0:T(8,128)(2,1)S(1)}, bf16[16,1792]{1,0:T(8,128)(2,1)S(1)}, u32[]{:S(2)}, u32[]{:S(2)}) collective-permute-start(bf16[16,1792]{1,0:T(8,128)(2,1)S(1)} %get-tuple-element.38), channel_id=1, source_target_pairs={{0,2},{2,0},{4,6},{6,4},{1,3},{3,1},{5,7},{7,5},{8,10},{10,8},{12,... | collective-permute-start | bytes 172040 | tf_op jit(solution)/shard_map/ppermute | solution.py:68
